TPU v7x, 128 devices: a whole 4x4x4 slice. The times are simulated.
128 devices in a mesh: gy: 32 (over y, x, core), gx: 4 (over z).
Axes of the slice: x: 4, y: 4, z: 4, core: 2. Of those that a mesh axis runs over, the one named last changes fastest.
Arguments:
- left_factor: bfloat16 [32768, 8192], P('gy', 'gx'), may hold values from -6 to 6
- right_factor: bfloat16 [8192, 8192], P('gy', 'gx'), may hold values from -0.0625 to 0.0625
Outputs:
- corrected: float32 [32768, 8192], P('gy', 'gx')
All inputs are finite; a program needn't handle non-finite values.
Results may differ from a plain program's by a relative error of at most 0.0003.
Values may be sent and summed in bfloat16 or wider, within the bound.
No kernel may reach another device: no remote copies, remote signals or barrier semaphores. Data moves between devices by JAX's collectives and lax.ppermute only.
A program may use at most 192 MiB of HBM per device.

v0:
```python
import functools

import jax
import jax.numpy as jnp
from jax import lax
from jax.experimental import pallas as pl
from jax.experimental.pallas import tpu as pltpu
from jax.sharding import PartitionSpec as P


ROW_CHUNKS = 4
NX = NY = NZ = 4
NC = 2
MT, NT = 512, 512

FAR_MIB = 6


def gy(y, x, c):
    return ((y % NY) * NX + x % NX) * NC + c


def along(axis, first):
    pairs = []
    for y in range(NY):
        for x in range(NX):
            for c in range(NC):
                step = 1 if (c == 0) == first else -1
                if axis == "x":
                    pairs.append((gy(y, x, c), gy(y, x + step, c)))
                elif axis == "y":
                    pairs.append((gy(y, x, c), gy(y + step, x, c)))
                elif axis == "core":
                    pairs.append((gy(y, x, c), gy(y, x, 1 - c)))
                else:
                    for z in range(NZ):
                        pairs.append((gy(y, x, c) * NZ + z, gy(y, x, c) * NZ + (z + step) % NZ))
    return pairs


def move(value, axis, first):
    name = ("gy", "gx") if axis == "z" else "gy"
    return lax.ppermute(value, name, along(axis, first))


def ring(value, axis):
    behind = move(value, axis, True)
    ahead = move(value, axis, False)
    return [value, behind, ahead, move(behind, axis, True)]


def exchange(power):
    opposite = lax.ppermute(power, "gx", [(i, (i + 2) % NZ) for i in range(NZ)])
    return [power, move(power, "z", True), move(power, "z", False), opposite]


def offset(slot, core):
    back = jnp.where(core == 0, 3, 1)
    return (0, back, 4 - back, 2)[slot]


def slot_of(distance, core):
    near = jnp.where((distance == 3) == (core == 0), 1, 2)
    return jnp.where(distance == 0, 0, jnp.where(distance == 2, 3, near))


def plan(pos):
    y0, core, z0 = pos[0], pos[2], pos[3]
    d = lax.rem(z0 - y0 + 4, 4)
    order = (
        jnp.where((d == 1) | (d == 2), 3, 0),
        jnp.where(d == 1, 0, 1),
        jnp.where(d == 2, 0, jnp.where(d == 1, 1, 3)),
    )
    where = []
    for b in range(3):
        distance = offset(b, core)
        where.append(jnp.where(distance == order[0], 0, jnp.where(distance == order[1], 1, 2)))
    return [lax.rem(z0 + o, 4) for o in order], where


def turned(x, x0):
    return lax.rem(x - x0 + 5, 4)


def copy_left_half(pos, pieces, n, y, lines, place, tile, sem):
    step = pieces[0][0][0].shape[0] // 4
    for q in range(2):
        core = pos[2] if q == 0 else 1 - pos[2]
        line = slot_of(lax.rem(y - pos[0] + 4, 4), core)
        to = [pl.multiple_of(place(lax.rem(offset(r, core) + 1, 4)) + core * step, step) for r in range(4)]
        for k in lines:
            @pl.when(line == k)
            def _():
                for r in range(4):
                    src = pieces[0][k][q].at[pl.ds(r * step, step), pl.ds(n, tile.shape[1])]
                    pltpu.make_async_copy(src, tile.at[pl.ds(to[r], step), :], sem).start()


def copy_right_half(pos, pieces, n, ys, lines, place, tile, sem):
    step = pieces[1][lines[0]][0].shape[0] // 4
    for q in range(2):
        core = pos[2] if q == 0 else 1 - pos[2]
        at = [pl.multiple_of(slot_of(lax.rem(y - pos[0] + 4, 4), core) * step, step) for y in ys]
        for k in lines:
            turn = lax.rem(offset(k, core) + 1, 4)
            for p in range(len(ys)):
                to = pl.multiple_of(place(p, turn) + core * step, step)
                src = pieces[1][k][q].at[pl.ds(at[p], step), pl.ds(n, tile.shape[1])]
                pltpu.make_async_copy(src, tile.at[pl.ds(to, step), :], sem).start()


def copy_left(sources, b, place, seg, dst, sem):
    for x in range(4):
        wanted, at = place(x)

        @pl.when(wanted)
        def _():
            col = pl.ds(pl.multiple_of(at, seg), seg)
            for i, chunk in enumerate(sources[b]):
                size = chunk.shape[0]
                pltpu.make_async_copy(chunk.at[:, pl.ds(x * seg, seg)], dst.at[pl.ds(i * size, size), col], sem).start()


def landed(ref, sem):
    pltpu.make_async_copy(ref, ref, sem).wait()


def nest(flat):
    return [[[flat[(h * 4 + line) * 2 + q] for q in range(2)] for line in range(4)] for h in range(2)]


def multiply(a_v, tile, acc, col, spans, add):
    rows, nt = a_v.shape[0], tile.shape[1]

    @pl.loop(0, rows // MT)
    def _(t):
        at = pl.ds(pl.multiple_of(t * MT, MT), MT)
        cols = pl.ds(col, nt)
        r = acc[at, cols] if add else None
        for a, b, size in spans:
            d = jnp.dot(a_v[at, pl.ds(a, size)], tile[pl.ds(b, size), :], preferred_element_type=jnp.float32)
            r = d if r is None else r + d
        acc[at, cols] = r


def left_kernel(pos, left, *refs):
    sources, lines = ([left], refs[:4], refs[4:8]), refs[8:14]
    acc, a_v, t_v, a_sem, t_sem = refs[14:]
    pieces = [[lines[2 * k:2 * k + 2] for k in range(3)]]
    _, depth = left.shape
    half, nt, seg, x0 = acc.shape[1] // 2, t_v.shape[2], depth // 4, pos[1]
    blocks, where = plan(pos)

    def fetch(s, p):
        copy_left_half(
            pos, pieces, s * nt, blocks[p], range(3), lambda t: (4 * p + t) * seg, t_v.at[s % 2], t_sem.at[s % 2, p])

    for b in range(3):
        copy_left(sources, b, lambda x: (where[b] < 2, (4 * where[b] + turned(x, x0)) * seg),
                  seg, a_v, a_sem.at[jnp.minimum(where[b], 1)])
        if b < 2:
            fetch(0, b)
    for s in range(half // nt):
        tile, col = t_v.at[s % 2], s * nt
        for p in range(2):
            if col + nt < half:
                fetch(s + 1, p)
        for p in range(2):
            if s == 0:
                landed(a_v.at[:, pl.ds(0, 4 * seg)], a_sem.at[p])
            landed(tile.at[pl.ds(0, 4 * seg), :], t_sem.at[s % 2, p])
            if s == 0:
                multiply(a_v, tile, acc, col, ((4 * p * seg, 4 * p * seg, 4 * seg),), p > 0)
        if s > 0:
            multiply(a_v, tile, acc, col, ((0, 0, 8 * seg),), False)


def right_kernel(pos, before, left, *refs):
    sources, lines = ([left], refs[:4], refs[4:8]), refs[8:14]
    acc, a_v, t_v, a_sem, t_sem = refs[14:]
    pieces = [None, [lines[2 * k:2 * k + 2] for k in range(3)]]
    _, depth = left.shape
    half, nt, seg, x0 = acc.shape[1] // 2, t_v.shape[2], depth // 4, pos[1]
    blocks, where = plan(pos)

    def fetch(s, p):
        copy_right_half(
            pos, pieces, s * nt, [blocks[p]], range(3), lambda _, t: (3 * p + t) * seg, t_v.at[s % 2], t_sem.at[s % 2, p])

    for b in range(3):
        copy_left(sources, b, lambda x: (turned(x, x0) < 3, (3 * where[b] + turned(x, x0)) * seg),
                  seg, a_v, a_sem.at[where[b]])
        fetch(0, b)
    for s in range(half // nt):
        tile, col = t_v.at[s % 2], half + s * nt
        for p in range(3):
            if (s + 1) * nt < half:
                fetch(s + 1, p)
        for p in range(3):
            if s == 0:
                landed(a_v.at[:, pl.ds(0, 3 * seg)], a_sem.at[p])
            landed(tile.at[pl.ds(0, 3 * seg), :], t_sem.at[s % 2, p])
            if s == 0:
                multiply(a_v, tile, acc, col, ((3 * p * seg, 3 * p * seg, 3 * seg),), p > 0)
        if s > 0:
            multiply(a_v, tile, acc, col, ((0, 0, 9 * seg),), False)


def rest_kernel(pos, before, left, *refs):
    sources, pieces = ([left], refs[:4], refs[4:8]), nest(refs[8:24])
    acc, far_v, a_v, t_v, a_sem, t_sem, f_sem = refs[24:]
    _, depth = left.shape
    half, nt, seg, x0 = acc.shape[1] // 2, t_v.shape[2], depth // 4, pos[1]
    blocks, where = plan(pos)
    parts = half // nt
    for s in range(parts):
        copy_left_half(
            pos, pieces, s * nt, blocks[2], range(4), lambda t: lax.rem(t + 1, 4) * seg, t_v.at[s], t_sem.at[s])
        if s == 0:
            for b in range(3):
                copy_left(sources, b, lambda x: (
                    (where[b] == 2) | (turned(x, x0) == 3),
                    jnp.where(turned(x, x0) == 3, where[b], 3 + turned(x, x0)) * seg), seg, a_v,
                    a_sem.at[jnp.where(where[b] == 2, 0, 1)])
    for s in range(parts):
        copy_right_half(
            pos, pieces, s * nt, blocks, (3,), lambda p, t: p * seg, t_v.at[parts + s], t_sem.at[parts + s])

    def place(t):
        return lax.rem(x0 + t + 3, 4) * seg

    opposite = lax.rem(pos[3] + 2, 4)
    for s in range(parts):
        copy_left_half(pos, pieces, s * nt, opposite, range(4), place, far_v.at[s], f_sem)
        copy_right_half(
            pos, pieces, s * nt, [opposite], range(4), lambda _, t: place(t), far_v.at[parts + s], f_sem)
    for s in range(2 * parts):
        if s == 0:
            landed(a_v.at[:, pl.ds(2 * seg, 4 * seg)], a_sem.at[0])
        if s == parts:
            landed(a_v.at[:, pl.ds(0, 2 * seg)], a_sem.at[1])
        first, size = (2 * seg, 4 * seg) if s < parts else (0, 3 * seg)
        landed(t_v.at[s, pl.ds(0, size), :], t_sem.at[s])
        multiply(a_v, t_v.at[s], acc, s * nt, ((first, 0, size),), True)
    landed(far_v, f_sem)


def far_multiply(low, mt, a_v, tile, acc, p_v, s):
    rows, nt = a_v.shape[0], tile.shape[1]

    @pl.loop(0, rows // mt)
    def _(t):
        at = pl.ds(pl.multiple_of(t * mt, mt), mt)
        to, cols = pl.ds(pl.multiple_of(low + t * mt, 128), mt), pl.ds(s * nt, nt)
        r = acc[to, cols] + jnp.dot(a_v[at, :], tile[...], preferred_element_type=jnp.float32)
        acc[to, cols] = r
        lanes = r[:, 0:128] * r[:, 0:128]
        for n in range(128, nt, 128):
            lanes = lanes + r[:, n:n + 128] * r[:, n:n + 128]
        p_v[at, :] = lanes if s == 0 else p_v[at, :] + lanes


def spread(p_v, power):
    for m in range(0, p_v.shape[0], 128):
        power[:, m:m + 128] = jnp.sum(p_v[m:m + 128, :].T, axis=0, keepdims=True) + jnp.zeros((8, 128), jnp.float32)


def far_kernel(low, before, t_in, *refs):
    count = len(refs) - 6
    chunks, (acc, t_v, power, a_v, p_v, a_sem) = refs[:count], refs[count:]
    rc = a_v.shape[0] // count
    for i, chunk in enumerate(chunks):
        pltpu.make_async_copy(chunk, a_v.at[pl.ds(i * rc, rc), :], a_sem).start()
    landed(a_v, a_sem)
    for s in range(t_v.shape[0]):
        far_multiply(low, min(256, a_v.shape[0]), a_v, t_in.at[s], acc, p_v, s)
    spread(p_v, power)


def scale_kernel(low, cols, acc, *refs):
    powers, (out, o_v, o_sem) = refs[:4], refs[-3:]
    size = o_v.shape[1]
    blocks = powers[0].shape[1] // size
    for i in range(blocks):
        if i >= 2:
            landed(o_v.at[i % 2], o_sem.at[i % 2])
        lanes = pl.ds(i * size, size)
        total = (powers[0][0:1, lanes] + powers[1][0:1, lanes]) + (powers[2][0:1, lanes] + powers[3][0:1, lanes])
        factor = jnp.broadcast_to(lax.rsqrt(total / cols + 1e-06), (size, size)).T[:, 0:1]
        o_v[i % 2] = acc[pl.ds(low + i * size, size), :] * factor
        pltpu.make_async_copy(o_v.at[i % 2], out.at[pl.ds(low + i * size, size), :], o_sem.at[i % 2]).start()
    for i in range(min(blocks, 2)):
        landed(o_v.at[i], o_sem.at[i])


ANY = pl.BlockSpec(memory_space=pltpu.HBM)
SMEM = pl.BlockSpec(memory_space=pltpu.SMEM)


VMEM = pl.BlockSpec(memory_space=pltpu.VMEM)


def kept(value):
    return pltpu.with_memory_space_constraint(value, pltpu.VMEM)


def apart(value):
    return pltpu.with_memory_space_constraint(value, pltpu.HBM)


def call(kernel, out_shape, in_specs, out_specs, scratch, flops, limit, aliases={}):
    return pl.pallas_call(
        kernel,
        out_shape=out_shape,
        in_specs=in_specs,
        out_specs=out_specs,
        scratch_shapes=scratch,
        input_output_aliases=aliases,
        cost_estimate=pl.CostEstimate(flops=flops, bytes_accessed=16 << 20, transcendentals=0),
        compiler_params=pltpu.CompilerParams(vmem_limit_bytes=limit << 20),
    )


def near(pos, left, behind, ahead, pieces):
    rows, depth = left.shape
    half, seg = pieces[0].shape[1], depth // 4
    total = pltpu.VMEM((rows, 2 * half), jnp.float32)
    flops = 2 * rows * half * seg
    dma = pltpu.SemaphoreType.DMA
    blocks = [left, *behind, *ahead]

    def scratch(size, depth, parts):
        return [pltpu.VMEM((rows, size), left.dtype), pltpu.VMEM((parts, depth, NT), left.dtype), dma((3,))]

    acc = call(
        left_kernel, total, [SMEM] + [ANY] * 15, VMEM, scratch(8 * seg, 8 * seg, 2) + [dma((2, 2))], 8 * flops, 18,
    )(pos, *blocks, *pieces[:6])
    acc = call(
        right_kernel, total, [SMEM, VMEM] + [ANY] * 15, VMEM, scratch(9 * seg, 9 * seg, 2) + [dma((2, 3))],
        9 * flops, 20, {1: 0},
    )(pos, kept(acc), *blocks, *pieces[8:14])
    parts = 2 * half // NT
    return call(
        rest_kernel, (total, pltpu.VMEM((parts, depth, NT), left.dtype)), [SMEM, VMEM] + [ANY] * 25, (VMEM, VMEM),
        scratch(6 * seg, depth, parts) + [dma((parts,)), dma], 7 * flops, 16, {1: 0},
    )(pos, kept(acc), *blocks, *pieces)


def far(low, acc, tile, chunks):
    rc, depth = chunks[0].shape
    rows = rc * len(chunks)
    out = pltpu.VMEM(acc.shape, acc.dtype), pltpu.VMEM(tile.shape, tile.dtype), jax.ShapeDtypeStruct((8, rows), jnp.float32)
    return call(
        functools.partial(far_kernel, low), out, [VMEM, VMEM] + [ANY] * len(chunks), (VMEM, VMEM, VMEM),
        [pltpu.VMEM((rows, depth), chunks[0].dtype), pltpu.VMEM((rows, 128), jnp.float32), pltpu.SemaphoreType.DMA],
        2 * rows * depth * acc.shape[1], FAR_MIB, {0: 0, 1: 1},
    )(kept(acc), kept(tile), *chunks)


def scale(low, cols, acc, powers, base):
    extra = [] if base is None else [base]
    return call(
        functools.partial(scale_kernel, low, cols), jax.ShapeDtypeStruct(acc.shape, jnp.float32),
        [VMEM] * 5 + [ANY] * len(extra), ANY,
        [pltpu.VMEM((2, 128, acc.shape[1]), jnp.float32), pltpu.SemaphoreType.DMA((2,))],
        powers[0].shape[1] * acc.shape[1] * 30, FAR_MIB, {5: 0} if extra else {},
    )(kept(acc), *powers, *extra)


def per_device(left, right):
    rows, _ = left.shape
    width = right.shape[1]
    rc, half = rows // ROW_CHUNKS, width // 2
    me, z = lax.axis_index("gy"), lax.axis_index("gx")
    pos = jnp.stack([me // (NX * NC), (me // NC) % NX, me % NC, z]).astype(jnp.int32)

    head, left_too = lax.optimization_barrier((left[:rc], left))
    lefts = [ring(left_too[i * rc:(i + 1) * rc] if i else head, "z") for i in range(ROW_CHUNKS)]
    pieces = []
    for h, (a, b) in enumerate((("x", "y"), ("y", "x"))):
        line = jnp.concatenate(ring(right[:, h * half:(h + 1) * half], a), axis=0)
        for v in ring(line, b):
            pieces += [v, move(v, "core", True)]

    pieces = [apart(v) for v in pieces]
    sides = [[apart(c[k]) for c in lefts] for k in (1, 2)]
    acc, tile = near(pos, apart(left), *sides, pieces)
    low = rows - rc
    acc, tile, power = far(0, acc, tile, [c[3] for c in lefts[:-1]])
    first = exchange(power)
    acc, tile, power = far(low, acc, tile, [lefts[-1][3]])
    second = exchange(power)
    return scale(low, width * NZ, acc, second, scale(0, width * NZ, acc, first, None))


def solution(mesh):
    placed = (P("gy", "gx"), P("gy", "gx"))
    return jax.shard_map(per_device, mesh=mesh, in_specs=placed, out_specs=P("gy", "gx"), check_vma=False)
```

profile of v0, /device:TPU:0, one launch (start us, length us, event | category | flops | bytes accessed | tf_op | source)
XLA Modules:
  0.0 241.3 jit_solution(17670302346068110512)
XLA Ops:
  0.0 1.4 fusion.1
  1.4 1.7 collective-permute-start.8
  3.1 1.6 collective-permute-start.9
  4.7 1.7 collective-permute-start.16
  6.4 1.5 collective-permute-start.17
  8.0 1.3 slice.18
  9.7 2.1 collective-permute-start.1
  11.8 4.3 %collective-permute-done.8 = bf16[256,1024]{1,0:T(8,128)(2,1)S(1)} collective-permute-done((bf16[256,1024]{1,0:T(8,128)(2,1)S(1)}, bf16[256,1024]{1,0:T(8,128)(2,1)S(1)}, u32[]{:S(2)}, u32[]{:S(2)}) %collective-permute-start.8) | collective-permute-done | bytes 524320 | tf_op jit(solution)/shard_map/ppermute | solution.py:43
  16.0 2.1 collective-permute-start.2
  18.2 1.9 collective-permute-start.3
  20.1 3.9 %collective-permute-start.5 = (bf16[256,2048]{1,0:T(8,128)(2,1)S(1)}, bf16[256,2048]{1,0:T(8,128)(2,1)S(1)}, u32[]{:S(2)}, u32[]{:S(2)}) collective-permute-start(bf16[256,2048]{1,0:T(8,128)(2,1)S(1)} %get-tuple-element.25), channel_id=1, source_target_pairs={{0,3},{1,0},{2,1},{3,2},{4,5},{5,6},{6,7},{7,4},{8,11},{9,8},{10,9... | collective-permute-start | bytes 3145736 | tf_op jit(solution)/shard_map/ppermute | solution.py:43
  24.1 10.3 %collective-permute-done.10 = bf16[256,1024]{1,0:T(8,128)(2,1)S(1)} collective-permute-done((bf16[256,1024]{1,0:T(8,128)(2,1)S(1)}, bf16[256,1024]{1,0:T(8,128)(2,1)S(1)}, u32[]{:S(2)}, u32[]{:S(2)}) %collective-permute-start.10) | collective-permute-done | bytes 524320 | tf_op jit(solution)/shard_map/ppermute | solution.py:43
  34.4 0.8 collective-permute-start.18
  35.2 0.4 collective-permute-start.6
  35.6 14.9 %collective-permute-done.2.refs_2_ = bf16[256,2048]{1,0:T(8,128)(2,1)S(1)} collective-permute-done((bf16[256,2048]{1,0:T(8,128)(2,1)S(1)}, bf16[256,2048]{1,0:T(8,128)(2,1)S(1)}, u32[]{:S(2)}, u32[]{:S(2)}) %collective-permute-start.2) | collective-permute-done | bytes 1048608 | tf_op jit(solution)/shard_map/ppermute | solution.py:43
  50.5 4.9 %collective-permute-start.7 = (bf16[256,2048]{1,0:T(8,128)(2,1)S(1)}, bf16[256,2048]{1,0:T(8,128)(2,1)S(1)}, u32[]{:S(2)}, u32[]{:S(2)}) collective-permute-start(bf16[256,2048]{1,0:T(8,128)(2,1)S(1)} %get-tuple-element.23), channel_id=1, source_target_pairs={{0,3},{1,0},{2,1},{3,2},{4,5},{5,6},{6,7},{7,4},{8,11},{9,8},{10,9... | collective-permute-start | bytes 3145736 | tf_op jit(solution)/shard_map/ppermute | solution.py:43
  55.4 17.6 %collective-permute-done.3.refs_3_ = bf16[256,2048]{1,0:T(8,128)(2,1)S(1)} collective-permute-done((bf16[256,2048]{1,0:T(8,128)(2,1)S(1)}, bf16[256,2048]{1,0:T(8,128)(2,1)S(1)}, u32[]{:S(2)}, u32[]{:S(2)}) %collective-permute-start.3) | collective-permute-done | bytes 1048608 | tf_op jit(solution)/shard_map/ppermute | solution.py:43
  73.0 2.3 collective-permute-start
  75.6 3.2 %collective-permute-start.14 = (bf16[1024,1024]{1,0:T(8,128)(2,1)S(1)}, bf16[1024,1024]{1,0:T(8,128)(2,1)S(1)}, u32[]{:S(2)}, u32[]{:S(2)}) collective-permute-start(bf16[1024,1024]{1,0:T(8,128)(2,1)S(1)} %pad_maximum_fusion.refs_8_), channel_id=1, source_target_pairs={{0,96},{4,36},{8,104},{12,44},{16,112},{20,52},{24,120},{28,60},{3... | collective-permute-start | bytes 6291464 | tf_op jit(solution)/shard_map/ppermute | solution.py:43
  78.8 1.6 pad_maximum_fusion.1.refs_8_.refs_16_
  80.5 8.0 %collective-permute-done.7.refs_7_ = bf16[256,2048]{1,0:T(8,128)(2,1)S(1)} collective-permute-done((bf16[256,2048]{1,0:T(8,128)(2,1)S(1)}, bf16[256,2048]{1,0:T(8,128)(2,1)S(1)}, u32[]{:S(2)}, u32[]{:S(2)}) %collective-permute-start.7) | collective-permute-done | bytes 1048608 | tf_op jit(solution)/shard_map/ppermute | solution.py:43
  88.6 5.5 %collective-permute-done.refs_0_ = bf16[256,2048]{1,0:T(8,128)(2,1)S(1)} collective-permute-done((bf16[256,2048]{1,0:T(8,128)(2,1)S(1)}, bf16[256,2048]{1,0:T(8,128)(2,1)S(1)}, u32[]{:S(2)}, u32[]{:S(2)}) %collective-permute-start) | collective-permute-done | bytes 1048608 | tf_op jit(solution)/shard_map/ppermute | solution.py:43
  94.1 2.0 collective-permute-start.4
  96.1 12.8 %collective-permute-done.4.refs_4_ = bf16[256,2048]{1,0:T(8,128)(2,1)S(1)} collective-permute-done((bf16[256,2048]{1,0:T(8,128)(2,1)S(1)}, bf16[256,2048]{1,0:T(8,128)(2,1)S(1)}, u32[]{:S(2)}, u32[]{:S(2)}) %collective-permute-start.4) | collective-permute-done | bytes 1048608 | tf_op jit(solution)/shard_map/ppermute | solution.py:43
  108.9 1.5 collective-permute-start.22
  110.4 14.1 %collective-permute-done.12.refs_10_ = bf16[1024,1024]{1,0:T(8,128)(2,1)S(1)} collective-permute-done((bf16[1024,1024]{1,0:T(8,128)(2,1)S(1)}, bf16[1024,1024]{1,0:T(8,128)(2,1)S(1)}, u32[]{:S(2)}, u32[]{:S(2)}) %collective-permute-start.12) | collective-permute-done | bytes 2097184 | tf_op jit(solution)/shard_map/ppermute | solution.py:43
  124.5 0.5 collective-permute-start.15
  125.5 16.8 %collective-permute-done.22.refs_12_.refs_20_ = bf16[1024,1024]{1,0:T(8,128)(2,1)} collective-permute-done((bf16[1024,1024]{1,0:T(8,128)(2,1)}, bf16[1024,1024]{1,0:T(8,128)(2,1)}, u32[]{:S(2)}, u32[]{:S(2)}) %collective-permute-start.22) | collective-permute-done | bytes 2097184 | tf_op jit(solution)/shard_map/ppermute | solution.py:43
  142.3 4.7 %collective-permute-start.19 = (bf16[1024,1024]{1,0:T(8,128)(2,1)}, bf16[1024,1024]{1,0:T(8,128)(2,1)}, u32[]{:S(2)}, u32[]{:S(2)}) collective-permute-start(bf16[1024,1024]{1,0:T(8,128)(2,1)} %pad_maximum_fusion.1.refs_8_.refs_16_), channel_id=1, source_target_pairs={{0,4},{4,0},{8,12},{12,8},{16,20},{20,16},{24,28},{28,24},{32,36},... | collective-permute-start | bytes 6291464 | tf_op jit(solution)/shard_map/ppermute | solution.py:43
  147.1 0.4 collective-permute-start.23
  147.5 4.9 %collective-permute-done.24.refs_14_ = bf16[1024,1024]{1,0:T(8,128)(2,1)} collective-permute-done((bf16[1024,1024]{1,0:T(8,128)(2,1)S(1)}, bf16[1024,1024]{1,0:T(8,128)(2,1)}, u32[]{:S(2)}, u32[]{:S(2)}) %collective-permute-start.24) | collective-permute-done | bytes 2097184 | tf_op jit(solution)/shard_map/ppermute | solution.py:43
  152.5 8.6 %collective-permute-done.26.refs_22_ = bf16[1024,1024]{1,0:T(8,128)(2,1)} collective-permute-done((bf16[1024,1024]{1,0:T(8,128)(2,1)}, bf16[1024,1024]{1,0:T(8,128)(2,1)}, u32[]{:S(2)}, u32[]{:S(2)}) %collective-permute-start.26) | collective-permute-done | bytes 2097184 | tf_op jit(solution)/shard_map/ppermute | solution.py:43
  161.2 14.6 %shard_map.28.before = f32[1024,2048]{1,0:T(8,128)S(1)} custom-call(s32[4]{0:T(128)S(1)} %pad_add_fusion.pos, bf16[1024,2048]{1,0:T(8,128)(2,1)} %left.5, bf16[256,2048]{1,0:T(8,128)(2,1)} %copy-done.9, bf16[256,2048]{1,0:T(8,128)(2,1)} %copy-done.4, bf16[256,2048]{1,0:T(8,128)(2,1)} %copy-done.6, bf16[256,2048]{1,0:T(8,128)(2,1)} %copy-done.2, ...), custom_call_target="tpu_custom_call" | custom-call | flops 8589934592 | bytes 16777216 | tf_op jit(solution)/shard_map/pallas_call | solution.py:336
  175.8 2.9 %collective-permute-start.29 = (bf16[256,2048]{1,0:T(8,128)(2,1)S(1)}, bf16[256,2048]{1,0:T(8,128)(2,1)S(1)}, u32[]{:S(2)}, u32[]{:S(2)}) collective-permute-start(bf16[256,2048]{1,0:T(8,128)(2,1)S(1)} %copy-done.5), channel_id=1, source_target_pairs={{0,1},{1,2},{2,3},{3,0},{4,7},{5,4},{6,5},{7,6},{8,9},{9,10},{10,1... | collective-permute-start | bytes 3145736 | tf_op jit(solution)/shard_map/ppermute | solution.py:43
  178.8 2.0 collective-permute-start.28
  180.8 16.0 %shard_map.29.before = f32[1024,2048]{1,0:T(8,128)S(1)} custom-call(s32[4]{0:T(128)S(1)} %pad_add_fusion.pos, f32[1024,2048]{1,0:T(8,128)S(1)} %shard_map.28.before, bf16[1024,2048]{1,0:T(8,128)(2,1)} %left.5, bf16[256,2048]{1,0:T(8,128)(2,1)} %copy-done.9, bf16[256,2048]{1,0:T(8,128)(2,1)} %copy-done.4, ...), custom_call_target="tpu_custom_call", output_to_operand_aliasing={{}: (1, {})} | custom-call | flops 9663676416 | bytes 16777216 | tf_op jit(solution)/shard_map/pallas_call | solution.py:339
  196.9 14.8 %shard_map.30 = (f32[1024,2048]{1,0:T(8,128)S(1)}, bf16[4,2048,512]{2,1,0:T(8,128)(2,1)S(1)}) custom-call(s32[4]{0:T(128)S(1)} %pad_add_fusion.pos, f32[1024,2048]{1,0:T(8,128)S(1)} %shard_map.29.before, bf16[1024,2048]{1,0:T(8,128)(2,1)} %left.5, bf16[256,2048]{1,0:T(8,128)(2,1)} %copy-done.9, ...), custom_call_target="tpu_custom_call", output_to_operand_aliasing={{0}: (1, {})} | custom-call | flops 7516192768 | bytes 16777216 | tf_op jit(solution)/shard_map/pallas_call | solution.py:344
  211.7 2.9 %collective-permute-done.28.refs_0_ = bf16[256,2048]{1,0:T(8,128)(2,1)S(1)} collective-permute-done((bf16[256,2048]{1,0:T(8,128)(2,1)S(1)}, bf16[256,2048]{1,0:T(8,128)(2,1)S(1)}, u32[]{:S(2)}, u32[]{:S(2)}) %collective-permute-start.28) | collective-permute-done | bytes 1048608 | tf_op jit(solution)/shard_map/ppermute | solution.py:43
  214.6 9.2 %shard_map.31 = (f32[1024,2048]{1,0:T(8,128)S(1)}, bf16[4,2048,512]{2,1,0:T(8,128)(2,1)S(1)}, f32[8,768]{1,0:T(8,128)S(1)}) custom-call(f32[1024,2048]{1,0:T(8,128)S(1)} %get-tuple-element.16.before, bf16[4,2048,512]{2,1,0:T(8,128)(2,1)S(1)} %get-tuple-element.17.t_in, ...), custom_call_target="tpu_custom_call", output_to_operand_aliasing={{0}: (0, {}), {1}: (1, {})} | custom-call | flops 6442450944 | bytes 16777216 | tf_op jit(solution)/shard_map/pallas_call | solution.py:354
  223.8 2.0 collective-permute-start.35
  225.8 1.6 collective-permute-start.36
  227.3 0.6 collective-permute-start.37
  227.9 2.6 %shard_map.32 = (f32[1024,2048]{1,0:T(8,128)S(1)}, bf16[4,2048,512]{2,1,0:T(8,128)(2,1)S(1)}, f32[8,256]{1,0:T(8,128)S(1)}) custom-call(f32[1024,2048]{1,0:T(8,128)S(1)} %get-tuple-element.18.before, bf16[4,2048,512]{2,1,0:T(8,128)(2,1)S(1)} %get-tuple-element.19.t_in, ...), custom_call_target="tpu_custom_call", output_to_operand_aliasing={{0}: (0, {}), {1}: (1, {})} | custom-call | flops 2147483648 | bytes 16777216 | tf_op jit(solution)/shard_map/pallas_call | solution.py:354
  230.5 1.1 collective-permute-start.32
  231.6 2.2 collective-permute-start.33
  233.8 1.7 collective-permute-start.34
  235.5 4.0 %shard_map.33.refs_4_ = f32[1024,2048]{1,0:T(8,128)} custom-call(f32[1024,2048]{1,0:T(8,128)S(1)} %get-tuple-element.20.acc, f32[8,768]{1,0:T(8,128)S(1)} %get-tuple-element.22.refs_0_, f32[8,768]{1,0:T(8,128)S(1)} %collective-permute-done.35.refs_1_, f32[8,768]{1,0:T(8,128)S(1)} %collective-permute-done.36.refs_2_, f32[8,768]{1,0:T(8,128)S(1)} %collective-permute-done.37.refs_3_), custom_call_target="tpu_custom_call" | custom-call | flops 47185920 | bytes 16777216 | tf_op jit(solution)/shard_map/pallas_call | solution.py:363
  239.6 1.6 shard_map.34
  (79 shorter events, 1.8 us)
Async XLA Ops:
  1.4 14.6 %collective-permute-start.8 = (bf16[256,1024]{1,0:T(8,128)(2,1)S(1)}, bf16[256,1024]{1,0:T(8,128)(2,1)S(1)}, u32[]{:S(2)}, u32[]{:S(2)}) collective-permute-start(bf16[256,1024]{1,0:T(8,128)(2,1)S(1)} %get-tuple-element.27), channel_id=1, source_target_pairs={{0,8},{4,28},{8,16},{12,4},{16,24},{20,12},{24,0},{28,20},{32,40},... | collective-permute-start | bytes 1572872 | tf_op jit(solution)/shard_map/ppermute | solution.py:43
  3.1 15.1 %collective-permute-start.9 = (bf16[256,1024]{1,0:T(8,128)(2,1)S(1)}, bf16[256,1024]{1,0:T(8,128)(2,1)S(1)}, u32[]{:S(2)}, u32[]{:S(2)}) collective-permute-start(bf16[256,1024]{1,0:T(8,128)(2,1)S(1)} %get-tuple-element.27), channel_id=1, source_target_pairs={{0,24},{4,12},{8,0},{12,20},{16,8},{20,28},{24,16},{28,4},{32,56},... | collective-permute-start | bytes 1572872 | tf_op jit(solution)/shard_map/ppermute | solution.py:43
  4.7 15.4 %collective-permute-start.16 = (bf16[256,1024]{1,0:T(8,128)(2,1)S(1)}, bf16[256,1024]{1,0:T(8,128)(2,1)S(1)}, u32[]{:S(2)}, u32[]{:S(2)}) collective-permute-start(bf16[256,1024]{1,0:T(8,128)(2,1)S(1)} %get-tuple-element.26), channel_id=1, source_target_pairs={{0,32},{4,100},{8,40},{12,108},{16,48},{20,116},{24,56},{28,124},{... | collective-permute-start | bytes 1572872 | tf_op jit(solution)/shard_map/ppermute | solution.py:43
  6.4 17.6 %collective-permute-start.17 = (bf16[256,1024]{1,0:T(8,128)(2,1)S(1)}, bf16[256,1024]{1,0:T(8,128)(2,1)S(1)}, u32[]{:S(2)}, u32[]{:S(2)}) collective-permute-start(bf16[256,1024]{1,0:T(8,128)(2,1)S(1)} %get-tuple-element.26), channel_id=1, source_target_pairs={{0,96},{4,36},{8,104},{12,44},{16,112},{20,52},{24,120},{28,60},{3... | collective-permute-start | bytes 1572872 | tf_op jit(solution)/shard_map/ppermute | solution.py:43
  9.7 25.5 %collective-permute-start.1 = (bf16[256,2048]{1,0:T(8,128)(2,1)S(1)}, bf16[256,2048]{1,0:T(8,128)(2,1)S(1)}, u32[]{:S(2)}, u32[]{:S(2)}) collective-permute-start(bf16[256,2048]{1,0:T(8,128)(2,1)S(1)} %get-tuple-element.25), channel_id=1, source_target_pairs={{0,1},{1,2},{2,3},{3,0},{4,7},{5,4},{6,5},{7,6},{8,9},{9,10},{10,1... | collective-permute-start | bytes 3145736 | tf_op jit(solution)/shard_map/ppermute | solution.py:43
  16.0 34.5 %collective-permute-start.2 = (bf16[256,2048]{1,0:T(8,128)(2,1)S(1)}, bf16[256,2048]{1,0:T(8,128)(2,1)S(1)}, u32[]{:S(2)}, u32[]{:S(2)}) collective-permute-start(bf16[256,2048]{1,0:T(8,128)(2,1)S(1)} %get-tuple-element.24), channel_id=1, source_target_pairs={{0,1},{1,2},{2,3},{3,0},{4,7},{5,4},{6,5},{7,6},{8,9},{9,10},{10,1... | collective-permute-start | bytes 3145736 | tf_op jit(solution)/shard_map/ppermute | solution.py:43
  18.2 54.8 %collective-permute-start.3 = (bf16[256,2048]{1,0:T(8,128)(2,1)S(1)}, bf16[256,2048]{1,0:T(8,128)(2,1)S(1)}, u32[]{:S(2)}, u32[]{:S(2)}) collective-permute-start(bf16[256,2048]{1,0:T(8,128)(2,1)S(1)} %get-tuple-element.23), channel_id=1, source_target_pairs={{0,1},{1,2},{2,3},{3,0},{4,7},{5,4},{6,5},{7,6},{8,9},{9,10},{10,1... | collective-permute-start | bytes 3145736 | tf_op jit(solution)/shard_map/ppermute | solution.py:43
  20.1 55.4 %collective-permute-start.5 = (bf16[256,2048]{1,0:T(8,128)(2,1)S(1)}, bf16[256,2048]{1,0:T(8,128)(2,1)S(1)}, u32[]{:S(2)}, u32[]{:S(2)}) collective-permute-start(bf16[256,2048]{1,0:T(8,128)(2,1)S(1)} %get-tuple-element.25), channel_id=1, source_target_pairs={{0,3},{1,0},{2,1},{3,2},{4,5},{5,6},{6,7},{7,4},{8,11},{9,8},{10,9... | collective-permute-start | bytes 3145736 | tf_op jit(solution)/shard_map/ppermute | solution.py:43
  24.0 10.4 %collective-permute-start.10 = (bf16[256,1024]{1,0:T(8,128)(2,1)S(1)}, bf16[256,1024]{1,0:T(8,128)(2,1)S(1)}, u32[]{:S(2)}, u32[]{:S(2)}) collective-permute-start(bf16[256,1024]{1,0:T(8,128)(2,1)S(1)} %collective-permute-done.8), channel_id=1, source_target_pairs={{0,8},{4,28},{8,16},{12,4},{16,24},{20,12},{24,0},{28,20},{32,40},... | collective-permute-start | bytes 1572872 | tf_op jit(solution)/shard_map/ppermute | solution.py:43
  34.4 41.2 %collective-permute-start.18 = (bf16[256,1024]{1,0:T(8,128)(2,1)S(1)}, bf16[256,1024]{1,0:T(8,128)(2,1)S(1)}, u32[]{:S(2)}, u32[]{:S(2)}) collective-permute-start(bf16[256,1024]{1,0:T(8,128)(2,1)S(1)} %collective-permute-done.16), channel_id=1, source_target_pairs={{0,32},{4,100},{8,40},{12,108},{16,48},{20,116},{24,56},{28,124},{... | collective-permute-start | bytes 1572872 | tf_op jit(solution)/shard_map/ppermute | solution.py:43
  35.2 37.8 %copy-start.4 = (bf16[256,2048]{1,0:T(8,128)(2,1)}, bf16[256,2048]{1,0:T(8,128)(2,1)S(1)}, u32[]{:S(2)}) copy-start(bf16[256,2048]{1,0:T(8,128)(2,1)S(1)} %collective-permute-done.1.refs_1_) | copy-start | bytes 3145732
  35.2 45.2 %collective-permute-start.6 = (bf16[256,2048]{1,0:T(8,128)(2,1)S(1)}, bf16[256,2048]{1,0:T(8,128)(2,1)S(1)}, u32[]{:S(2)}, u32[]{:S(2)}) collective-permute-start(bf16[256,2048]{1,0:T(8,128)(2,1)S(1)} %get-tuple-element.24), channel_id=1, source_target_pairs={{0,3},{1,0},{2,1},{3,2},{4,5},{5,6},{6,7},{7,4},{8,11},{9,8},{10,9... | collective-permute-start | bytes 3145736 | tf_op jit(solution)/shard_map/ppermute | solution.py:43
  50.5 22.5 %copy-start.6 = (bf16[256,2048]{1,0:T(8,128)(2,1)}, bf16[256,2048]{1,0:T(8,128)(2,1)S(1)}, u32[]{:S(2)}) copy-start(bf16[256,2048]{1,0:T(8,128)(2,1)S(1)} %collective-permute-done.2.refs_2_) | copy-start | bytes 3145732
  50.5 38.0 %collective-permute-start.7 = (bf16[256,2048]{1,0:T(8,128)(2,1)S(1)}, bf16[256,2048]{1,0:T(8,128)(2,1)S(1)}, u32[]{:S(2)}, u32[]{:S(2)}) collective-permute-start(bf16[256,2048]{1,0:T(8,128)(2,1)S(1)} %get-tuple-element.23), channel_id=1, source_target_pairs={{0,3},{1,0},{2,1},{3,2},{4,5},{5,6},{6,7},{7,4},{8,11},{9,8},{10,9... | collective-permute-start | bytes 3145736 | tf_op jit(solution)/shard_map/ppermute | solution.py:43
  73.0 21.1 %collective-permute-start = (bf16[256,2048]{1,0:T(8,128)(2,1)S(1)}, bf16[256,2048]{1,0:T(8,128)(2,1)S(1)}, u32[]{:S(2)}, u32[]{:S(2)}) collective-permute-start(bf16[256,2048]{1,0:T(8,128)(2,1)S(1)} %slice.18), channel_id=1, source_target_pairs={{0,1},{1,2},{2,3},{3,0},{4,7},{5,4},{6,5},{7,6},{8,9},{9,10},{10,1... | collective-permute-start | bytes 3145736 | tf_op jit(solution)/shard_map/ppermute | solution.py:43
  75.5 85.7 %copy-start.1 = (bf16[1024,1024]{1,0:T(8,128)(2,1)}, bf16[1024,1024]{1,0:T(8,128)(2,1)S(1)}, u32[]{:S(2)}) copy-start(bf16[1024,1024]{1,0:T(8,128)(2,1)S(1)} %pad_maximum_fusion.refs_8_) | copy-start | bytes 6291460
  75.5 49.5 %copy-start.8 = (bf16[256,2048]{1,0:T(8,128)(2,1)}, bf16[256,2048]{1,0:T(8,128)(2,1)S(1)}, u32[]{:S(2)}) copy-start(bf16[256,2048]{1,0:T(8,128)(2,1)S(1)} %collective-permute-done.5.refs_5_) | copy-start | bytes 3145732
  75.5 49.0 %collective-permute-start.12 = (bf16[1024,1024]{1,0:T(8,128)(2,1)S(1)}, bf16[1024,1024]{1,0:T(8,128)(2,1)S(1)}, u32[]{:S(2)}, u32[]{:S(2)}) collective-permute-start(bf16[1024,1024]{1,0:T(8,128)(2,1)S(1)} %pad_maximum_fusion.refs_8_), channel_id=1, source_target_pairs={{0,32},{4,100},{8,40},{12,108},{16,48},{20,116},{24,56},{28,124},{... | collective-permute-start | bytes 6291464 | tf_op jit(solution)/shard_map/ppermute | solution.py:43
  75.6 48.9 %collective-permute-start.14 = (bf16[1024,1024]{1,0:T(8,128)(2,1)S(1)}, bf16[1024,1024]{1,0:T(8,128)(2,1)S(1)}, u32[]{:S(2)}, u32[]{:S(2)}) collective-permute-start(bf16[1024,1024]{1,0:T(8,128)(2,1)S(1)} %pad_maximum_fusion.refs_8_), channel_id=1, source_target_pairs={{0,96},{4,36},{8,104},{12,44},{16,112},{20,52},{24,120},{28,60},{3... | collective-permute-start | bytes 6291464 | tf_op jit(solution)/shard_map/ppermute | solution.py:43
  80.4 44.7 %copy-start.11 = (bf16[256,2048]{1,0:T(8,128)(2,1)}, bf16[256,2048]{1,0:T(8,128)(2,1)S(1)}, u32[]{:S(2)}) copy-start(bf16[256,2048]{1,0:T(8,128)(2,1)S(1)} %collective-permute-done.6.refs_6_) | copy-start | bytes 3145732
  80.4 44.6 %collective-permute-start.11 = (bf16[1024,1024]{1,0:T(8,128)(2,1)S(1)}, bf16[1024,1024]{1,0:T(8,128)(2,1)S(1)}, u32[]{:S(2)}, u32[]{:S(2)}) collective-permute-start(bf16[1024,1024]{1,0:T(8,128)(2,1)S(1)} %pad_maximum_fusion.refs_8_), channel_id=1, source_target_pairs={{0,4},{4,0},{8,12},{12,8},{16,20},{20,16},{24,28},{28,24},{32,36},... | collective-permute-start | bytes 6291464 | tf_op jit(solution)/shard_map/ppermute | solution.py:43
  88.5 36.9 %copy-start.12 = (bf16[256,2048]{1,0:T(8,128)(2,1)}, bf16[256,2048]{1,0:T(8,128)(2,1)S(1)}, u32[]{:S(2)}) copy-start(bf16[256,2048]{1,0:T(8,128)(2,1)S(1)} %collective-permute-done.7.refs_7_) | copy-start | bytes 3145732
  88.6 36.6 %collective-permute-start.20 = (bf16[1024,1024]{1,0:T(8,128)(2,1)}, bf16[1024,1024]{1,0:T(8,128)(2,1)}, u32[]{:S(2)}, u32[]{:S(2)}) collective-permute-start(bf16[1024,1024]{1,0:T(8,128)(2,1)} %pad_maximum_fusion.1.refs_8_.refs_16_), channel_id=1, source_target_pairs={{0,8},{4,28},{8,16},{12,4},{16,24},{20,12},{24,0},{28,20},{32,40},... | collective-permute-start | bytes 6291464 | tf_op jit(solution)/shard_map/ppermute | solution.py:43
  94.1 31.0 %copy-start.9 = (bf16[256,2048]{1,0:T(8,128)(2,1)}, bf16[256,2048]{1,0:T(8,128)(2,1)S(1)}, u32[]{:S(2)}) copy-start(bf16[256,2048]{1,0:T(8,128)(2,1)S(1)} %collective-permute-done.refs_0_) | copy-start | bytes 3145732
  94.1 14.8 %collective-permute-start.4 = (bf16[256,2048]{1,0:T(8,128)(2,1)S(1)}, bf16[256,2048]{1,0:T(8,128)(2,1)S(1)}, u32[]{:S(2)}, u32[]{:S(2)}) collective-permute-start(bf16[256,2048]{1,0:T(8,128)(2,1)S(1)} %slice.18), channel_id=1, source_target_pairs={{0,3},{1,0},{2,1},{3,2},{4,5},{5,6},{6,7},{7,4},{8,11},{9,8},{10,9... | collective-permute-start | bytes 3145736 | tf_op jit(solution)/shard_map/ppermute | solution.py:43
  108.9 52.3 %copy-start.13 = (bf16[256,2048]{1,0:T(8,128)(2,1)}, bf16[256,2048]{1,0:T(8,128)(2,1)S(1)}, u32[]{:S(2)}) copy-start(bf16[256,2048]{1,0:T(8,128)(2,1)S(1)} %collective-permute-done.4.refs_4_) | copy-start | bytes 3145732
  108.9 33.4 %collective-permute-start.22 = (bf16[1024,1024]{1,0:T(8,128)(2,1)}, bf16[1024,1024]{1,0:T(8,128)(2,1)}, u32[]{:S(2)}, u32[]{:S(2)}) collective-permute-start(bf16[1024,1024]{1,0:T(8,128)(2,1)} %pad_maximum_fusion.1.refs_8_.refs_16_), channel_id=1, source_target_pairs={{0,24},{4,12},{8,0},{12,20},{16,8},{20,28},{24,16},{28,4},{32,56},... | collective-permute-start | bytes 6291464 | tf_op jit(solution)/shard_map/ppermute | solution.py:43
  124.5 22.5 %collective-permute-start.13 = (bf16[1024,1024]{1,0:T(8,128)(2,1)S(1)}, bf16[1024,1024]{1,0:T(8,128)(2,1)S(1)}, u32[]{:S(2)}, u32[]{:S(2)}) collective-permute-start(bf16[1024,1024]{1,0:T(8,128)(2,1)S(1)} %collective-permute-done.12.refs_10_), channel_id=1, source_target_pairs={{0,4},{4,0},{8,12},{12,8},{16,20},{20,16},{24,28},{28,24},{32,36},... | collective-permute-start | bytes 6291464 | tf_op jit(solution)/shard_map/ppermute | solution.py:43
  124.5 27.9 %copy-start.15 = (bf16[1024,1024]{1,0:T(8,128)(2,1)}, bf16[1024,1024]{1,0:T(8,128)(2,1)S(1)}, u32[]{:S(2)}) copy-start(bf16[1024,1024]{1,0:T(8,128)(2,1)S(1)} %collective-permute-done.14.refs_12_) | copy-start | bytes 6291460
  124.5 22.6 %collective-permute-start.15 = (bf16[1024,1024]{1,0:T(8,128)(2,1)S(1)}, bf16[1024,1024]{1,0:T(8,128)(2,1)S(1)}, u32[]{:S(2)}, u32[]{:S(2)}) collective-permute-start(bf16[1024,1024]{1,0:T(8,128)(2,1)S(1)} %collective-permute-done.14.refs_12_), channel_id=1, source_target_pairs={{0,4},{4,0},{8,12},{12,8},{16,20},{20,16},{24,28},{28,24},{32,36},... | collective-permute-start | bytes 6291464 | tf_op jit(solution)/shard_map/ppermute | solution.py:43
  125.0 27.4 %copy-start.16 = (bf16[1024,1024]{1,0:T(8,128)(2,1)}, bf16[1024,1024]{1,0:T(8,128)(2,1)S(1)}, u32[]{:S(2)}) copy-start(bf16[1024,1024]{1,0:T(8,128)(2,1)S(1)} %collective-permute-done.11.refs_9_) | copy-start | bytes 6291460
  125.0 27.4 %collective-permute-start.24 = (bf16[1024,1024]{1,0:T(8,128)(2,1)S(1)}, bf16[1024,1024]{1,0:T(8,128)(2,1)}, u32[]{:S(2)}, u32[]{:S(2)}) collective-permute-start(bf16[1024,1024]{1,0:T(8,128)(2,1)S(1)} %collective-permute-done.12.refs_10_), channel_id=1, source_target_pairs={{0,32},{4,100},{8,40},{12,108},{16,48},{20,116},{24,56},{28,124},{... | collective-permute-start | bytes 6291464 | tf_op jit(solution)/shard_map/ppermute | solution.py:43
  125.1 35.9 %collective-permute-start.26 = (bf16[1024,1024]{1,0:T(8,128)(2,1)}, bf16[1024,1024]{1,0:T(8,128)(2,1)}, u32[]{:S(2)}, u32[]{:S(2)}) collective-permute-start(bf16[1024,1024]{1,0:T(8,128)(2,1)} %collective-permute-done.20.refs_10_.refs_18_), channel_id=1, source_target_pairs={{0,8},{4,28},{8,16},{12,4},{16,24},{20,12},{24,0},{28,20},{32,40},... | collective-permute-start | bytes 6291464 | tf_op jit(solution)/shard_map/ppermute | solution.py:43
  142.3 33.5 %collective-permute-start.19 = (bf16[1024,1024]{1,0:T(8,128)(2,1)}, bf16[1024,1024]{1,0:T(8,128)(2,1)}, u32[]{:S(2)}, u32[]{:S(2)}) collective-permute-start(bf16[1024,1024]{1,0:T(8,128)(2,1)} %pad_maximum_fusion.1.refs_8_.refs_16_), channel_id=1, source_target_pairs={{0,4},{4,0},{8,12},{12,8},{16,20},{20,16},{24,28},{28,24},{32,36},... | collective-permute-start | bytes 6291464 | tf_op jit(solution)/shard_map/ppermute | solution.py:43
  147.0 31.7 %collective-permute-start.21 = (bf16[1024,1024]{1,0:T(8,128)(2,1)}, bf16[1024,1024]{1,0:T(8,128)(2,1)}, u32[]{:S(2)}, u32[]{:S(2)}) collective-permute-start(bf16[1024,1024]{1,0:T(8,128)(2,1)} %collective-permute-done.20.refs_10_.refs_18_), channel_id=1, source_target_pairs={{0,4},{4,0},{8,12},{12,8},{16,20},{20,16},{24,28},{28,24},{32,36},... | collective-permute-start | bytes 6291464 | tf_op jit(solution)/shard_map/ppermute | solution.py:43
  147.1 31.7 %collective-permute-start.23 = (bf16[1024,1024]{1,0:T(8,128)(2,1)}, bf16[1024,1024]{1,0:T(8,128)(2,1)}, u32[]{:S(2)}, u32[]{:S(2)}) collective-permute-start(bf16[1024,1024]{1,0:T(8,128)(2,1)} %collective-permute-done.22.refs_12_.refs_20_), channel_id=1, source_target_pairs={{0,4},{4,0},{8,12},{12,8},{16,20},{20,16},{24,28},{28,24},{32,36},... | collective-permute-start | bytes 6291464 | tf_op jit(solution)/shard_map/ppermute | solution.py:43
  152.4 44.3 %collective-permute-start.25 = (bf16[1024,1024]{1,0:T(8,128)(2,1)}, bf16[1024,1024]{1,0:T(8,128)(2,1)}, u32[]{:S(2)}, u32[]{:S(2)}) collective-permute-start(bf16[1024,1024]{1,0:T(8,128)(2,1)} %collective-permute-done.24.refs_14_), channel_id=1, source_target_pairs={{0,4},{4,0},{8,12},{12,8},{16,20},{20,16},{24,28},{28,24},{32,36},... | collective-permute-start | bytes 6291464 | tf_op jit(solution)/shard_map/ppermute | solution.py:43
  161.1 35.8 %collective-permute-start.27 = (bf16[1024,1024]{1,0:T(8,128)(2,1)}, bf16[1024,1024]{1,0:T(8,128)(2,1)}, u32[]{:S(2)}, u32[]{:S(2)}) collective-permute-start(bf16[1024,1024]{1,0:T(8,128)(2,1)} %collective-permute-done.26.refs_22_), channel_id=1, source_target_pairs={{0,4},{4,0},{8,12},{12,8},{16,20},{20,16},{24,28},{28,24},{32,36},... | collective-permute-start | bytes 6291464 | tf_op jit(solution)/shard_map/ppermute | solution.py:43
  175.8 35.9 %collective-permute-start.29 = (bf16[256,2048]{1,0:T(8,128)(2,1)S(1)}, bf16[256,2048]{1,0:T(8,128)(2,1)S(1)}, u32[]{:S(2)}, u32[]{:S(2)}) collective-permute-start(bf16[256,2048]{1,0:T(8,128)(2,1)S(1)} %copy-done.5), channel_id=1, source_target_pairs={{0,1},{1,2},{2,3},{3,0},{4,7},{5,4},{6,5},{7,6},{8,9},{9,10},{10,1... | collective-permute-start | bytes 3145736 | tf_op jit(solution)/shard_map/ppermute | solution.py:43
  178.7 33.0 %collective-permute-start.30 = (bf16[256,2048]{1,0:T(8,128)(2,1)S(1)}, bf16[256,2048]{1,0:T(8,128)(2,1)S(1)}, u32[]{:S(2)}, u32[]{:S(2)}) collective-permute-start(bf16[256,2048]{1,0:T(8,128)(2,1)S(1)} %copy-done.7), channel_id=1, source_target_pairs={{0,1},{1,2},{2,3},{3,0},{4,7},{5,4},{6,5},{7,6},{8,9},{9,10},{10,1... | collective-permute-start | bytes 3145736 | tf_op jit(solution)/shard_map/ppermute | solution.py:43
  178.8 35.8 %collective-permute-start.28 = (bf16[256,2048]{1,0:T(8,128)(2,1)S(1)}, bf16[256,2048]{1,0:T(8,128)(2,1)S(1)}, u32[]{:S(2)}, u32[]{:S(2)}) collective-permute-start(bf16[256,2048]{1,0:T(8,128)(2,1)S(1)} %copy-done.10), channel_id=1, source_target_pairs={{0,1},{1,2},{2,3},{3,0},{4,7},{5,4},{6,5},{7,6},{8,9},{9,10},{10,1... | collective-permute-start | bytes 3145736 | tf_op jit(solution)/shard_map/ppermute | solution.py:43
  196.8 31.1 %collective-permute-start.31 = (bf16[256,2048]{1,0:T(8,128)(2,1)S(1)}, bf16[256,2048]{1,0:T(8,128)(2,1)S(1)}, u32[]{:S(2)}, u32[]{:S(2)}) collective-permute-start(bf16[256,2048]{1,0:T(8,128)(2,1)S(1)} %copy-done.3), channel_id=1, source_target_pairs={{0,1},{1,2},{2,3},{3,0},{4,7},{5,4},{6,5},{7,6},{8,9},{9,10},{10,1... | collective-permute-start | bytes 3145736 | tf_op jit(solution)/shard_map/ppermute | solution.py:43
  223.8 10.0 %collective-permute-start.35 = (f32[8,768]{1,0:T(8,128)S(1)}, f32[8,768]{1,0:T(8,128)S(1)}, u32[]{:S(2)}, u32[]{:S(2)}) collective-permute-start(f32[8,768]{1,0:T(8,128)S(1)} %get-tuple-element.22.refs_0_), channel_id=1, source_target_pairs={{0,1},{1,2},{2,3},{3,0},{4,7},{5,4},{6,5},{7,6},{8,9},{9,10},{10,1... | collective-permute-start | bytes 73736 | tf_op jit(solution)/shard_map/ppermute | solution.py:43
  225.8 9.8 %collective-permute-start.36 = (f32[8,768]{1,0:T(8,128)S(1)}, f32[8,768]{1,0:T(8,128)S(1)}, u32[]{:S(2)}, u32[]{:S(2)}) collective-permute-start(f32[8,768]{1,0:T(8,128)S(1)} %get-tuple-element.22.refs_0_), channel_id=1, source_target_pairs={{0,3},{1,0},{2,1},{3,2},{4,5},{5,6},{6,7},{7,4},{8,11},{9,8},{10,9... | collective-permute-start | bytes 73736 | tf_op jit(solution)/shard_map/ppermute | solution.py:43
  227.3 8.2 %collective-permute-start.37 = (f32[8,768]{1,0:T(8,128)S(1)}, f32[8,768]{1,0:T(8,128)S(1)}, u32[]{:S(2)}, u32[]{:S(2)}) collective-permute-start(f32[8,768]{1,0:T(8,128)S(1)} %get-tuple-element.22.refs_0_), channel_id=1, source_target_pairs={{0,2},{1,3},{2,0},{3,1},{4,6},{5,7},{6,4},{7,5},{8,10},{9,11},{10,... | collective-permute-start | bytes 73736 | tf_op jit(solution)/shard_map/ppermute | solution.py:53
  230.5 9.0 %collective-permute-start.32 = (f32[8,256]{1,0:T(8,128)S(1)}, f32[8,256]{1,0:T(8,128)S(1)}, u32[]{:S(2)}, u32[]{:S(2)}) collective-permute-start(f32[8,256]{1,0:T(8,128)S(1)} %get-tuple-element.21.refs_0_), channel_id=1, source_target_pairs={{0,1},{1,2},{2,3},{3,0},{4,7},{5,4},{6,5},{7,6},{8,9},{9,10},{10,1... | collective-permute-start | bytes 24584 | tf_op jit(solution)/shard_map/ppermute | solution.py:43
  231.6 7.9 %collective-permute-start.33 = (f32[8,256]{1,0:T(8,128)S(1)}, f32[8,256]{1,0:T(8,128)S(1)}, u32[]{:S(2)}, u32[]{:S(2)}) collective-permute-start(f32[8,256]{1,0:T(8,128)S(1)} %get-tuple-element.21.refs_0_), channel_id=1, source_target_pairs={{0,3},{1,0},{2,1},{3,2},{4,5},{5,6},{6,7},{7,4},{8,11},{9,8},{10,9... | collective-permute-start | bytes 24584 | tf_op jit(solution)/shard_map/ppermute | solution.py:43
  233.8 5.7 %collective-permute-start.34 = (f32[8,256]{1,0:T(8,128)S(1)}, f32[8,256]{1,0:T(8,128)S(1)}, u32[]{:S(2)}, u32[]{:S(2)}) collective-permute-start(f32[8,256]{1,0:T(8,128)S(1)} %get-tuple-element.21.refs_0_), channel_id=1, source_target_pairs={{0,2},{1,3},{2,0},{3,1},{4,6},{5,7},{6,4},{7,5},{8,10},{9,11},{10,... | collective-permute-start | bytes 24584 | tf_op jit(solution)/shard_map/ppermute | solution.py:53
  (9 other events, 133.3 us)
where the time goes:
time: 242 us; the launch traced here: 241 us
  waiting for transfers between devices  121 us (50%)
  Pallas kernels  62.6 us (26%)
  starting transfers between devices  52.4 us (22%)
  local copies, waits for them, and re-layouts  3.19 us (1%)
    ppermute x36, waiting for transfers between devices, move(): return lax.ppermute(value, name, along(axis, first))  121 us
    ppermute x36, starting transfers between devices, move(): return lax.ppermute(value, name, along(axis, first))  50.1 us
    pallas_call x1, Pallas kernels, near(): call(right_kernel, total, [SMEM, VMEM] + [ANY] * 15, VMEM, scratch(9 * se...  16 us
    pallas_call x1, Pallas kernels, near(): call(rest_kernel, (total, pltpu.VMEM((parts, depth, NT), left.dtype)), [S...  14.8 us
    pallas_call x1, Pallas kernels, near(): call(left_kernel, total, [SMEM] + [ANY] * 15, VMEM, scratch(8 * seg, 8 *...  14.6 us
    pallas_call x2, Pallas kernels, far(): call(functools.partial(far_kernel, low), out, [VMEM, VMEM] + [ANY] * len(...  11.7 us
    pallas_call x2, Pallas kernels, scale(): call(functools.partial(scale_kernel, low, cols), jax.ShapeDtypeStruct(acc...  5.58 us
  transfers between devices with their start and end apart: 38, of which 12 were waited for; matrix products, arithmetic and copies ran while one was open for 1% of the time, Pallas kernels for 25%

commit v1 on v0

--- a/solution.py
+++ b/solution.py
@@ -8,12 +8,12 @@
 from jax.sharding import PartitionSpec as P
 
 
-ROW_CHUNKS = 4
+ROW_CHUNKS = (384, 384, 256)
 NX = NY = NZ = 4
 NC = 2
 MT, NT = 512, 512
 
-FAR_MIB = 6
+NEAR_MIB, FAR_MIB = 11, 6
 
 
 def gy(y, x, c):
@@ -112,14 +112,12 @@
 
 def copy_left(sources, b, place, seg, dst, sem):
     for x in range(4):
-        wanted, at = place(x)
-
-        @pl.when(wanted)
-        def _():
-            col = pl.ds(pl.multiple_of(at, seg), seg)
-            for i, chunk in enumerate(sources[b]):
-                size = chunk.shape[0]
-                pltpu.make_async_copy(chunk.at[:, pl.ds(x * seg, seg)], dst.at[pl.ds(i * size, size), col], sem).start()
+        col = pl.ds(pl.multiple_of(place(x), seg), seg)
+        low = 0
+        for chunk in sources[b]:
+            to = dst.at[pl.ds(low, chunk.shape[0]), col]
+            pltpu.make_async_copy(chunk.at[:, pl.ds(x * seg, seg)], to, sem).start()
+            low += chunk.shape[0]
 
 
 def landed(ref, sem):
@@ -128,6 +126,10 @@
 
 def nest(flat):
     return [[[flat[(h * 4 + line) * 2 + q] for q in range(2)] for line in range(4)] for h in range(2)]
+
+
+def spot(p, t, seg):
+    return jnp.where(t == 3, jnp.where(p == 2, 11, p), 2 + 3 * p + t) * seg
 
 
 def multiply(a_v, tile, acc, col, spans, add):
@@ -145,90 +147,75 @@
 
 
 def left_kernel(pos, left, *refs):
-    sources, lines = ([left], refs[:4], refs[4:8]), refs[8:14]
-    acc, a_v, t_v, a_sem, t_sem = refs[14:]
+    count = len(ROW_CHUNKS)
+    sources, lines = ([left], refs[:count], refs[count:count + 1]), refs[count + 1:count + 7]
+    acc, a_v, t_v, a_sem, t_sem = refs[count + 7:]
     pieces = [[lines[2 * k:2 * k + 2] for k in range(3)]]
     _, depth = left.shape
     half, nt, seg, x0 = acc.shape[1] // 2, t_v.shape[2], depth // 4, pos[1]
     blocks, where = plan(pos)
 
-    def fetch(s, p):
-        copy_left_half(
-            pos, pieces, s * nt, blocks[p], range(3), lambda t: (4 * p + t) * seg, t_v.at[s % 2], t_sem.at[s % 2, p])
+    def fetch(s):
+        for p in range(2):
+            copy_left_half(
+                pos, pieces, s * nt, blocks[p], range(3), lambda t: spot(p, t, seg), t_v.at[s % 2], t_sem.at[s % 2, p])
 
     for b in range(3):
-        copy_left(sources, b, lambda x: (where[b] < 2, (4 * where[b] + turned(x, x0)) * seg),
-                  seg, a_v, a_sem.at[jnp.minimum(where[b], 1)])
-        if b < 2:
-            fetch(0, b)
+        copy_left(sources, b, lambda x: spot(where[b], turned(x, x0), seg), seg, a_v, a_sem.at[where[b]])
+        if b == 0:
+            fetch(0)
     for s in range(half // nt):
-        tile, col = t_v.at[s % 2], s * nt
-        for p in range(2):
-            if col + nt < half:
-                fetch(s + 1, p)
+        if (s + 1) * nt < half:
+            fetch(s + 1)
         for p in range(2):
             if s == 0:
                 landed(a_v.at[:, pl.ds(0, 4 * seg)], a_sem.at[p])
-            landed(tile.at[pl.ds(0, 4 * seg), :], t_sem.at[s % 2, p])
+            landed(t_v.at[s % 2, pl.ds(0, 4 * seg), :], t_sem.at[s % 2, p])
             if s == 0:
-                multiply(a_v, tile, acc, col, ((4 * p * seg, 4 * p * seg, 4 * seg),), p > 0)
+                one, three = p * seg, (2 + 3 * p) * seg
+                multiply(a_v, t_v.at[0], acc, 0, ((one, one, seg), (three, three, 3 * seg)), p > 0)
         if s > 0:
-            multiply(a_v, tile, acc, col, ((0, 0, 8 * seg),), False)
-
-
-def right_kernel(pos, before, left, *refs):
-    sources, lines = ([left], refs[:4], refs[4:8]), refs[8:14]
-    acc, a_v, t_v, a_sem, t_sem = refs[14:]
+            multiply(a_v, t_v.at[s % 2], acc, s * nt, ((0, 0, 8 * seg),), False)
+    landed(a_v.at[:, pl.ds(0, 4 * seg)], a_sem.at[2])
+
+
+def right_kernel(pos, a_v, before, *refs):
+    lines, (acc, _, t_v, t_sem) = refs[:6], refs[6:]
     pieces = [None, [lines[2 * k:2 * k + 2] for k in range(3)]]
-    _, depth = left.shape
-    half, nt, seg, x0 = acc.shape[1] // 2, t_v.shape[2], depth // 4, pos[1]
-    blocks, where = plan(pos)
+    half, nt, seg = acc.shape[1] // 2, t_v.shape[2], a_v.shape[1] // 12
+    blocks, _ = plan(pos)
 
     def fetch(s, p):
         copy_right_half(
             pos, pieces, s * nt, [blocks[p]], range(3), lambda _, t: (3 * p + t) * seg, t_v.at[s % 2], t_sem.at[s % 2, p])
 
-    for b in range(3):
-        copy_left(sources, b, lambda x: (turned(x, x0) < 3, (3 * where[b] + turned(x, x0)) * seg),
-                  seg, a_v, a_sem.at[where[b]])
-        fetch(0, b)
+    for p in range(3):
+        fetch(0, p)
     for s in range(half // nt):
-        tile, col = t_v.at[s % 2], half + s * nt
         for p in range(3):
             if (s + 1) * nt < half:
                 fetch(s + 1, p)
         for p in range(3):
+            landed(t_v.at[s % 2, pl.ds(0, 3 * seg), :], t_sem.at[s % 2, p])
             if s == 0:
-                landed(a_v.at[:, pl.ds(0, 3 * seg)], a_sem.at[p])
-            landed(tile.at[pl.ds(0, 3 * seg), :], t_sem.at[s % 2, p])
-            if s == 0:
-                multiply(a_v, tile, acc, col, ((3 * p * seg, 3 * p * seg, 3 * seg),), p > 0)
+                multiply(a_v, t_v.at[0], acc, half, (((2 + 3 * p) * seg, 3 * p * seg, 3 * seg),), p > 0)
         if s > 0:
-            multiply(a_v, tile, acc, col, ((0, 0, 9 * seg),), False)
-
-
-def rest_kernel(pos, before, left, *refs):
-    sources, pieces = ([left], refs[:4], refs[4:8]), nest(refs[8:24])
-    acc, far_v, a_v, t_v, a_sem, t_sem, f_sem = refs[24:]
-    _, depth = left.shape
-    half, nt, seg, x0 = acc.shape[1] // 2, t_v.shape[2], depth // 4, pos[1]
-    blocks, where = plan(pos)
+            multiply(a_v, t_v.at[s % 2], acc, half + s * nt, ((2 * seg, 0, 9 * seg),), False)
+
+
+def rest_kernel(pos, a_v, before, *refs):
+    pieces, (acc, far_v, t_v, t_sem, f_sem) = nest(refs[:16]), refs[16:]
+    half, nt, seg = acc.shape[1] // 2, t_v.shape[2], a_v.shape[1] // 12
+    blocks, _ = plan(pos)
     parts = half // nt
     for s in range(parts):
-        copy_left_half(
-            pos, pieces, s * nt, blocks[2], range(4), lambda t: lax.rem(t + 1, 4) * seg, t_v.at[s], t_sem.at[s])
-        if s == 0:
-            for b in range(3):
-                copy_left(sources, b, lambda x: (
-                    (where[b] == 2) | (turned(x, x0) == 3),
-                    jnp.where(turned(x, x0) == 3, where[b], 3 + turned(x, x0)) * seg), seg, a_v,
-                    a_sem.at[jnp.where(where[b] == 2, 0, 1)])
+        copy_left_half(pos, pieces, s * nt, blocks[2], range(4), lambda t: t * seg, t_v.at[s], t_sem.at[s])
     for s in range(parts):
         copy_right_half(
             pos, pieces, s * nt, blocks, (3,), lambda p, t: p * seg, t_v.at[parts + s], t_sem.at[parts + s])
 
     def place(t):
-        return lax.rem(x0 + t + 3, 4) * seg
+        return lax.rem(pos[1] + t + 3, 4) * seg
 
     opposite = lax.rem(pos[3] + 2, 4)
     for s in range(parts):
@@ -236,13 +223,10 @@
         copy_right_half(
             pos, pieces, s * nt, [opposite], range(4), lambda _, t: place(t), far_v.at[parts + s], f_sem)
     for s in range(2 * parts):
-        if s == 0:
-            landed(a_v.at[:, pl.ds(2 * seg, 4 * seg)], a_sem.at[0])
-        if s == parts:
-            landed(a_v.at[:, pl.ds(0, 2 * seg)], a_sem.at[1])
-        first, size = (2 * seg, 4 * seg) if s < parts else (0, 3 * seg)
+        size = (4 if s < parts else 3) * seg
         landed(t_v.at[s, pl.ds(0, size), :], t_sem.at[s])
-        multiply(a_v, t_v.at[s], acc, s * nt, ((first, 0, size),), True)
+        spans = ((8 * seg, 0, 4 * seg),) if s < parts else ((0, 0, 2 * seg), (11 * seg, 2 * seg, seg))
+        multiply(a_v, t_v.at[s], acc, s * nt, spans, True)
     landed(far_v, f_sem)
 
 
@@ -267,11 +251,11 @@
 
 
 def far_kernel(low, before, t_in, *refs):
-    count = len(refs) - 6
-    chunks, (acc, t_v, power, a_v, p_v, a_sem) = refs[:count], refs[count:]
-    rc = a_v.shape[0] // count
-    for i, chunk in enumerate(chunks):
-        pltpu.make_async_copy(chunk, a_v.at[pl.ds(i * rc, rc), :], a_sem).start()
+    chunks, (acc, t_v, power, a_v, p_v, a_sem) = refs[:-6], refs[-6:]
+    at = 0
+    for chunk in chunks:
+        pltpu.make_async_copy(chunk, a_v.at[pl.ds(at, chunk.shape[0]), :], a_sem).start()
+        at += chunk.shape[0]
     landed(a_v, a_sem)
     for s in range(t_v.shape[0]):
         far_multiply(low, min(256, a_v.shape[0]), a_v, t_in.at[s], acc, p_v, s)
@@ -328,28 +312,24 @@
     total = pltpu.VMEM((rows, 2 * half), jnp.float32)
     flops = 2 * rows * half * seg
     dma = pltpu.SemaphoreType.DMA
-    blocks = [left, *behind, *ahead]
-
-    def scratch(size, depth, parts):
-        return [pltpu.VMEM((rows, size), left.dtype), pltpu.VMEM((parts, depth, NT), left.dtype), dma((3,))]
-
-    acc = call(
-        left_kernel, total, [SMEM] + [ANY] * 15, VMEM, scratch(8 * seg, 8 * seg, 2) + [dma((2, 2))], 8 * flops, 18,
-    )(pos, *blocks, *pieces[:6])
-    acc = call(
-        right_kernel, total, [SMEM, VMEM] + [ANY] * 15, VMEM, scratch(9 * seg, 9 * seg, 2) + [dma((2, 3))],
-        9 * flops, 20, {1: 0},
-    )(pos, kept(acc), *blocks, *pieces[8:14])
+    acc, blocks = call(
+        left_kernel, (total, pltpu.VMEM((rows, 12 * seg), left.dtype)), [SMEM] + [ANY] * (8 + len(ROW_CHUNKS)), (VMEM, VMEM),
+        [pltpu.VMEM((2, 8 * seg, NT), left.dtype), dma((3,)), dma((2, 2))], 8 * flops, NEAR_MIB,
+    )(pos, left, *behind, ahead, *pieces[:6])
+    acc, blocks = call(
+        right_kernel, (total, pltpu.VMEM(blocks.shape, blocks.dtype)), [SMEM, VMEM, VMEM] + [ANY] * 6, (VMEM, VMEM),
+        [pltpu.VMEM((2, 9 * seg, NT), left.dtype), dma((2, 3))], 9 * flops, NEAR_MIB, {1: 1, 2: 0},
+    )(pos, kept(blocks), kept(acc), *pieces[8:14])
     parts = 2 * half // NT
     return call(
-        rest_kernel, (total, pltpu.VMEM((parts, depth, NT), left.dtype)), [SMEM, VMEM] + [ANY] * 25, (VMEM, VMEM),
-        scratch(6 * seg, depth, parts) + [dma((parts,)), dma], 7 * flops, 16, {1: 0},
-    )(pos, kept(acc), *blocks, *pieces)
+        rest_kernel, (total, pltpu.VMEM((parts, depth, NT), left.dtype)), [SMEM, VMEM, VMEM] + [ANY] * 16, (VMEM, VMEM),
+        [pltpu.VMEM((parts, depth, NT), left.dtype), dma((parts,)), dma], 7 * flops, NEAR_MIB, {2: 0},
+    )(pos, kept(blocks), kept(acc), *pieces)
 
 
 def far(low, acc, tile, chunks):
-    rc, depth = chunks[0].shape
-    rows = rc * len(chunks)
+    depth = chunks[0].shape[1]
+    rows = sum(chunk.shape[0] for chunk in chunks)
     out = pltpu.VMEM(acc.shape, acc.dtype), pltpu.VMEM(tile.shape, tile.dtype), jax.ShapeDtypeStruct((8, rows), jnp.float32)
     return call(
         functools.partial(far_kernel, low), out, [VMEM, VMEM] + [ANY] * len(chunks), (VMEM, VMEM, VMEM),
@@ -371,12 +351,16 @@
 def per_device(left, right):
     rows, _ = left.shape
     width = right.shape[1]
-    rc, half = rows // ROW_CHUNKS, width // 2
+    half = width // 2
     me, z = lax.axis_index("gy"), lax.axis_index("gx")
     pos = jnp.stack([me // (NX * NC), (me // NC) % NX, me % NC, z]).astype(jnp.int32)
 
-    head, left_too = lax.optimization_barrier((left[:rc], left))
-    lefts = [ring(left_too[i * rc:(i + 1) * rc] if i else head, "z") for i in range(ROW_CHUNKS)]
+    ahead = move(left, "z", False)
+    behind, opposite, low = [], [], 0
+    for i, size in enumerate(ROW_CHUNKS):
+        behind.append(move(left[low:low + size], "z", True))
+        opposite.append(move(behind[i], "z", True))
+        low += size
     pieces = []
     for h, (a, b) in enumerate((("x", "y"), ("y", "x"))):
         line = jnp.concatenate(ring(right[:, h * half:(h + 1) * half], a), axis=0)
@@ -384,12 +368,11 @@
             pieces += [v, move(v, "core", True)]
 
     pieces = [apart(v) for v in pieces]
-    sides = [[apart(c[k]) for c in lefts] for k in (1, 2)]
-    acc, tile = near(pos, apart(left), *sides, pieces)
-    low = rows - rc
-    acc, tile, power = far(0, acc, tile, [c[3] for c in lefts[:-1]])
+    acc, tile = near(pos, apart(left), [apart(v) for v in behind], apart(ahead), pieces)
+    low = rows - ROW_CHUNKS[-1]
+    acc, tile, power = far(0, acc, tile, opposite[:-1])
     first = exchange(power)
-    acc, tile, power = far(low, acc, tile, [lefts[-1][3]])
+    acc, tile, power = far(low, acc, tile, opposite[-1:])
     second = exchange(power)
     return scale(low, width * NZ, acc, second, scale(0, width * NZ, acc, first, None))
 

time: 242 us -> 253 us (1.045)
  waiting for transfers between devices: 121 us -> 143 us
  starting transfers between devices: 52.4 us -> 44.6 us
  Pallas kernels: 62.6 us -> 57.4 us
    ppermute x36 -> x31, waiting for transfers between devices: 121 us -> 143 us  [move(): return lax.ppermute(value, name, along(axis, first))]
    ppermute x36 -> x31, starting transfers between devices: 50.1 us -> 42.3 us  [move(): return lax.ppermute(value, name, along(axis, first))]
    pallas_call x1, Pallas kernels: 14.8 us -> 11.7 us  [near(): call(rest_kernel, (total, pltpu.VMEM((parts, depth, NT), left.dtype)), [S...]
  transfers between devices with their start and end apart: 38 -> 33, of which waited for: 12 -> 13; matrix products, arithmetic and copies ran while one was open for 1% -> 2% of each run, Pallas kernels for 25% -> 22%
where the time goes in v1:
time: 253 us; the launch traced here: 252 us
  waiting for transfers between devices  143 us (57%)
  Pallas kernels  57.4 us (23%)
  starting transfers between devices  44.6 us (18%)
  local copies, waits for them, and re-layouts  3.7 us (1%)
    ppermute x31, waiting for transfers between devices, move(): return lax.ppermute(value, name, along(axis, first))  143 us
    ppermute x31, starting transfers between devices, move(): return lax.ppermute(value, name, along(axis, first))  42.3 us
    pallas_call x1, Pallas kernels, near(): call(left_kernel, (total, pltpu.VMEM((rows, 12 * seg), left.dtype)), [SME...  15.5 us
    pallas_call x1, Pallas kernels, near(): call(right_kernel, (total, pltpu.VMEM(blocks.shape, blocks.dtype)), [SMEM...  13.1 us
    pallas_call x1, Pallas kernels, near(): call(rest_kernel, (total, pltpu.VMEM((parts, depth, NT), left.dtype)), [S...  11.7 us
    pallas_call x2, Pallas kernels, far(): call(functools.partial(far_kernel, low), out, [VMEM, VMEM] + [ANY] * len(...  11.5 us
    pallas_call x2, Pallas kernels, scale(): call(functools.partial(scale_kernel, low, cols), jax.ShapeDtypeStruct(acc...  5.58 us
  transfers between devices with their start and end apart: 33, of which 13 were waited for; matrix products, arithmetic and copies ran while one was open for 2% of the time, Pallas kernels for 22%

profile of v1, /device:TPU:0, one launch (start us, length us, event | category | flops | bytes accessed | tf_op | source)
XLA Modules:
  0.0 251.5 jit_solution(12836216113021406468)
XLA Ops:
  0.0 1.3 fusion.1
  1.3 1.7 collective-permute-start.4
  2.9 1.6 collective-permute-start.5
  4.6 11.3 %collective-permute-done.4 = bf16[256,1024]{1,0:T(8,128)(2,1)S(1)} collective-permute-done((bf16[256,1024]{1,0:T(8,128)(2,1)S(1)}, bf16[256,1024]{1,0:T(8,128)(2,1)S(1)}, u32[]{:S(2)}, u32[]{:S(2)}) %collective-permute-start.4) | collective-permute-done | bytes 524320 | tf_op jit(solution)/shard_map/ppermute | solution.py:43
  15.9 1.7 collective-permute-start.6
  17.6 2.3 fusion
  19.9 2.0 collective-permute-start
  21.9 1.6 collective-permute-start.12
  23.5 2.8 %collective-permute-done.6 = bf16[256,1024]{1,0:T(8,128)(2,1)S(1)} collective-permute-done((bf16[256,1024]{1,0:T(8,128)(2,1)S(1)}, bf16[256,1024]{1,0:T(8,128)(2,1)S(1)}, u32[]{:S(2)}, u32[]{:S(2)}) %collective-permute-start.6) | collective-permute-done | bytes 524320 | tf_op jit(solution)/shard_map/ppermute | solution.py:43
  26.5 1.9 collective-permute-start.8
  28.4 2.0 collective-permute-start.2
  30.4 1.7 collective-permute-start.13
  32.3 3.5 %collective-permute-start.1 = (bf16[384,2048]{1,0:T(8,128)(2,1)S(1)}, bf16[384,2048]{1,0:T(8,128)(2,1)S(1)}, u32[]{:S(2)}, u32[]{:S(2)}) collective-permute-start(bf16[384,2048]{1,0:T(8,128)(2,1)S(1)} %get-tuple-element.27), channel_id=1, source_target_pairs={{0,1},{1,2},{2,3},{3,0},{4,7},{5,4},{6,5},{7,6},{8,9},{9,10},{10,1... | collective-permute-start | bytes 4718600 | tf_op jit(solution)/shard_map/ppermute | solution.py:43
  35.8 9.5 %collective-permute-done.13 = bf16[256,1024]{1,0:T(8,128)(2,1)S(1)} collective-permute-done((bf16[256,1024]{1,0:T(8,128)(2,1)S(1)}, bf16[256,1024]{1,0:T(8,128)(2,1)S(1)}, u32[]{:S(2)}, u32[]{:S(2)}) %collective-permute-start.13) | collective-permute-done | bytes 524320 | tf_op jit(solution)/shard_map/ppermute | solution.py:43
  45.2 1.6 collective-permute-start.14
  46.8 6.8 %collective-permute-done.2.refs_2_ = bf16[256,2048]{1,0:T(8,128)(2,1)S(1)} collective-permute-done((bf16[256,2048]{1,0:T(8,128)(2,1)S(1)}, bf16[256,2048]{1,0:T(8,128)(2,1)S(1)}, u32[]{:S(2)}, u32[]{:S(2)}) %collective-permute-start.2) | collective-permute-done | bytes 1048608 | tf_op jit(solution)/shard_map/ppermute | solution.py:43
  53.6 2.0 collective-permute-start.3
  55.7 10.3 %collective-permute-done.14 = bf16[256,1024]{1,0:T(8,128)(2,1)S(1)} collective-permute-done((bf16[256,1024]{1,0:T(8,128)(2,1)S(1)}, bf16[256,1024]{1,0:T(8,128)(2,1)S(1)}, u32[]{:S(2)}, u32[]{:S(2)}) %collective-permute-start.14) | collective-permute-done | bytes 524320 | tf_op jit(solution)/shard_map/ppermute | solution.py:43
  66.0 1.8 collective-permute-start.10
  67.8 1.7 pad_maximum_fusion.1.refs_0_.refs_8_
  69.5 14.9 %collective-permute-done.1.refs_1_ = bf16[384,2048]{1,0:T(8,128)(2,1)S(1)} collective-permute-done((bf16[384,2048]{1,0:T(8,128)(2,1)S(1)}, bf16[384,2048]{1,0:T(8,128)(2,1)S(1)}, u32[]{:S(2)}, u32[]{:S(2)}) %collective-permute-start.1) | collective-permute-done | bytes 1572896 | tf_op jit(solution)/shard_map/ppermute | solution.py:43
  84.4 3.2 %collective-permute-start.16 = (bf16[1024,1024]{1,0:T(8,128)(2,1)}, bf16[1024,1024]{1,0:T(8,128)(2,1)}, u32[]{:S(2)}, u32[]{:S(2)}) collective-permute-start(bf16[1024,1024]{1,0:T(8,128)(2,1)} %pad_maximum_fusion.1.refs_0_.refs_8_), channel_id=1, source_target_pairs={{0,8},{4,28},{8,16},{12,4},{16,24},{20,12},{24,0},{28,20},{32,40},... | collective-permute-start | bytes 6291464 | tf_op jit(solution)/shard_map/ppermute | solution.py:43
  87.7 4.3 %collective-permute-done.10.refs_8_.refs_4_ = bf16[1024,1024]{1,0:T(8,128)(2,1)S(1)} collective-permute-done((bf16[1024,1024]{1,0:T(8,128)(2,1)S(1)}, bf16[1024,1024]{1,0:T(8,128)(2,1)S(1)}, u32[]{:S(2)}, u32[]{:S(2)}) %collective-permute-start.10) | collective-permute-done | bytes 2097184 | tf_op jit(solution)/shard_map/ppermute | solution.py:43
  92.0 1.2 collective-permute-start.9
  93.3 36.7 %collective-permute-done.16.refs_2_.refs_10_ = bf16[1024,1024]{1,0:T(8,128)(2,1)} collective-permute-done((bf16[1024,1024]{1,0:T(8,128)(2,1)}, bf16[1024,1024]{1,0:T(8,128)(2,1)}, u32[]{:S(2)}, u32[]{:S(2)}) %collective-permute-start.16) | collective-permute-done | bytes 2097184 | tf_op jit(solution)/shard_map/ppermute | solution.py:43
  130.0 1.6 collective-permute-start.20
  131.6 0.5 collective-permute-start.22
  132.2 0.5 collective-permute-start.17
  132.8 24.6 %collective-permute-done.20.refs_6_ = bf16[1024,1024]{1,0:T(8,128)(2,1)} collective-permute-done((bf16[1024,1024]{1,0:T(8,128)(2,1)S(1)}, bf16[1024,1024]{1,0:T(8,128)(2,1)}, u32[]{:S(2)}, u32[]{:S(2)}) %collective-permute-start.20) | collective-permute-done | bytes 2097184 | tf_op jit(solution)/shard_map/ppermute | solution.py:43
  157.4 1.8 collective-permute-done.22.refs_14_
  159.3 15.5 %shard_map.28 = (f32[1024,2048]{1,0:T(8,128)S(1)}, bf16[1024,6144]{1,0:T(8,128)(2,1)S(1)}) custom-call(s32[4]{0:T(128)S(1)} %pad_add_fusion.pos, bf16[1024,2048]{1,0:T(8,128)(2,1)} %left.1, bf16[384,2048]{1,0:T(8,128)(2,1)} %copy-done.8, bf16[384,2048]{1,0:T(8,128)(2,1)} %copy-done.10, bf16[256,2048]{1,0:T(8,128)(2,1)} %copy-done.12, ...), custom_call_target="tpu_custom_call" | custom-call | flops 8589934592 | bytes 16777216 | tf_op jit(solution)/shard_map/pallas_call | solution.py:315
  174.9 2.2 collective-permute-start.26
  177.1 1.3 collective-permute-start.24
  178.3 1.9 collective-permute-start.25
  180.2 13.1 %shard_map.29 = (f32[1024,2048]{1,0:T(8,128)S(1)}, bf16[1024,6144]{1,0:T(8,128)(2,1)S(1)}) custom-call(s32[4]{0:T(128)S(1)} %pad_add_fusion.pos, bf16[1024,6144]{1,0:T(8,128)(2,1)S(1)} %get-tuple-element.16.a_v, f32[1024,2048]{1,0:T(8,128)S(1)} %get-tuple-element.17.before, ...), custom_call_target="tpu_custom_call", output_to_operand_aliasing={{1}: (1, {}), {0}: (2, {})} | custom-call | flops 9663676416 | bytes 16777216 | tf_op jit(solution)/shard_map/pallas_call | solution.py:319
  193.4 11.7 %shard_map.30 = (f32[1024,2048]{1,0:T(8,128)S(1)}, bf16[4,2048,512]{2,1,0:T(8,128)(2,1)S(1)}) custom-call(s32[4]{0:T(128)S(1)} %pad_add_fusion.pos, bf16[1024,6144]{1,0:T(8,128)(2,1)S(1)} %get-tuple-element.18.a_v, f32[1024,2048]{1,0:T(8,128)S(1)} %get-tuple-element.19.before, bf16[1024,1024]{1,0:T(8,128)(2,1)} %copy-done, ...), custom_call_target="tpu_custom_call", output_to_operand_aliasing={{0}: (2, {})} | custom-call | flops 7516192768 | bytes 16777216 | tf_op jit(solution)/shard_map/pallas_call | solution.py:324
  205.1 3.4 %collective-permute-done.24.refs_0_ = bf16[384,2048]{1,0:T(8,128)(2,1)S(1)} collective-permute-done((bf16[384,2048]{1,0:T(8,128)(2,1)S(1)}, bf16[384,2048]{1,0:T(8,128)(2,1)S(1)}, u32[]{:S(2)}, u32[]{:S(2)}) %collective-permute-start.24) | collective-permute-done | bytes 1572896 | tf_op jit(solution)/shard_map/ppermute | solution.py:43
  208.4 16.9 %collective-permute-done.25.refs_1_ = bf16[384,2048]{1,0:T(8,128)(2,1)S(1)} collective-permute-done((bf16[384,2048]{1,0:T(8,128)(2,1)S(1)}, bf16[384,2048]{1,0:T(8,128)(2,1)S(1)}, u32[]{:S(2)}, u32[]{:S(2)}) %collective-permute-start.25) | collective-permute-done | bytes 1572896 | tf_op jit(solution)/shard_map/ppermute | solution.py:43
  225.3 9.0 %shard_map.31 = (f32[1024,2048]{1,0:T(8,128)S(1)}, bf16[4,2048,512]{2,1,0:T(8,128)(2,1)S(1)}, f32[8,768]{1,0:T(8,128)S(1)}) custom-call(f32[1024,2048]{1,0:T(8,128)S(1)} %get-tuple-element.20.before, bf16[4,2048,512]{2,1,0:T(8,128)(2,1)S(1)} %get-tuple-element.21.t_in, ...), custom_call_target="tpu_custom_call", output_to_operand_aliasing={{0}: (0, {}), {1}: (1, {})} | custom-call | flops 6442450944 | bytes 16777216 | tf_op jit(solution)/shard_map/pallas_call | solution.py:334
  234.3 0.4 collective-permute-start.30
  234.6 2.9 %collective-permute-start.31 = (f32[8,768]{1,0:T(8,128)S(1)}, f32[8,768]{1,0:T(8,128)S(1)}, u32[]{:S(2)}, u32[]{:S(2)}) collective-permute-start(f32[8,768]{1,0:T(8,128)S(1)} %get-tuple-element.26.refs_0_), channel_id=1, source_target_pairs={{0,3},{1,0},{2,1},{3,2},{4,5},{5,6},{6,7},{7,4},{8,11},{9,8},{10,9... | collective-permute-start | bytes 73736 | tf_op jit(solution)/shard_map/ppermute | solution.py:43
  237.6 0.4 collective-permute-start.32
  238.0 2.5 %shard_map.32 = (f32[1024,2048]{1,0:T(8,128)S(1)}, bf16[4,2048,512]{2,1,0:T(8,128)(2,1)S(1)}, f32[8,256]{1,0:T(8,128)S(1)}) custom-call(f32[1024,2048]{1,0:T(8,128)S(1)} %get-tuple-element.22.before, bf16[4,2048,512]{2,1,0:T(8,128)(2,1)S(1)} %get-tuple-element.23.t_in, ...), custom_call_target="tpu_custom_call", output_to_operand_aliasing={{0}: (0, {}), {1}: (1, {})} | custom-call | flops 2147483648 | bytes 16777216 | tf_op jit(solution)/shard_map/pallas_call | solution.py:334
  240.5 1.4 collective-permute-start.27
  241.9 2.0 collective-permute-start.28
  243.8 1.9 collective-permute-start.29
  245.8 4.0 %shard_map.33.refs_4_ = f32[1024,2048]{1,0:T(8,128)} custom-call(f32[1024,2048]{1,0:T(8,128)S(1)} %get-tuple-element.24.acc, f32[8,768]{1,0:T(8,128)S(1)} %get-tuple-element.26.refs_0_, f32[8,768]{1,0:T(8,128)S(1)} %collective-permute-done.30.refs_1_, f32[8,768]{1,0:T(8,128)S(1)} %collective-permute-done.31.refs_2_, f32[8,768]{1,0:T(8,128)S(1)} %collective-permute-done.32.refs_3_), custom_call_target="tpu_custom_call" | custom-call | flops 47185920 | bytes 16777216 | tf_op jit(solution)/shard_map/pallas_call | solution.py:343
  249.8 1.6 shard_map.34
  (59 shorter events, 1.1 us)
Async XLA Ops:
  1.3 14.6 %collective-permute-start.4 = (bf16[256,1024]{1,0:T(8,128)(2,1)S(1)}, bf16[256,1024]{1,0:T(8,128)(2,1)S(1)}, u32[]{:S(2)}, u32[]{:S(2)}) collective-permute-start(bf16[256,1024]{1,0:T(8,128)(2,1)S(1)} %get-tuple-element.30), channel_id=1, source_target_pairs={{0,8},{4,28},{8,16},{12,4},{16,24},{20,12},{24,0},{28,20},{32,40},... | collective-permute-start | bytes 1572872 | tf_op jit(solution)/shard_map/ppermute | solution.py:43
  2.9 20.5 %collective-permute-start.5 = (bf16[256,1024]{1,0:T(8,128)(2,1)S(1)}, bf16[256,1024]{1,0:T(8,128)(2,1)S(1)}, u32[]{:S(2)}, u32[]{:S(2)}) collective-permute-start(bf16[256,1024]{1,0:T(8,128)(2,1)S(1)} %get-tuple-element.30), channel_id=1, source_target_pairs={{0,24},{4,12},{8,0},{12,20},{16,8},{20,28},{24,16},{28,4},{32,56},... | collective-permute-start | bytes 1572872 | tf_op jit(solution)/shard_map/ppermute | solution.py:43
  15.9 10.4 %collective-permute-start.6 = (bf16[256,1024]{1,0:T(8,128)(2,1)S(1)}, bf16[256,1024]{1,0:T(8,128)(2,1)S(1)}, u32[]{:S(2)}, u32[]{:S(2)}) collective-permute-start(bf16[256,1024]{1,0:T(8,128)(2,1)S(1)} %collective-permute-done.4), channel_id=1, source_target_pairs={{0,8},{4,28},{8,16},{12,4},{16,24},{20,12},{24,0},{28,20},{32,40},... | collective-permute-start | bytes 1572872 | tf_op jit(solution)/shard_map/ppermute | solution.py:43
  19.9 47.9 %collective-permute-start = (bf16[384,2048]{1,0:T(8,128)(2,1)S(1)}, bf16[384,2048]{1,0:T(8,128)(2,1)S(1)}, u32[]{:S(2)}, u32[]{:S(2)}) collective-permute-start(bf16[384,2048]{1,0:T(8,128)(2,1)S(1)} %get-tuple-element.28), channel_id=1, source_target_pairs={{0,1},{1,2},{2,3},{3,0},{4,7},{5,4},{6,5},{7,6},{8,9},{9,10},{10,1... | collective-permute-start | bytes 4718600 | tf_op jit(solution)/shard_map/ppermute | solution.py:43
  21.9 6.5 %copy-start.1 = (bf16[1024,2048]{1,0:T(8,128)(2,1)S(1)}, bf16[1024,2048]{1,0:T(8,128)(2,1)}, u32[]{:S(2)}) copy-start(bf16[1024,2048]{1,0:T(8,128)(2,1)} %left.1) | copy-start | bytes 12582916
  21.9 10.4 %collective-permute-start.12 = (bf16[256,1024]{1,0:T(8,128)(2,1)S(1)}, bf16[256,1024]{1,0:T(8,128)(2,1)S(1)}, u32[]{:S(2)}, u32[]{:S(2)}) collective-permute-start(bf16[256,1024]{1,0:T(8,128)(2,1)S(1)} %get-tuple-element.29), channel_id=1, source_target_pairs={{0,32},{4,100},{8,40},{12,108},{16,48},{20,116},{24,56},{28,124},{... | collective-permute-start | bytes 1572872 | tf_op jit(solution)/shard_map/ppermute | solution.py:43
  26.5 43.0 %copy-start = (bf16[1024,1024]{1,0:T(8,128)(2,1)}, bf16[1024,1024]{1,0:T(8,128)(2,1)S(1)}, u32[]{:S(2)}) copy-start(bf16[1024,1024]{1,0:T(8,128)(2,1)S(1)} %pad_maximum_fusion.refs_4_.refs_0_) | copy-start | bytes 6291460
  26.5 61.1 %collective-permute-start.8 = (bf16[1024,1024]{1,0:T(8,128)(2,1)S(1)}, bf16[1024,1024]{1,0:T(8,128)(2,1)S(1)}, u32[]{:S(2)}, u32[]{:S(2)}) collective-permute-start(bf16[1024,1024]{1,0:T(8,128)(2,1)S(1)} %pad_maximum_fusion.refs_4_.refs_0_), channel_id=1, source_target_pairs={{0,32},{4,100},{8,40},{12,108},{16,48},{20,116},{24,56},{28,124},{... | collective-permute-start | bytes 6291464 | tf_op jit(solution)/shard_map/ppermute | solution.py:43
  28.4 25.2 %collective-permute-start.2 = (bf16[256,2048]{1,0:T(8,128)(2,1)S(1)}, bf16[256,2048]{1,0:T(8,128)(2,1)S(1)}, u32[]{:S(2)}, u32[]{:S(2)}) collective-permute-start(bf16[256,2048]{1,0:T(8,128)(2,1)S(1)} %slice.17), channel_id=1, source_target_pairs={{0,1},{1,2},{2,3},{3,0},{4,7},{5,4},{6,5},{7,6},{8,9},{9,10},{10,1... | collective-permute-start | bytes 3145736 | tf_op jit(solution)/shard_map/ppermute | solution.py:43
  30.4 14.8 %collective-permute-start.13 = (bf16[256,1024]{1,0:T(8,128)(2,1)S(1)}, bf16[256,1024]{1,0:T(8,128)(2,1)S(1)}, u32[]{:S(2)}, u32[]{:S(2)}) collective-permute-start(bf16[256,1024]{1,0:T(8,128)(2,1)S(1)} %get-tuple-element.29), channel_id=1, source_target_pairs={{0,96},{4,36},{8,104},{12,44},{16,112},{20,52},{24,120},{28,60},{3... | collective-permute-start | bytes 1572872 | tf_op jit(solution)/shard_map/ppermute | solution.py:43
  32.3 52.1 %collective-permute-start.1 = (bf16[384,2048]{1,0:T(8,128)(2,1)S(1)}, bf16[384,2048]{1,0:T(8,128)(2,1)S(1)}, u32[]{:S(2)}, u32[]{:S(2)}) collective-permute-start(bf16[384,2048]{1,0:T(8,128)(2,1)S(1)} %get-tuple-element.27), channel_id=1, source_target_pairs={{0,1},{1,2},{2,3},{3,0},{4,7},{5,4},{6,5},{7,6},{8,9},{9,10},{10,1... | collective-permute-start | bytes 4718600 | tf_op jit(solution)/shard_map/ppermute | solution.py:43
  45.2 20.7 %collective-permute-start.14 = (bf16[256,1024]{1,0:T(8,128)(2,1)S(1)}, bf16[256,1024]{1,0:T(8,128)(2,1)S(1)}, u32[]{:S(2)}, u32[]{:S(2)}) collective-permute-start(bf16[256,1024]{1,0:T(8,128)(2,1)S(1)} %collective-permute-done.12), channel_id=1, source_target_pairs={{0,32},{4,100},{8,40},{12,108},{16,48},{20,116},{24,56},{28,124},{... | collective-permute-start | bytes 1572872 | tf_op jit(solution)/shard_map/ppermute | solution.py:43
  53.6 105.6 %copy-start.12 = (bf16[256,2048]{1,0:T(8,128)(2,1)}, bf16[256,2048]{1,0:T(8,128)(2,1)S(1)}, u32[]{:S(2)}) copy-start(bf16[256,2048]{1,0:T(8,128)(2,1)S(1)} %collective-permute-done.2.refs_2_) | copy-start | bytes 3145732
  53.6 78.4 %collective-permute-start.3 = (bf16[1024,2048]{1,0:T(8,128)(2,1)S(1)}, bf16[1024,2048]{1,0:T(8,128)(2,1)S(1)}, u32[]{:S(2)}, u32[]{:S(2)}) collective-permute-start(bf16[1024,2048]{1,0:T(8,128)(2,1)S(1)} %copy-done.1), channel_id=1, source_target_pairs={{0,3},{1,0},{2,1},{3,2},{4,5},{5,6},{6,7},{7,4},{8,11},{9,8},{10,9... | collective-permute-start | bytes 12582920 | tf_op jit(solution)/shard_map/ppermute | solution.py:43
  66.0 26.0 %collective-permute-start.10 = (bf16[1024,1024]{1,0:T(8,128)(2,1)S(1)}, bf16[1024,1024]{1,0:T(8,128)(2,1)S(1)}, u32[]{:S(2)}, u32[]{:S(2)}) collective-permute-start(bf16[1024,1024]{1,0:T(8,128)(2,1)S(1)} %pad_maximum_fusion.refs_4_.refs_0_), channel_id=1, source_target_pairs={{0,96},{4,36},{8,104},{12,44},{16,112},{20,52},{24,120},{28,60},{3... | collective-permute-start | bytes 6291464 | tf_op jit(solution)/shard_map/ppermute | solution.py:43
  67.8 91.4 %copy-start.8 = (bf16[384,2048]{1,0:T(8,128)(2,1)}, bf16[384,2048]{1,0:T(8,128)(2,1)S(1)}, u32[]{:S(2)}) copy-start(bf16[384,2048]{1,0:T(8,128)(2,1)S(1)} %collective-permute-done.refs_0_) | copy-start | bytes 4718596
  67.8 25.4 %collective-permute-start.7 = (bf16[1024,1024]{1,0:T(8,128)(2,1)S(1)}, bf16[1024,1024]{1,0:T(8,128)(2,1)S(1)}, u32[]{:S(2)}, u32[]{:S(2)}) collective-permute-start(bf16[1024,1024]{1,0:T(8,128)(2,1)S(1)} %pad_maximum_fusion.refs_4_.refs_0_), channel_id=1, source_target_pairs={{0,4},{4,0},{8,12},{12,8},{16,20},{20,16},{24,28},{28,24},{32,36},... | collective-permute-start | bytes 6291464 | tf_op jit(solution)/shard_map/ppermute | solution.py:43
  84.4 74.8 %copy-start.10 = (bf16[384,2048]{1,0:T(8,128)(2,1)}, bf16[384,2048]{1,0:T(8,128)(2,1)S(1)}, u32[]{:S(2)}) copy-start(bf16[384,2048]{1,0:T(8,128)(2,1)S(1)} %collective-permute-done.1.refs_1_) | copy-start | bytes 4718596
  84.4 45.6 %collective-permute-start.16 = (bf16[1024,1024]{1,0:T(8,128)(2,1)}, bf16[1024,1024]{1,0:T(8,128)(2,1)}, u32[]{:S(2)}, u32[]{:S(2)}) collective-permute-start(bf16[1024,1024]{1,0:T(8,128)(2,1)} %pad_maximum_fusion.1.refs_0_.refs_8_), channel_id=1, source_target_pairs={{0,8},{4,28},{8,16},{12,4},{16,24},{20,12},{24,0},{28,20},{32,40},... | collective-permute-start | bytes 6291464 | tf_op jit(solution)/shard_map/ppermute | solution.py:43
  87.6 44.5 %copy-start.2 = (bf16[1024,1024]{1,0:T(8,128)(2,1)}, bf16[1024,1024]{1,0:T(8,128)(2,1)S(1)}, u32[]{:S(2)}) copy-start(bf16[1024,1024]{1,0:T(8,128)(2,1)S(1)} %collective-permute-done.8.refs_6_.refs_2_) | copy-start | bytes 6291460
  87.6 44.0 %collective-permute-start.18 = (bf16[1024,1024]{1,0:T(8,128)(2,1)}, bf16[1024,1024]{1,0:T(8,128)(2,1)}, u32[]{:S(2)}, u32[]{:S(2)}) collective-permute-start(bf16[1024,1024]{1,0:T(8,128)(2,1)} %pad_maximum_fusion.1.refs_0_.refs_8_), channel_id=1, source_target_pairs={{0,24},{4,12},{8,0},{12,20},{16,8},{20,28},{24,16},{28,4},{32,56},... | collective-permute-start | bytes 6291464 | tf_op jit(solution)/shard_map/ppermute | solution.py:43
  92.0 65.4 %copy-start.3 = (bf16[1024,1024]{1,0:T(8,128)(2,1)}, bf16[1024,1024]{1,0:T(8,128)(2,1)S(1)}, u32[]{:S(2)}) copy-start(bf16[1024,1024]{1,0:T(8,128)(2,1)S(1)} %collective-permute-done.10.refs_8_.refs_4_) | copy-start | bytes 6291460
  92.0 40.1 %collective-permute-start.9 = (bf16[1024,1024]{1,0:T(8,128)(2,1)S(1)}, bf16[1024,1024]{1,0:T(8,128)(2,1)S(1)}, u32[]{:S(2)}, u32[]{:S(2)}) collective-permute-start(bf16[1024,1024]{1,0:T(8,128)(2,1)S(1)} %collective-permute-done.8.refs_6_.refs_2_), channel_id=1, source_target_pairs={{0,4},{4,0},{8,12},{12,8},{16,20},{20,16},{24,28},{28,24},{32,36},... | collective-permute-start | bytes 6291464 | tf_op jit(solution)/shard_map/ppermute | solution.py:43
  93.2 64.2 %copy-start.4 = (bf16[1024,1024]{1,0:T(8,128)(2,1)}, bf16[1024,1024]{1,0:T(8,128)(2,1)S(1)}, u32[]{:S(2)}) copy-start(bf16[1024,1024]{1,0:T(8,128)(2,1)S(1)} %collective-permute-done.7.refs_5_.refs_1_) | copy-start | bytes 6291460
  93.2 39.4 %collective-permute-start.11 = (bf16[1024,1024]{1,0:T(8,128)(2,1)S(1)}, bf16[1024,1024]{1,0:T(8,128)(2,1)S(1)}, u32[]{:S(2)}, u32[]{:S(2)}) collective-permute-start(bf16[1024,1024]{1,0:T(8,128)(2,1)S(1)} %collective-permute-done.10.refs_8_.refs_4_), channel_id=1, source_target_pairs={{0,4},{4,0},{8,12},{12,8},{16,20},{20,16},{24,28},{28,24},{32,36},... | collective-permute-start | bytes 6291464 | tf_op jit(solution)/shard_map/ppermute | solution.py:43
  130.0 27.4 %collective-permute-start.20 = (bf16[1024,1024]{1,0:T(8,128)(2,1)S(1)}, bf16[1024,1024]{1,0:T(8,128)(2,1)}, u32[]{:S(2)}, u32[]{:S(2)}) collective-permute-start(bf16[1024,1024]{1,0:T(8,128)(2,1)S(1)} %collective-permute-done.8.refs_6_.refs_2_), channel_id=1, source_target_pairs={{0,32},{4,100},{8,40},{12,108},{16,48},{20,116},{24,56},{28,124},{... | collective-permute-start | bytes 6291464 | tf_op jit(solution)/shard_map/ppermute | solution.py:43
  131.6 27.6 %collective-permute-start.22 = (bf16[1024,1024]{1,0:T(8,128)(2,1)}, bf16[1024,1024]{1,0:T(8,128)(2,1)}, u32[]{:S(2)}, u32[]{:S(2)}) collective-permute-start(bf16[1024,1024]{1,0:T(8,128)(2,1)} %collective-permute-done.16.refs_2_.refs_10_), channel_id=1, source_target_pairs={{0,8},{4,28},{8,16},{12,4},{16,24},{20,12},{24,0},{28,20},{32,40},... | collective-permute-start | bytes 6291464 | tf_op jit(solution)/shard_map/ppermute | solution.py:43
  132.1 27.1 %copy-start.7 = (bf16[1024,2048]{1,0:T(8,128)(2,1)}, bf16[1024,2048]{1,0:T(8,128)(2,1)S(1)}, u32[]{:S(2)}) copy-start(bf16[1024,2048]{1,0:T(8,128)(2,1)S(1)} %collective-permute-done.3.refs_3_) | copy-start | bytes 12582916
  132.1 42.8 %collective-permute-start.15 = (bf16[1024,1024]{1,0:T(8,128)(2,1)}, bf16[1024,1024]{1,0:T(8,128)(2,1)}, u32[]{:S(2)}, u32[]{:S(2)}) collective-permute-start(bf16[1024,1024]{1,0:T(8,128)(2,1)} %pad_maximum_fusion.1.refs_0_.refs_8_), channel_id=1, source_target_pairs={{0,4},{4,0},{8,12},{12,8},{16,20},{20,16},{24,28},{28,24},{32,36},... | collective-permute-start | bytes 6291464 | tf_op jit(solution)/shard_map/ppermute | solution.py:43
  132.2 27.0 %copy-start.5 = (bf16[1024,1024]{1,0:T(8,128)(2,1)}, bf16[1024,1024]{1,0:T(8,128)(2,1)S(1)}, u32[]{:S(2)}) copy-start(bf16[1024,1024]{1,0:T(8,128)(2,1)S(1)} %collective-permute-done.9.refs_7_.refs_3_) | copy-start | bytes 6291460
  132.2 44.9 %collective-permute-start.17 = (bf16[1024,1024]{1,0:T(8,128)(2,1)}, bf16[1024,1024]{1,0:T(8,128)(2,1)}, u32[]{:S(2)}, u32[]{:S(2)}) collective-permute-start(bf16[1024,1024]{1,0:T(8,128)(2,1)} %collective-permute-done.16.refs_2_.refs_10_), channel_id=1, source_target_pairs={{0,4},{4,0},{8,12},{12,8},{16,20},{20,16},{24,28},{28,24},{32,36},... | collective-permute-start | bytes 6291464 | tf_op jit(solution)/shard_map/ppermute | solution.py:43
  132.7 26.7 %copy-start.6 = (bf16[1024,1024]{1,0:T(8,128)(2,1)}, bf16[1024,1024]{1,0:T(8,128)(2,1)S(1)}, u32[]{:S(2)}) copy-start(bf16[1024,1024]{1,0:T(8,128)(2,1)S(1)} %collective-permute-done.11.refs_9_.refs_5_) | copy-start | bytes 6291460
  132.7 45.7 %collective-permute-start.19 = (bf16[1024,1024]{1,0:T(8,128)(2,1)}, bf16[1024,1024]{1,0:T(8,128)(2,1)}, u32[]{:S(2)}, u32[]{:S(2)}) collective-permute-start(bf16[1024,1024]{1,0:T(8,128)(2,1)} %collective-permute-done.18.refs_4_.refs_12_), channel_id=1, source_target_pairs={{0,4},{4,0},{8,12},{12,8},{16,20},{20,16},{24,28},{28,24},{32,36},... | collective-permute-start | bytes 6291464 | tf_op jit(solution)/shard_map/ppermute | solution.py:43
  157.4 36.0 %collective-permute-start.21 = (bf16[1024,1024]{1,0:T(8,128)(2,1)}, bf16[1024,1024]{1,0:T(8,128)(2,1)}, u32[]{:S(2)}, u32[]{:S(2)}) collective-permute-start(bf16[1024,1024]{1,0:T(8,128)(2,1)} %collective-permute-done.20.refs_6_), channel_id=1, source_target_pairs={{0,4},{4,0},{8,12},{12,8},{16,20},{20,16},{24,28},{28,24},{32,36},... | collective-permute-start | bytes 6291464 | tf_op jit(solution)/shard_map/ppermute | solution.py:43
  159.2 34.2 %collective-permute-start.23 = (bf16[1024,1024]{1,0:T(8,128)(2,1)}, bf16[1024,1024]{1,0:T(8,128)(2,1)}, u32[]{:S(2)}, u32[]{:S(2)}) collective-permute-start(bf16[1024,1024]{1,0:T(8,128)(2,1)} %collective-permute-done.22.refs_14_), channel_id=1, source_target_pairs={{0,4},{4,0},{8,12},{12,8},{16,20},{20,16},{24,28},{28,24},{32,36},... | collective-permute-start | bytes 6291464 | tf_op jit(solution)/shard_map/ppermute | solution.py:43
  159.3 15.5 %copy-start.13 = (bf16[256,2048]{1,0:T(8,128)(2,1)S(1)}, bf16[256,2048]{1,0:T(8,128)(2,1)}, u32[]{:S(2)}) copy-start(bf16[256,2048]{1,0:T(8,128)(2,1)} %copy-done.12) | copy-start | bytes 3145732
  159.3 17.7 %copy-start.9 = (bf16[384,2048]{1,0:T(8,128)(2,1)S(1)}, bf16[384,2048]{1,0:T(8,128)(2,1)}, u32[]{:S(2)}) copy-start(bf16[384,2048]{1,0:T(8,128)(2,1)} %copy-done.8) | copy-start | bytes 4718596
  159.3 19.0 %copy-start.11 = (bf16[384,2048]{1,0:T(8,128)(2,1)S(1)}, bf16[384,2048]{1,0:T(8,128)(2,1)}, u32[]{:S(2)}) copy-start(bf16[384,2048]{1,0:T(8,128)(2,1)} %copy-done.10) | copy-start | bytes 4718596
  174.9 63.1 %collective-permute-start.26 = (bf16[256,2048]{1,0:T(8,128)(2,1)S(1)}, bf16[256,2048]{1,0:T(8,128)(2,1)S(1)}, u32[]{:S(2)}, u32[]{:S(2)}) collective-permute-start(bf16[256,2048]{1,0:T(8,128)(2,1)S(1)} %copy-done.13), channel_id=1, source_target_pairs={{0,1},{1,2},{2,3},{3,0},{4,7},{5,4},{6,5},{7,6},{8,9},{9,10},{10,1... | collective-permute-start | bytes 3145736 | tf_op jit(solution)/shard_map/ppermute | solution.py:43
  177.1 31.4 %collective-permute-start.24 = (bf16[384,2048]{1,0:T(8,128)(2,1)S(1)}, bf16[384,2048]{1,0:T(8,128)(2,1)S(1)}, u32[]{:S(2)}, u32[]{:S(2)}) collective-permute-start(bf16[384,2048]{1,0:T(8,128)(2,1)S(1)} %copy-done.9), channel_id=1, source_target_pairs={{0,1},{1,2},{2,3},{3,0},{4,7},{5,4},{6,5},{7,6},{8,9},{9,10},{10,1... | collective-permute-start | bytes 4718600 | tf_op jit(solution)/shard_map/ppermute | solution.py:43
  178.3 46.9 %collective-permute-start.25 = (bf16[384,2048]{1,0:T(8,128)(2,1)S(1)}, bf16[384,2048]{1,0:T(8,128)(2,1)S(1)}, u32[]{:S(2)}, u32[]{:S(2)}) collective-permute-start(bf16[384,2048]{1,0:T(8,128)(2,1)S(1)} %copy-done.11), channel_id=1, source_target_pairs={{0,1},{1,2},{2,3},{3,0},{4,7},{5,4},{6,5},{7,6},{8,9},{9,10},{10,1... | collective-permute-start | bytes 4718600 | tf_op jit(solution)/shard_map/ppermute | solution.py:43
  234.3 9.6 %collective-permute-start.30 = (f32[8,768]{1,0:T(8,128)S(1)}, f32[8,768]{1,0:T(8,128)S(1)}, u32[]{:S(2)}, u32[]{:S(2)}) collective-permute-start(f32[8,768]{1,0:T(8,128)S(1)} %get-tuple-element.26.refs_0_), channel_id=1, source_target_pairs={{0,1},{1,2},{2,3},{3,0},{4,7},{5,4},{6,5},{7,6},{8,9},{9,10},{10,1... | collective-permute-start | bytes 73736 | tf_op jit(solution)/shard_map/ppermute | solution.py:43
  234.6 11.1 %collective-permute-start.31 = (f32[8,768]{1,0:T(8,128)S(1)}, f32[8,768]{1,0:T(8,128)S(1)}, u32[]{:S(2)}, u32[]{:S(2)}) collective-permute-start(f32[8,768]{1,0:T(8,128)S(1)} %get-tuple-element.26.refs_0_), channel_id=1, source_target_pairs={{0,3},{1,0},{2,1},{3,2},{4,5},{5,6},{6,7},{7,4},{8,11},{9,8},{10,9... | collective-permute-start | bytes 73736 | tf_op jit(solution)/shard_map/ppermute | solution.py:43
  237.6 8.2 %collective-permute-start.32 = (f32[8,768]{1,0:T(8,128)S(1)}, f32[8,768]{1,0:T(8,128)S(1)}, u32[]{:S(2)}, u32[]{:S(2)}) collective-permute-start(f32[8,768]{1,0:T(8,128)S(1)} %get-tuple-element.26.refs_0_), channel_id=1, source_target_pairs={{0,2},{1,3},{2,0},{3,1},{4,6},{5,7},{6,4},{7,5},{8,10},{9,11},{10,... | collective-permute-start | bytes 73736 | tf_op jit(solution)/shard_map/ppermute | solution.py:53
  240.5 9.2 %collective-permute-start.27 = (f32[8,256]{1,0:T(8,128)S(1)}, f32[8,256]{1,0:T(8,128)S(1)}, u32[]{:S(2)}, u32[]{:S(2)}) collective-permute-start(f32[8,256]{1,0:T(8,128)S(1)} %get-tuple-element.25.refs_0_), channel_id=1, source_target_pairs={{0,1},{1,2},{2,3},{3,0},{4,7},{5,4},{6,5},{7,6},{8,9},{9,10},{10,1... | collective-permute-start | bytes 24584 | tf_op jit(solution)/shard_map/ppermute | solution.py:43
  241.9 7.9 %collective-permute-start.28 = (f32[8,256]{1,0:T(8,128)S(1)}, f32[8,256]{1,0:T(8,128)S(1)}, u32[]{:S(2)}, u32[]{:S(2)}) collective-permute-start(f32[8,256]{1,0:T(8,128)S(1)} %get-tuple-element.25.refs_0_), channel_id=1, source_target_pairs={{0,3},{1,0},{2,1},{3,2},{4,5},{5,6},{6,7},{7,4},{8,11},{9,8},{10,9... | collective-permute-start | bytes 24584 | tf_op jit(solution)/shard_map/ppermute | solution.py:43
  243.8 5.9 %collective-permute-start.29 = (f32[8,256]{1,0:T(8,128)S(1)}, f32[8,256]{1,0:T(8,128)S(1)}, u32[]{:S(2)}, u32[]{:S(2)}) collective-permute-start(f32[8,256]{1,0:T(8,128)S(1)} %get-tuple-element.25.refs_0_), channel_id=1, source_target_pairs={{0,2},{1,3},{2,0},{3,1},{4,6},{5,7},{6,4},{7,5},{8,10},{9,11},{10,... | collective-permute-start | bytes 24584 | tf_op jit(solution)/shard_map/ppermute | solution.py:53

commit v2 on v1

--- a/solution.py
+++ b/solution.py
@@ -11,7 +11,7 @@
 ROW_CHUNKS = (384, 384, 256)
 NX = NY = NZ = 4
 NC = 2
-MT, NT = 512, 512
+NT = 512
 
 NEAR_MIB, FAR_MIB = 11, 6
 
@@ -110,14 +110,13 @@
                 pltpu.make_async_copy(src, tile.at[pl.ds(to, step), :], sem).start()
 
 
-def copy_left(sources, b, place, seg, dst, sem):
-    for x in range(4):
-        col = pl.ds(pl.multiple_of(place(x), seg), seg)
-        low = 0
-        for chunk in sources[b]:
-            to = dst.at[pl.ds(low, chunk.shape[0]), col]
-            pltpu.make_async_copy(chunk.at[:, pl.ds(x * seg, seg)], to, sem).start()
-            low += chunk.shape[0]
+def copy_left(chunks, low, place, seg, dst, sem):
+    for chunk in chunks:
+        rows = pl.ds(low, chunk.shape[0])
+        for x in range(4):
+            col = pl.ds(pl.multiple_of(place(x), seg), seg)
+            pltpu.make_async_copy(chunk.at[:, pl.ds(x * seg, seg)], dst.at[rows, col], sem).start()
+        low += chunk.shape[0]
 
 
 def landed(ref, sem):
@@ -132,12 +131,13 @@
     return jnp.where(t == 3, jnp.where(p == 2, 11, p), 2 + 3 * p + t) * seg
 
 
-def multiply(a_v, tile, acc, col, spans, add):
-    rows, nt = a_v.shape[0], tile.shape[1]
-
-    @pl.loop(0, rows // MT)
+def multiply(a_v, tile, acc, col, spans, add, low=0, high=None):
+    rows, nt = (high or a_v.shape[0]) - low, tile.shape[1]
+    mt = max(m for m in (512, 384, 256) if rows % m == 0)
+
+    @pl.loop(0, rows // mt)
     def _(t):
-        at = pl.ds(pl.multiple_of(t * MT, MT), MT)
+        at = pl.ds(pl.multiple_of(low + t * mt, 128), mt)
         cols = pl.ds(col, nt)
         r = acc[at, cols] if add else None
         for a, b, size in spans:
@@ -146,61 +146,94 @@
         acc[at, cols] = r
 
 
-def left_kernel(pos, left, *refs):
-    count = len(ROW_CHUNKS)
-    sources, lines = ([left], refs[:count], refs[count:count + 1]), refs[count + 1:count + 7]
-    acc, a_v, t_v, a_sem, t_sem = refs[count + 7:]
+def left_tiles(pos, lines, blocks, nt, seg, t_v, t_sem):
     pieces = [[lines[2 * k:2 * k + 2] for k in range(3)]]
-    _, depth = left.shape
-    half, nt, seg, x0 = acc.shape[1] // 2, t_v.shape[2], depth // 4, pos[1]
+
+    def fetch(s, p):
+        copy_left_half(
+            pos, pieces, s * nt, blocks[p], range(3), lambda t: spot(p, t, seg), t_v.at[s % 2], t_sem.at[s % 2, p])
+
+    return fetch
+
+
+def left_kernel(low, pos, left, *refs):
+    (first, second, side), lines, (acc, a_v, t_v, a_sem, t_sem) = refs[:3], refs[3:9], refs[9:]
+    sources = [left.at[pl.ds(0, low), :]], [first, second], [side]
+    half, nt, seg = acc.shape[1] // 2, t_v.shape[2], a_v.shape[1] // 12
     blocks, where = plan(pos)
-
-    def fetch(s):
+    fetch = left_tiles(pos, lines, blocks, nt, seg, t_v, t_sem)
+    for p in range(2):
+        for b in range(3):
+            @pl.when(where[b] == p)
+            def _():
+                copy_left(sources[b], 0, lambda x: spot(p, turned(x, pos[1]), seg), seg, a_v, a_sem.at[p])
+        fetch(0, p)
+    for s in range(half // nt):
         for p in range(2):
-            copy_left_half(
-                pos, pieces, s * nt, blocks[p], range(3), lambda t: spot(p, t, seg), t_v.at[s % 2], t_sem.at[s % 2, p])
-
-    for b in range(3):
-        copy_left(sources, b, lambda x: spot(where[b], turned(x, x0), seg), seg, a_v, a_sem.at[where[b]])
-        if b == 0:
-            fetch(0)
-    for s in range(half // nt):
-        if (s + 1) * nt < half:
-            fetch(s + 1)
+            if (s + 1) * nt < half:
+                fetch(s + 1, p)
         for p in range(2):
             if s == 0:
-                landed(a_v.at[:, pl.ds(0, 4 * seg)], a_sem.at[p])
+                landed(a_v.at[pl.ds(0, low), pl.ds(0, 4 * seg)], a_sem.at[p])
             landed(t_v.at[s % 2, pl.ds(0, 4 * seg), :], t_sem.at[s % 2, p])
             if s == 0:
                 one, three = p * seg, (2 + 3 * p) * seg
-                multiply(a_v, t_v.at[0], acc, 0, ((one, one, seg), (three, three, 3 * seg)), p > 0)
+                multiply(a_v, t_v.at[0], acc, 0, ((one, one, seg), (three, three, 3 * seg)), p > 0, 0, low)
         if s > 0:
-            multiply(a_v, t_v.at[s % 2], acc, s * nt, ((0, 0, 8 * seg),), False)
-    landed(a_v.at[:, pl.ds(0, 4 * seg)], a_sem.at[2])
-
-
-def right_kernel(pos, a_v, before, *refs):
-    lines, (acc, _, t_v, t_sem) = refs[:6], refs[6:]
+            multiply(a_v, t_v.at[s % 2], acc, s * nt, ((0, 0, 8 * seg),), False, 0, low)
+
+
+def right_kernel(low, pos, a_in, before, left, *refs):
+    chunks, lines, (acc, a_v, t_v, a_sem, t_sem) = refs[:5], refs[5:11], refs[11:]
+    rows = left.shape[0]
+    upper = [left.at[pl.ds(0, low), :]], chunks[:2], chunks[3:4]
+    lower = [left.at[pl.ds(low, rows - low), :]], chunks[2:3], chunks[4:]
     pieces = [None, [lines[2 * k:2 * k + 2] for k in range(3)]]
     half, nt, seg = acc.shape[1] // 2, t_v.shape[2], a_v.shape[1] // 12
-    blocks, _ = plan(pos)
+    blocks, where = plan(pos)
 
     def fetch(s, p):
         copy_right_half(
             pos, pieces, s * nt, [blocks[p]], range(3), lambda _, t: (3 * p + t) * seg, t_v.at[s % 2], t_sem.at[s % 2, p])
 
-    for p in range(3):
+    fetch(0, 0)
+    for b in range(3):
+        copy_left(lower[b], low, lambda x: spot(where[b], turned(x, pos[1]), seg), seg, a_v, a_sem.at[0])
+    for p in range(1, 3):
         fetch(0, p)
+    for b in range(3):
+        @pl.when(where[b] == 2)
+        def _():
+            copy_left(upper[b], 0, lambda x: spot(2, turned(x, pos[1]), seg), seg, a_v, a_sem.at[1])
     for s in range(half // nt):
         for p in range(3):
             if (s + 1) * nt < half:
                 fetch(s + 1, p)
         for p in range(3):
+            if (s, p) == (0, 0):
+                landed(a_v.at[pl.ds(low, rows - low), :], a_sem.at[0])
+            if (s, p) == (0, 2):
+                landed(a_v.at[pl.ds(0, low), pl.ds(0, 4 * seg)], a_sem.at[1])
             landed(t_v.at[s % 2, pl.ds(0, 3 * seg), :], t_sem.at[s % 2, p])
             if s == 0:
                 multiply(a_v, t_v.at[0], acc, half, (((2 + 3 * p) * seg, 3 * p * seg, 3 * seg),), p > 0)
         if s > 0:
             multiply(a_v, t_v.at[s % 2], acc, half + s * nt, ((2 * seg, 0, 9 * seg),), False)
+
+
+def tail_kernel(low, pos, a_in, before, *refs):
+    lines, (acc, a_v, t_v, t_sem) = refs[:6], refs[6:]
+    half, nt, seg = acc.shape[1] // 2, t_v.shape[2], a_v.shape[1] // 12
+    blocks, _ = plan(pos)
+    fetch = left_tiles(pos, lines, blocks, nt, seg, t_v, t_sem)
+    for s in range(half // nt):
+        for p in range(2):
+            fetch(s, p)
+    for s in range(half // nt):
+        for p in range(2):
+            landed(t_v.at[s, pl.ds(0, 4 * seg), :], t_sem.at[s, p])
+            one, three = p * seg, (2 + 3 * p) * seg
+            multiply(a_v, t_v.at[s], acc, s * nt, ((one, one, seg), (three, three, 3 * seg)), p > 0, low)
 
 
 def rest_kernel(pos, a_v, before, *refs):
@@ -245,36 +278,33 @@
         p_v[at, :] = lanes if s == 0 else p_v[at, :] + lanes
 
 
-def spread(p_v, power):
-    for m in range(0, p_v.shape[0], 128):
-        power[:, m:m + 128] = jnp.sum(p_v[m:m + 128, :].T, axis=0, keepdims=True) + jnp.zeros((8, 128), jnp.float32)
-
-
 def far_kernel(low, before, t_in, *refs):
-    chunks, (acc, t_v, power, a_v, p_v, a_sem) = refs[:-6], refs[-6:]
+    acc, t_v, power, a_v, p_v, a_sem = refs[-6:]
+    chunks = refs[:-6] if low == 0 else refs[1:-6]
     at = 0
     for chunk in chunks:
         pltpu.make_async_copy(chunk, a_v.at[pl.ds(at, chunk.shape[0]), :], a_sem).start()
         at += chunk.shape[0]
+    if low > 0:
+        power[:, 0:low] = refs[0][...]
     landed(a_v, a_sem)
     for s in range(t_v.shape[0]):
         far_multiply(low, min(256, a_v.shape[0]), a_v, t_in.at[s], acc, p_v, s)
-    spread(p_v, power)
-
-
-def scale_kernel(low, cols, acc, *refs):
-    powers, (out, o_v, o_sem) = refs[:4], refs[-3:]
-    size = o_v.shape[1]
-    blocks = powers[0].shape[1] // size
+    for m in range(0, p_v.shape[0], 128):
+        power[:, low + m:low + m + 128] = (
+            jnp.sum(p_v[m:m + 128, :].T, axis=0, keepdims=True) + jnp.zeros((8, 128), jnp.float32))
+
+
+def scale_kernel(cols, acc, *refs):
+    powers, (out, o_v, o_sem) = refs[:4], refs[4:]
+    blocks, size, _ = o_v.shape
     for i in range(blocks):
-        if i >= 2:
-            landed(o_v.at[i % 2], o_sem.at[i % 2])
         lanes = pl.ds(i * size, size)
         total = (powers[0][0:1, lanes] + powers[1][0:1, lanes]) + (powers[2][0:1, lanes] + powers[3][0:1, lanes])
         factor = jnp.broadcast_to(lax.rsqrt(total / cols + 1e-06), (size, size)).T[:, 0:1]
-        o_v[i % 2] = acc[pl.ds(low + i * size, size), :] * factor
-        pltpu.make_async_copy(o_v.at[i % 2], out.at[pl.ds(low + i * size, size), :], o_sem.at[i % 2]).start()
-    for i in range(min(blocks, 2)):
+        o_v[i] = acc[pl.ds(i * size, size), :] * factor
+        pltpu.make_async_copy(o_v.at[i], out.at[pl.ds(i * size, size), :], o_sem.at[i]).start()
+    for i in range(blocks):
         landed(o_v.at[i], o_sem.at[i])
 
 
@@ -308,18 +338,24 @@
 
 def near(pos, left, behind, ahead, pieces):
     rows, depth = left.shape
-    half, seg = pieces[0].shape[1], depth // 4
-    total = pltpu.VMEM((rows, 2 * half), jnp.float32)
+    half, seg, low = pieces[0].shape[1], depth // 4, ahead[0].shape[0]
+    total, gathered = pltpu.VMEM((rows, 2 * half), jnp.float32), pltpu.VMEM((rows, 12 * seg), left.dtype)
+    both = total, gathered
     flops = 2 * rows * half * seg
     dma = pltpu.SemaphoreType.DMA
+    tile = pltpu.VMEM((2, 8 * seg, NT), left.dtype)
     acc, blocks = call(
-        left_kernel, (total, pltpu.VMEM((rows, 12 * seg), left.dtype)), [SMEM] + [ANY] * (8 + len(ROW_CHUNKS)), (VMEM, VMEM),
-        [pltpu.VMEM((2, 8 * seg, NT), left.dtype), dma((3,)), dma((2, 2))], 8 * flops, NEAR_MIB,
-    )(pos, left, *behind, ahead, *pieces[:6])
+        functools.partial(left_kernel, low), both, [SMEM] + [ANY] * 10, (VMEM, VMEM),
+        [tile, dma((2,)), dma((2, 2))], 6 * flops, NEAR_MIB,
+    )(pos, left, *behind[:2], ahead[0], *pieces[:6])
     acc, blocks = call(
-        right_kernel, (total, pltpu.VMEM(blocks.shape, blocks.dtype)), [SMEM, VMEM, VMEM] + [ANY] * 6, (VMEM, VMEM),
-        [pltpu.VMEM((2, 9 * seg, NT), left.dtype), dma((2, 3))], 9 * flops, NEAR_MIB, {1: 1, 2: 0},
-    )(pos, kept(blocks), kept(acc), *pieces[8:14])
+        functools.partial(right_kernel, low), both, [SMEM, VMEM, VMEM] + [ANY] * 12, (VMEM, VMEM),
+        [pltpu.VMEM((2, 9 * seg, NT), left.dtype), dma((2,)), dma((2, 3))], 9 * flops, NEAR_MIB, {1: 1, 2: 0},
+    )(pos, kept(blocks), kept(acc), left, *behind, *ahead, *pieces[8:14])
+    acc, blocks = call(
+        functools.partial(tail_kernel, low), both, [SMEM, VMEM, VMEM] + [ANY] * 6, (VMEM, VMEM),
+        [tile, dma((2, 2))], 2 * flops, NEAR_MIB, {1: 1, 2: 0},
+    )(pos, kept(blocks), kept(acc), *pieces[:6])
     parts = 2 * half // NT
     return call(
         rest_kernel, (total, pltpu.VMEM((parts, depth, NT), left.dtype)), [SMEM, VMEM, VMEM] + [ANY] * 16, (VMEM, VMEM),
@@ -327,35 +363,35 @@
     )(pos, kept(blocks), kept(acc), *pieces)
 
 
-def far(low, acc, tile, chunks):
+def far(acc, tile, chunks, powers):
     depth = chunks[0].shape[1]
     rows = sum(chunk.shape[0] for chunk in chunks)
-    out = pltpu.VMEM(acc.shape, acc.dtype), pltpu.VMEM(tile.shape, tile.dtype), jax.ShapeDtypeStruct((8, rows), jnp.float32)
+    low = powers[0].shape[1] if powers else 0
+    out = pltpu.VMEM(acc.shape, acc.dtype), pltpu.VMEM(tile.shape, tile.dtype), jax.ShapeDtypeStruct((8, low + rows), jnp.float32)
     return call(
-        functools.partial(far_kernel, low), out, [VMEM, VMEM] + [ANY] * len(chunks), (VMEM, VMEM, VMEM),
+        functools.partial(far_kernel, low), out, [VMEM, VMEM] + [VMEM] * len(powers) + [ANY] * len(chunks), (VMEM, VMEM, VMEM),
         [pltpu.VMEM((rows, depth), chunks[0].dtype), pltpu.VMEM((rows, 128), jnp.float32), pltpu.SemaphoreType.DMA],
         2 * rows * depth * acc.shape[1], FAR_MIB, {0: 0, 1: 1},
-    )(kept(acc), kept(tile), *chunks)
-
-
-def scale(low, cols, acc, powers, base):
-    extra = [] if base is None else [base]
+    )(kept(acc), kept(tile), *powers, *chunks)
+
+
+def scale(cols, acc, powers):
+    rows, width = acc.shape
     return call(
-        functools.partial(scale_kernel, low, cols), jax.ShapeDtypeStruct(acc.shape, jnp.float32),
-        [VMEM] * 5 + [ANY] * len(extra), ANY,
-        [pltpu.VMEM((2, 128, acc.shape[1]), jnp.float32), pltpu.SemaphoreType.DMA((2,))],
-        powers[0].shape[1] * acc.shape[1] * 30, FAR_MIB, {5: 0} if extra else {},
-    )(kept(acc), *powers, *extra)
+        functools.partial(scale_kernel, cols), jax.ShapeDtypeStruct(acc.shape, jnp.float32), [VMEM] * 5, ANY,
+        [pltpu.VMEM((rows // 128, 128, width), jnp.float32), pltpu.SemaphoreType.DMA((rows // 128,))],
+        rows * width * 30, 12,
+    )(kept(acc), *powers)
 
 
 def per_device(left, right):
-    rows, _ = left.shape
     width = right.shape[1]
     half = width // 2
     me, z = lax.axis_index("gy"), lax.axis_index("gx")
     pos = jnp.stack([me // (NX * NC), (me // NC) % NX, me % NC, z]).astype(jnp.int32)
 
-    ahead = move(left, "z", False)
+    most = sum(ROW_CHUNKS[:-1])
+    ahead = [move(left[:most], "z", False), move(left[most:], "z", False)]
     behind, opposite, low = [], [], 0
     for i, size in enumerate(ROW_CHUNKS):
         behind.append(move(left[low:low + size], "z", True))
@@ -368,13 +404,10 @@
             pieces += [v, move(v, "core", True)]
 
     pieces = [apart(v) for v in pieces]
-    acc, tile = near(pos, apart(left), [apart(v) for v in behind], apart(ahead), pieces)
-    low = rows - ROW_CHUNKS[-1]
-    acc, tile, power = far(0, acc, tile, opposite[:-1])
-    first = exchange(power)
-    acc, tile, power = far(low, acc, tile, opposite[-1:])
-    second = exchange(power)
-    return scale(low, width * NZ, acc, second, scale(0, width * NZ, acc, first, None))
+    acc, tile = near(pos, apart(left), [apart(v) for v in behind], [apart(v) for v in ahead], pieces)
+    acc, tile, power = far(acc, tile, opposite[:-1], [])
+    acc, tile, power = far(acc, tile, opposite[-1:], [power])
+    return scale(width * NZ, acc, exchange(power))
 
 
 def solution(mesh):

time: 253 us -> 258 us (1.020)
  waiting for transfers between devices: 143 us -> 158 us
  starting transfers between devices: 44.6 us -> 35.6 us
    ppermute x31 -> x30, waiting for transfers between devices: 143 us -> 155 us  [move(): return lax.ppermute(value, name, along(axis, first))]
    ppermute x31 -> x30, starting transfers between devices: 42.3 us -> 35.3 us  [move(): return lax.ppermute(value, name, along(axis, first))]
    ppermute x2 -> x1, waiting for transfers between devices: 0.01 us -> 3.53 us  [exchange(): opposite = lax.ppermute(power, 'gx', [(i, (i + 2) % NZ) for i in range(NZ)])]
  transfers between devices with their start and end apart: 33 -> 31, of which waited for: 13 -> 13; matrix products, arithmetic and copies ran while one was open for 2% -> 2% of each run, Pallas kernels for 22% -> 20%
where the time goes in v2:
time: 258 us
  waiting for transfers between devices  158 us (61%)
  Pallas kernels  58.2 us (23%)
  starting transfers between devices  35.6 us (14%)
  local copies, waits for them, and re-layouts  3.45 us (1%)
    ppermute x30, waiting for transfers between devices, move(): return lax.ppermute(value, name, along(axis, first))  155 us
    ppermute x30, starting transfers between devices, move(): return lax.ppermute(value, name, along(axis, first))  35.3 us
    pallas_call x1, Pallas kernels, near(): call(functools.partial(right_kernel, low), both, [SMEM, VMEM, VMEM] + [AN...  14.6 us
    pallas_call x1, Pallas kernels, near(): call(functools.partial(left_kernel, low), both, [SMEM] + [ANY] * 10, (VME...  11.9 us
    pallas_call x1, Pallas kernels, near(): call(rest_kernel, (total, pltpu.VMEM((parts, depth, NT), left.dtype)), [S...  11.7 us
    pallas_call x2, Pallas kernels, far(): call(functools.partial(far_kernel, low), out, [VMEM, VMEM] + [VMEM] * len...  11.5 us
  transfers between devices with their start and end apart: 31, of which 13 were waited for; matrix products, arithmetic and copies ran while one was open for 2% of the time, Pallas kernels for 20%

profile of v2, /device:TPU:0, one launch (start us, length us, event | category | flops | bytes accessed | tf_op | source)
XLA Modules:
  0.0 258.1 jit_solution(6519454371810376161)
XLA Ops:
  0.0 1.3 fusion.1
  1.3 1.7 collective-permute-start.3
  2.9 1.6 collective-permute-start.4
  4.6 1.7 collective-permute-start.13
  6.3 9.6 %collective-permute-done.3 = bf16[256,1024]{1,0:T(8,128)(2,1)S(1)} collective-permute-done((bf16[256,1024]{1,0:T(8,128)(2,1)S(1)}, bf16[256,1024]{1,0:T(8,128)(2,1)S(1)}, u32[]{:S(2)}, u32[]{:S(2)}) %collective-permute-start.3) | collective-permute-done | bytes 524320 | tf_op jit(solution)/shard_map/ppermute | solution.py:43
  15.9 1.7 collective-permute-start.5
  17.6 3.0 %collective-permute-start.14 = (bf16[256,1024]{1,0:T(8,128)(2,1)S(1)}, bf16[256,1024]{1,0:T(8,128)(2,1)S(1)}, u32[]{:S(2)}, u32[]{:S(2)}) collective-permute-start(bf16[256,1024]{1,0:T(8,128)(2,1)S(1)} %get-tuple-element.33), channel_id=1, source_target_pairs={{0,96},{4,36},{8,104},{12,44},{16,112},{20,52},{24,120},{28,60},{3... | collective-permute-start | bytes 1572872 | tf_op jit(solution)/shard_map/ppermute | solution.py:43
  20.6 1.3 slice.23
  22.0 2.0 collective-permute-start.11
  24.0 2.2 collective-permute-start.12
  26.2 0.1 collective-permute-done.5
  26.3 0.2 pad_maximum_fusion.refs_3_.refs_0_
  26.5 1.9 collective-permute-start.7
  28.3 0.4 fusion
  28.8 0.2 collective-permute-done.14
  29.0 4.0 %collective-permute-start = (bf16[384,2048]{1,0:T(8,128)(2,1)S(1)}, bf16[384,2048]{1,0:T(8,128)(2,1)S(1)}, u32[]{:S(2)}, u32[]{:S(2)}) collective-permute-start(bf16[384,2048]{1,0:T(8,128)(2,1)S(1)} %get-tuple-element.32), channel_id=1, source_target_pairs={{0,1},{1,2},{2,3},{3,0},{4,7},{5,4},{6,5},{7,6},{8,9},{9,10},{10,1... | collective-permute-start | bytes 4718600 | tf_op jit(solution)/shard_map/ppermute | solution.py:43
  33.0 3.6 %collective-permute-done.15 = bf16[256,1024]{1,0:T(8,128)(2,1)S(1)} collective-permute-done((bf16[256,1024]{1,0:T(8,128)(2,1)S(1)}, bf16[256,1024]{1,0:T(8,128)(2,1)S(1)}, u32[]{:S(2)}, u32[]{:S(2)}) %collective-permute-start.15) | collective-permute-done | bytes 524320 | tf_op jit(solution)/shard_map/ppermute | solution.py:43
  36.6 13.5 %collective-permute-done.11.refs_2_ = bf16[256,2048]{1,0:T(8,128)(2,1)S(1)} collective-permute-done((bf16[256,2048]{1,0:T(8,128)(2,1)S(1)}, bf16[256,2048]{1,0:T(8,128)(2,1)S(1)}, u32[]{:S(2)}, u32[]{:S(2)}) %collective-permute-start.11) | collective-permute-done | bytes 1048608 | tf_op jit(solution)/shard_map/ppermute | solution.py:43
  50.2 0.4 slice.21
  50.6 16.3 %collective-permute-done.refs_0_ = bf16[384,2048]{1,0:T(8,128)(2,1)S(1)} collective-permute-done((bf16[384,2048]{1,0:T(8,128)(2,1)S(1)}, bf16[384,2048]{1,0:T(8,128)(2,1)S(1)}, u32[]{:S(2)}, u32[]{:S(2)}) %collective-permute-start) | collective-permute-done | bytes 1572896 | tf_op jit(solution)/shard_map/ppermute | solution.py:43
  66.9 1.7 pad_maximum_fusion.1.refs_5_.refs_8_
  68.6 30.8 %collective-permute-done.1.refs_1_ = bf16[384,2048]{1,0:T(8,128)(2,1)S(1)} collective-permute-done((bf16[384,2048]{1,0:T(8,128)(2,1)S(1)}, bf16[384,2048]{1,0:T(8,128)(2,1)S(1)}, u32[]{:S(2)}, u32[]{:S(2)}) %collective-permute-start.1) | collective-permute-done | bytes 1572896 | tf_op jit(solution)/shard_map/ppermute | solution.py:43
  99.4 3.2 %collective-permute-start.19 = (bf16[1024,1024]{1,0:T(8,128)(2,1)}, bf16[1024,1024]{1,0:T(8,128)(2,1)}, u32[]{:S(2)}, u32[]{:S(2)}) collective-permute-start(bf16[1024,1024]{1,0:T(8,128)(2,1)} %pad_maximum_fusion.1.refs_5_.refs_8_), channel_id=1, source_target_pairs={{0,24},{4,12},{8,0},{12,20},{16,8},{20,28},{24,16},{28,4},{32,56},... | collective-permute-start | bytes 6291464 | tf_op jit(solution)/shard_map/ppermute | solution.py:43
  102.6 0.1 collective-permute-start.8
  102.7 0.5 collective-permute-start.10
  103.2 38.7 %collective-permute-done.17.refs_7_.refs_10_ = bf16[1024,1024]{1,0:T(8,128)(2,1)} collective-permute-done((bf16[1024,1024]{1,0:T(8,128)(2,1)}, bf16[1024,1024]{1,0:T(8,128)(2,1)}, u32[]{:S(2)}, u32[]{:S(2)}) %collective-permute-start.17) | collective-permute-done | bytes 2097184 | tf_op jit(solution)/shard_map/ppermute | solution.py:43
  141.9 2.4 collective-permute-start.21
  144.3 0.5 collective-permute-start.23
  144.8 0.5 collective-permute-start.18
  145.3 0.1 collective-permute-start.20
  145.4 23.9 %collective-permute-done.21.refs_6_ = bf16[1024,1024]{1,0:T(8,128)(2,1)} collective-permute-done((bf16[1024,1024]{1,0:T(8,128)(2,1)S(1)}, bf16[1024,1024]{1,0:T(8,128)(2,1)}, u32[]{:S(2)}, u32[]{:S(2)}) %collective-permute-start.21) | collective-permute-done | bytes 2097184 | tf_op jit(solution)/shard_map/ppermute | solution.py:43
  169.3 2.6 %collective-permute-done.23.refs_14_ = bf16[1024,1024]{1,0:T(8,128)(2,1)} collective-permute-done((bf16[1024,1024]{1,0:T(8,128)(2,1)}, bf16[1024,1024]{1,0:T(8,128)(2,1)}, u32[]{:S(2)}, u32[]{:S(2)}) %collective-permute-start.23) | collective-permute-done | bytes 2097184 | tf_op jit(solution)/shard_map/ppermute | solution.py:43
  172.0 0.1 pad_add_fusion.pos
  172.0 11.9 %shard_map.28 = (f32[1024,2048]{1,0:T(8,128)S(1)}, bf16[1024,6144]{1,0:T(8,128)(2,1)S(1)}) custom-call(s32[4]{0:T(128)S(1)} %pad_add_fusion.pos, bf16[1024,2048]{1,0:T(8,128)(2,1)} %left.3, bf16[384,2048]{1,0:T(8,128)(2,1)} %copy-done.8, bf16[384,2048]{1,0:T(8,128)(2,1)} %copy-done.10, bf16[768,2048]{1,0:T(8,128)(2,1)} %copy-done.7, ...), custom_call_target="tpu_custom_call" | custom-call | flops 6442450944 | bytes 16777216 | tf_op jit(solution)/shard_map/pallas_call | solution.py:347
  184.0 0.1 collective-permute-start.27
  184.1 2.3 collective-permute-start.25
  186.4 2.5 collective-permute-start.26
  188.9 14.6 %shard_map.29 = (f32[1024,2048]{1,0:T(8,128)S(1)}, bf16[1024,6144]{1,0:T(8,128)(2,1)S(1)}) custom-call(s32[4]{0:T(128)S(1)} %pad_add_fusion.pos, bf16[1024,6144]{1,0:T(8,128)(2,1)S(1)} %get-tuple-element.18.a_in, f32[1024,2048]{1,0:T(8,128)S(1)} %get-tuple-element.19.before, bf16[1024,2048]{1,0:T(8,128)(2,1)} %left.3, ...), custom_call_target="tpu_custom_call", output_to_operand_aliasing={{1}: (1, {}), {0}: (2, {})} | custom-call | flops 9663676416 | bytes 16777216 | tf_op jit(solution)/shard_map/pallas_call | solution.py:351
  203.5 4.9 %shard_map.30 = (f32[1024,2048]{1,0:T(8,128)S(1)}, bf16[1024,6144]{1,0:T(8,128)(2,1)S(1)}) custom-call(s32[4]{0:T(128)S(1)} %pad_add_fusion.pos, bf16[1024,6144]{1,0:T(8,128)(2,1)S(1)} %get-tuple-element.20.a_in, f32[1024,2048]{1,0:T(8,128)S(1)} %get-tuple-element.21.before, ...), custom_call_target="tpu_custom_call", output_to_operand_aliasing={{1}: (1, {}), {0}: (2, {})} | custom-call | flops 2147483648 | bytes 16777216 | tf_op jit(solution)/shard_map/pallas_call | solution.py:355
  208.4 11.7 %shard_map.31 = (f32[1024,2048]{1,0:T(8,128)S(1)}, bf16[4,2048,512]{2,1,0:T(8,128)(2,1)S(1)}) custom-call(s32[4]{0:T(128)S(1)} %pad_add_fusion.pos, bf16[1024,6144]{1,0:T(8,128)(2,1)S(1)} %get-tuple-element.22.a_v, f32[1024,2048]{1,0:T(8,128)S(1)} %get-tuple-element.23.before, bf16[1024,1024]{1,0:T(8,128)(2,1)} %copy-done.1, ...), custom_call_target="tpu_custom_call", output_to_operand_aliasing={{0}: (2, {})} | custom-call | flops 7516192768 | bytes 16777216 | tf_op jit(solution)/shard_map/pallas_call | solution.py:360
  220.1 13.8 %collective-permute-done.26.refs_1_ = bf16[384,2048]{1,0:T(8,128)(2,1)S(1)} collective-permute-done((bf16[384,2048]{1,0:T(8,128)(2,1)S(1)}, bf16[384,2048]{1,0:T(8,128)(2,1)S(1)}, u32[]{:S(2)}, u32[]{:S(2)}) %collective-permute-start.26) | collective-permute-done | bytes 1572896 | tf_op jit(solution)/shard_map/ppermute | solution.py:43
  234.0 9.0 %shard_map.32 = (f32[1024,2048]{1,0:T(8,128)S(1)}, bf16[4,2048,512]{2,1,0:T(8,128)(2,1)S(1)}, f32[8,768]{1,0:T(8,128)S(1)}) custom-call(f32[1024,2048]{1,0:T(8,128)S(1)} %get-tuple-element.24.before, bf16[4,2048,512]{2,1,0:T(8,128)(2,1)S(1)} %get-tuple-element.25.t_in, ...), custom_call_target="tpu_custom_call", output_to_operand_aliasing={{0}: (0, {}), {1}: (1, {})} | custom-call | flops 6442450944 | bytes 16777216 | tf_op jit(solution)/shard_map/pallas_call | solution.py:371
  243.0 2.5 shard_map.33
  245.6 3.2 %collective-permute-start.29 = (f32[8,1024]{1,0:T(8,128)S(1)}, f32[8,1024]{1,0:T(8,128)S(1)}, u32[]{:S(2)}, u32[]{:S(2)}) collective-permute-start(f32[8,1024]{1,0:T(8,128)S(1)} %get-tuple-element.30.refs_0_), channel_id=1, source_target_pairs={{0,3},{1,0},{2,1},{3,2},{4,5},{5,6},{6,7},{7,4},{8,11},{9,8},{10,9... | collective-permute-start | bytes 98312 | tf_op jit(solution)/shard_map/ppermute | solution.py:43
  248.8 0.2 collective-permute-start.30
  249.1 1.6 collective-permute-done.28.refs_1_
  250.7 3.5 %collective-permute-done.30.refs_3_ = f32[8,1024]{1,0:T(8,128)S(1)} collective-permute-done((f32[8,1024]{1,0:T(8,128)S(1)}, f32[8,1024]{1,0:T(8,128)S(1)}, u32[]{:S(2)}, u32[]{:S(2)}) %collective-permute-start.30) | collective-permute-done | bytes 32800 | tf_op jit(solution)/shard_map/ppermute | solution.py:53
  254.2 3.7 %shard_map.34 = f32[1024,2048]{1,0:T(8,128)} custom-call(f32[1024,2048]{1,0:T(8,128)S(1)} %get-tuple-element.29.acc, f32[8,1024]{1,0:T(8,128)S(1)} %get-tuple-element.30.refs_0_, f32[8,1024]{1,0:T(8,128)S(1)} %collective-permute-done.28.refs_1_, f32[8,1024]{1,0:T(8,128)S(1)} %collective-permute-done.29.refs_2_, f32[8,1024]{1,0:T(8,128)S(1)} %collective-permute-done.30.refs_3_), custom_call_target="tpu_custom_call" | custom-call | flops 62914560 | bytes 16777216 | tf_op jit(solution)/shard_map/pallas_call | solution.py:380
  (54 shorter events, 0.3 us)
Async XLA Ops:
  1.3 14.6 %collective-permute-start.3 = (bf16[256,1024]{1,0:T(8,128)(2,1)S(1)}, bf16[256,1024]{1,0:T(8,128)(2,1)S(1)}, u32[]{:S(2)}, u32[]{:S(2)}) collective-permute-start(bf16[256,1024]{1,0:T(8,128)(2,1)S(1)} %get-tuple-element.34), channel_id=1, source_target_pairs={{0,8},{4,28},{8,16},{12,4},{16,24},{20,12},{24,0},{28,20},{32,40},... | collective-permute-start | bytes 1572872 | tf_op jit(solution)/shard_map/ppermute | solution.py:43
  2.9 21.0 %collective-permute-start.4 = (bf16[256,1024]{1,0:T(8,128)(2,1)S(1)}, bf16[256,1024]{1,0:T(8,128)(2,1)S(1)}, u32[]{:S(2)}, u32[]{:S(2)}) collective-permute-start(bf16[256,1024]{1,0:T(8,128)(2,1)S(1)} %get-tuple-element.34), channel_id=1, source_target_pairs={{0,24},{4,12},{8,0},{12,20},{16,8},{20,28},{24,16},{28,4},{32,56},... | collective-permute-start | bytes 1572872 | tf_op jit(solution)/shard_map/ppermute | solution.py:43
  4.6 21.6 %collective-permute-start.13 = (bf16[256,1024]{1,0:T(8,128)(2,1)S(1)}, bf16[256,1024]{1,0:T(8,128)(2,1)S(1)}, u32[]{:S(2)}, u32[]{:S(2)}) collective-permute-start(bf16[256,1024]{1,0:T(8,128)(2,1)S(1)} %get-tuple-element.33), channel_id=1, source_target_pairs={{0,32},{4,100},{8,40},{12,108},{16,48},{20,116},{24,56},{28,124},{... | collective-permute-start | bytes 1572872 | tf_op jit(solution)/shard_map/ppermute | solution.py:43
  15.9 10.4 %collective-permute-start.5 = (bf16[256,1024]{1,0:T(8,128)(2,1)S(1)}, bf16[256,1024]{1,0:T(8,128)(2,1)S(1)}, u32[]{:S(2)}, u32[]{:S(2)}) collective-permute-start(bf16[256,1024]{1,0:T(8,128)(2,1)S(1)} %collective-permute-done.3), channel_id=1, source_target_pairs={{0,8},{4,28},{8,16},{12,4},{16,24},{20,12},{24,0},{28,20},{32,40},... | collective-permute-start | bytes 1572872 | tf_op jit(solution)/shard_map/ppermute | solution.py:43
  17.6 11.3 %collective-permute-start.14 = (bf16[256,1024]{1,0:T(8,128)(2,1)S(1)}, bf16[256,1024]{1,0:T(8,128)(2,1)S(1)}, u32[]{:S(2)}, u32[]{:S(2)}) collective-permute-start(bf16[256,1024]{1,0:T(8,128)(2,1)S(1)} %get-tuple-element.33), channel_id=1, source_target_pairs={{0,96},{4,36},{8,104},{12,44},{16,112},{20,52},{24,120},{28,60},{3... | collective-permute-start | bytes 1572872 | tf_op jit(solution)/shard_map/ppermute | solution.py:43
  22.0 6.4 %copy-start = (bf16[1024,2048]{1,0:T(8,128)(2,1)S(1)}, bf16[1024,2048]{1,0:T(8,128)(2,1)}, u32[]{:S(2)}) copy-start(bf16[1024,2048]{1,0:T(8,128)(2,1)} %left.3) | copy-start | bytes 12582916
  22.0 28.1 %collective-permute-start.11 = (bf16[256,2048]{1,0:T(8,128)(2,1)S(1)}, bf16[256,2048]{1,0:T(8,128)(2,1)S(1)}, u32[]{:S(2)}, u32[]{:S(2)}) collective-permute-start(bf16[256,2048]{1,0:T(8,128)(2,1)S(1)} %slice.23), channel_id=1, source_target_pairs={{0,1},{1,2},{2,3},{3,0},{4,7},{5,4},{6,5},{7,6},{8,9},{9,10},{10,1... | collective-permute-start | bytes 3145736 | tf_op jit(solution)/shard_map/ppermute | solution.py:43
  24.0 26.1 %collective-permute-start.12 = (bf16[256,2048]{1,0:T(8,128)(2,1)S(1)}, bf16[256,2048]{1,0:T(8,128)(2,1)}, u32[]{:S(2)}, u32[]{:S(2)}) collective-permute-start(bf16[256,2048]{1,0:T(8,128)(2,1)S(1)} %slice.23), channel_id=1, source_target_pairs={{0,3},{1,0},{2,1},{3,2},{4,5},{5,6},{6,7},{7,4},{8,11},{9,8},{10,9... | collective-permute-start | bytes 3145736 | tf_op jit(solution)/shard_map/ppermute | solution.py:43
  26.2 10.4 %collective-permute-start.15 = (bf16[256,1024]{1,0:T(8,128)(2,1)S(1)}, bf16[256,1024]{1,0:T(8,128)(2,1)S(1)}, u32[]{:S(2)}, u32[]{:S(2)}) collective-permute-start(bf16[256,1024]{1,0:T(8,128)(2,1)S(1)} %collective-permute-done.13), channel_id=1, source_target_pairs={{0,32},{4,100},{8,40},{12,108},{16,48},{20,116},{24,56},{28,124},{... | collective-permute-start | bytes 1572872 | tf_op jit(solution)/shard_map/ppermute | solution.py:43
  26.5 23.6 %copy-start.1 = (bf16[1024,1024]{1,0:T(8,128)(2,1)}, bf16[1024,1024]{1,0:T(8,128)(2,1)S(1)}, u32[]{:S(2)}) copy-start(bf16[1024,1024]{1,0:T(8,128)(2,1)S(1)} %pad_maximum_fusion.refs_3_.refs_0_) | copy-start | bytes 6291460
  26.5 72.9 %collective-permute-start.7 = (bf16[1024,1024]{1,0:T(8,128)(2,1)S(1)}, bf16[1024,1024]{1,0:T(8,128)(2,1)S(1)}, u32[]{:S(2)}, u32[]{:S(2)}) collective-permute-start(bf16[1024,1024]{1,0:T(8,128)(2,1)S(1)} %pad_maximum_fusion.refs_3_.refs_0_), channel_id=1, source_target_pairs={{0,32},{4,100},{8,40},{12,108},{16,48},{20,116},{24,56},{28,124},{... | collective-permute-start | bytes 6291464 | tf_op jit(solution)/shard_map/ppermute | solution.py:43
  29.0 37.9 %collective-permute-start = (bf16[384,2048]{1,0:T(8,128)(2,1)S(1)}, bf16[384,2048]{1,0:T(8,128)(2,1)S(1)}, u32[]{:S(2)}, u32[]{:S(2)}) collective-permute-start(bf16[384,2048]{1,0:T(8,128)(2,1)S(1)} %get-tuple-element.32), channel_id=1, source_target_pairs={{0,1},{1,2},{2,3},{3,0},{4,7},{5,4},{6,5},{7,6},{8,9},{9,10},{10,1... | collective-permute-start | bytes 4718600 | tf_op jit(solution)/shard_map/ppermute | solution.py:43
  36.6 62.8 %collective-permute-start.1 = (bf16[384,2048]{1,0:T(8,128)(2,1)S(1)}, bf16[384,2048]{1,0:T(8,128)(2,1)S(1)}, u32[]{:S(2)}, u32[]{:S(2)}) collective-permute-start(bf16[384,2048]{1,0:T(8,128)(2,1)S(1)} %get-tuple-element.31), channel_id=1, source_target_pairs={{0,1},{1,2},{2,3},{3,0},{4,7},{5,4},{6,5},{7,6},{8,9},{9,10},{10,1... | collective-permute-start | bytes 4718600 | tf_op jit(solution)/shard_map/ppermute | solution.py:43
  50.0 133.9 %copy-start.12 = (bf16[256,2048]{1,0:T(8,128)(2,1)}, bf16[256,2048]{1,0:T(8,128)(2,1)S(1)}, u32[]{:S(2)}) copy-start(bf16[256,2048]{1,0:T(8,128)(2,1)S(1)} %collective-permute-done.11.refs_2_) | copy-start | bytes 3145732
  50.0 52.6 %collective-permute-start.9 = (bf16[1024,1024]{1,0:T(8,128)(2,1)S(1)}, bf16[1024,1024]{1,0:T(8,128)(2,1)S(1)}, u32[]{:S(2)}, u32[]{:S(2)}) collective-permute-start(bf16[1024,1024]{1,0:T(8,128)(2,1)S(1)} %pad_maximum_fusion.refs_3_.refs_0_), channel_id=1, source_target_pairs={{0,96},{4,36},{8,104},{12,44},{16,112},{20,52},{24,120},{28,60},{3... | collective-permute-start | bytes 6291464 | tf_op jit(solution)/shard_map/ppermute | solution.py:43
  50.1 52.6 %collective-permute-start.6 = (bf16[1024,1024]{1,0:T(8,128)(2,1)S(1)}, bf16[1024,1024]{1,0:T(8,128)(2,1)S(1)}, u32[]{:S(2)}, u32[]{:S(2)}) collective-permute-start(bf16[1024,1024]{1,0:T(8,128)(2,1)S(1)} %pad_maximum_fusion.refs_3_.refs_0_), channel_id=1, source_target_pairs={{0,4},{4,0},{8,12},{12,8},{16,20},{20,16},{24,28},{28,24},{32,36},... | collective-permute-start | bytes 6291464 | tf_op jit(solution)/shard_map/ppermute | solution.py:43
  66.9 35.7 %copy-start.8 = (bf16[384,2048]{1,0:T(8,128)(2,1)}, bf16[384,2048]{1,0:T(8,128)(2,1)S(1)}, u32[]{:S(2)}) copy-start(bf16[384,2048]{1,0:T(8,128)(2,1)S(1)} %collective-permute-done.refs_0_) | copy-start | bytes 4718596
  66.9 77.9 %collective-permute-start.2 = (bf16[768,2048]{1,0:T(8,128)(2,1)S(1)}, bf16[768,2048]{1,0:T(8,128)(2,1)S(1)}, u32[]{:S(2)}, u32[]{:S(2)}) collective-permute-start(bf16[768,2048]{1,0:T(8,128)(2,1)S(1)} %slice.21), channel_id=1, source_target_pairs={{0,3},{1,0},{2,1},{3,2},{4,5},{5,6},{6,7},{7,4},{8,11},{9,8},{10,9... | collective-permute-start | bytes 9437192 | tf_op jit(solution)/shard_map/ppermute | solution.py:43
  99.4 72.5 %copy-start.10 = (bf16[384,2048]{1,0:T(8,128)(2,1)}, bf16[384,2048]{1,0:T(8,128)(2,1)S(1)}, u32[]{:S(2)}) copy-start(bf16[384,2048]{1,0:T(8,128)(2,1)S(1)} %collective-permute-done.1.refs_1_) | copy-start | bytes 4718596
  99.4 42.6 %collective-permute-start.17 = (bf16[1024,1024]{1,0:T(8,128)(2,1)}, bf16[1024,1024]{1,0:T(8,128)(2,1)}, u32[]{:S(2)}, u32[]{:S(2)}) collective-permute-start(bf16[1024,1024]{1,0:T(8,128)(2,1)} %pad_maximum_fusion.1.refs_5_.refs_8_), channel_id=1, source_target_pairs={{0,8},{4,28},{8,16},{12,4},{16,24},{20,12},{24,0},{28,20},{32,40},... | collective-permute-start | bytes 6291464 | tf_op jit(solution)/shard_map/ppermute | solution.py:43
  99.4 42.6 %copy-start.2 = (bf16[1024,1024]{1,0:T(8,128)(2,1)}, bf16[1024,1024]{1,0:T(8,128)(2,1)S(1)}, u32[]{:S(2)}) copy-start(bf16[1024,1024]{1,0:T(8,128)(2,1)S(1)} %collective-permute-done.7.refs_5_.refs_2_) | copy-start | bytes 6291460
  99.4 45.0 %collective-permute-start.19 = (bf16[1024,1024]{1,0:T(8,128)(2,1)}, bf16[1024,1024]{1,0:T(8,128)(2,1)}, u32[]{:S(2)}, u32[]{:S(2)}) collective-permute-start(bf16[1024,1024]{1,0:T(8,128)(2,1)} %pad_maximum_fusion.1.refs_5_.refs_8_), channel_id=1, source_target_pairs={{0,24},{4,12},{8,0},{12,20},{16,8},{20,28},{24,16},{28,4},{32,56},... | collective-permute-start | bytes 6291464 | tf_op jit(solution)/shard_map/ppermute | solution.py:43
  102.6 66.7 %copy-start.3 = (bf16[1024,1024]{1,0:T(8,128)(2,1)}, bf16[1024,1024]{1,0:T(8,128)(2,1)S(1)}, u32[]{:S(2)}) copy-start(bf16[1024,1024]{1,0:T(8,128)(2,1)S(1)} %collective-permute-done.9.refs_7_.refs_4_) | copy-start | bytes 6291460
  102.6 42.2 %collective-permute-start.8 = (bf16[1024,1024]{1,0:T(8,128)(2,1)S(1)}, bf16[1024,1024]{1,0:T(8,128)(2,1)S(1)}, u32[]{:S(2)}, u32[]{:S(2)}) collective-permute-start(bf16[1024,1024]{1,0:T(8,128)(2,1)S(1)} %collective-permute-done.7.refs_5_.refs_2_), channel_id=1, source_target_pairs={{0,4},{4,0},{8,12},{12,8},{16,20},{20,16},{24,28},{28,24},{32,36},... | collective-permute-start | bytes 6291464 | tf_op jit(solution)/shard_map/ppermute | solution.py:43
  102.7 66.6 %copy-start.4 = (bf16[1024,1024]{1,0:T(8,128)(2,1)}, bf16[1024,1024]{1,0:T(8,128)(2,1)S(1)}, u32[]{:S(2)}) copy-start(bf16[1024,1024]{1,0:T(8,128)(2,1)S(1)} %collective-permute-done.6.refs_4_.refs_1_) | copy-start | bytes 6291460
  102.7 42.6 %collective-permute-start.10 = (bf16[1024,1024]{1,0:T(8,128)(2,1)S(1)}, bf16[1024,1024]{1,0:T(8,128)(2,1)S(1)}, u32[]{:S(2)}, u32[]{:S(2)}) collective-permute-start(bf16[1024,1024]{1,0:T(8,128)(2,1)S(1)} %collective-permute-done.9.refs_7_.refs_4_), channel_id=1, source_target_pairs={{0,4},{4,0},{8,12},{12,8},{16,20},{20,16},{24,28},{28,24},{32,36},... | collective-permute-start | bytes 6291464 | tf_op jit(solution)/shard_map/ppermute | solution.py:43
  141.9 27.4 %collective-permute-start.21 = (bf16[1024,1024]{1,0:T(8,128)(2,1)S(1)}, bf16[1024,1024]{1,0:T(8,128)(2,1)}, u32[]{:S(2)}, u32[]{:S(2)}) collective-permute-start(bf16[1024,1024]{1,0:T(8,128)(2,1)S(1)} %collective-permute-done.7.refs_5_.refs_2_), channel_id=1, source_target_pairs={{0,32},{4,100},{8,40},{12,108},{16,48},{20,116},{24,56},{28,124},{... | collective-permute-start | bytes 6291464 | tf_op jit(solution)/shard_map/ppermute | solution.py:43
  144.3 27.6 %collective-permute-start.23 = (bf16[1024,1024]{1,0:T(8,128)(2,1)}, bf16[1024,1024]{1,0:T(8,128)(2,1)}, u32[]{:S(2)}, u32[]{:S(2)}) collective-permute-start(bf16[1024,1024]{1,0:T(8,128)(2,1)} %collective-permute-done.17.refs_7_.refs_10_), channel_id=1, source_target_pairs={{0,8},{4,28},{8,16},{12,4},{16,24},{20,12},{24,0},{28,20},{32,40},... | collective-permute-start | bytes 6291464 | tf_op jit(solution)/shard_map/ppermute | solution.py:43
  144.8 27.1 %copy-start.7 = (bf16[768,2048]{1,0:T(8,128)(2,1)}, bf16[768,2048]{1,0:T(8,128)(2,1)S(1)}, u32[]{:S(2)}) copy-start(bf16[768,2048]{1,0:T(8,128)(2,1)S(1)} %collective-permute-done.2.refs_2_.refs_3_) | copy-start | bytes 9437188
  144.8 39.1 %collective-permute-start.16 = (bf16[1024,1024]{1,0:T(8,128)(2,1)}, bf16[1024,1024]{1,0:T(8,128)(2,1)}, u32[]{:S(2)}, u32[]{:S(2)}) collective-permute-start(bf16[1024,1024]{1,0:T(8,128)(2,1)} %pad_maximum_fusion.1.refs_5_.refs_8_), channel_id=1, source_target_pairs={{0,4},{4,0},{8,12},{12,8},{16,20},{20,16},{24,28},{28,24},{32,36},... | collective-permute-start | bytes 6291464 | tf_op jit(solution)/shard_map/ppermute | solution.py:43
  144.8 27.1 %copy-start.5 = (bf16[1024,1024]{1,0:T(8,128)(2,1)}, bf16[1024,1024]{1,0:T(8,128)(2,1)S(1)}, u32[]{:S(2)}) copy-start(bf16[1024,1024]{1,0:T(8,128)(2,1)S(1)} %collective-permute-done.8.refs_6_.refs_3_) | copy-start | bytes 6291460
  144.8 39.2 %collective-permute-start.18 = (bf16[1024,1024]{1,0:T(8,128)(2,1)}, bf16[1024,1024]{1,0:T(8,128)(2,1)}, u32[]{:S(2)}, u32[]{:S(2)}) collective-permute-start(bf16[1024,1024]{1,0:T(8,128)(2,1)} %collective-permute-done.17.refs_7_.refs_10_), channel_id=1, source_target_pairs={{0,4},{4,0},{8,12},{12,8},{16,20},{20,16},{24,28},{28,24},{32,36},... | collective-permute-start | bytes 6291464 | tf_op jit(solution)/shard_map/ppermute | solution.py:43
  145.3 26.7 %copy-start.6 = (bf16[1024,1024]{1,0:T(8,128)(2,1)}, bf16[1024,1024]{1,0:T(8,128)(2,1)S(1)}, u32[]{:S(2)}) copy-start(bf16[1024,1024]{1,0:T(8,128)(2,1)S(1)} %collective-permute-done.10.refs_8_.refs_5_) | copy-start | bytes 6291460
  145.3 41.0 %collective-permute-start.20 = (bf16[1024,1024]{1,0:T(8,128)(2,1)}, bf16[1024,1024]{1,0:T(8,128)(2,1)}, u32[]{:S(2)}, u32[]{:S(2)}) collective-permute-start(bf16[1024,1024]{1,0:T(8,128)(2,1)} %collective-permute-done.19.refs_9_.refs_12_), channel_id=1, source_target_pairs={{0,4},{4,0},{8,12},{12,8},{16,20},{20,16},{24,28},{28,24},{32,36},... | collective-permute-start | bytes 6291464 | tf_op jit(solution)/shard_map/ppermute | solution.py:43
  169.3 39.1 %collective-permute-start.22 = (bf16[1024,1024]{1,0:T(8,128)(2,1)}, bf16[1024,1024]{1,0:T(8,128)(2,1)}, u32[]{:S(2)}, u32[]{:S(2)}) collective-permute-start(bf16[1024,1024]{1,0:T(8,128)(2,1)} %collective-permute-done.21.refs_6_), channel_id=1, source_target_pairs={{0,4},{4,0},{8,12},{12,8},{16,20},{20,16},{24,28},{28,24},{32,36},... | collective-permute-start | bytes 6291464 | tf_op jit(solution)/shard_map/ppermute | solution.py:43
  171.9 36.5 %collective-permute-start.24 = (bf16[1024,1024]{1,0:T(8,128)(2,1)}, bf16[1024,1024]{1,0:T(8,128)(2,1)}, u32[]{:S(2)}, u32[]{:S(2)}) collective-permute-start(bf16[1024,1024]{1,0:T(8,128)(2,1)} %collective-permute-done.23.refs_14_), channel_id=1, source_target_pairs={{0,4},{4,0},{8,12},{12,8},{16,20},{20,16},{24,28},{28,24},{32,36},... | collective-permute-start | bytes 6291464 | tf_op jit(solution)/shard_map/ppermute | solution.py:43
  172.0 12.0 %copy-start.9 = (bf16[384,2048]{1,0:T(8,128)(2,1)S(1)}, bf16[384,2048]{1,0:T(8,128)(2,1)}, u32[]{:S(2)}) copy-start(bf16[384,2048]{1,0:T(8,128)(2,1)} %copy-done.8) | copy-start | bytes 4718596
  172.0 14.3 %copy-start.11 = (bf16[384,2048]{1,0:T(8,128)(2,1)S(1)}, bf16[384,2048]{1,0:T(8,128)(2,1)}, u32[]{:S(2)}) copy-start(bf16[384,2048]{1,0:T(8,128)(2,1)} %copy-done.10) | copy-start | bytes 4718596
  184.0 59.0 %collective-permute-start.27 = (bf16[256,2048]{1,0:T(8,128)(2,1)S(1)}, bf16[256,2048]{1,0:T(8,128)(2,1)S(1)}, u32[]{:S(2)}, u32[]{:S(2)}) collective-permute-start(bf16[256,2048]{1,0:T(8,128)(2,1)S(1)} %collective-permute-done.11.refs_2_), channel_id=1, source_target_pairs={{0,1},{1,2},{2,3},{3,0},{4,7},{5,4},{6,5},{7,6},{8,9},{9,10},{10,1... | collective-permute-start | bytes 3145736 | tf_op jit(solution)/shard_map/ppermute | solution.py:43
  184.1 36.1 %collective-permute-start.25 = (bf16[384,2048]{1,0:T(8,128)(2,1)S(1)}, bf16[384,2048]{1,0:T(8,128)(2,1)S(1)}, u32[]{:S(2)}, u32[]{:S(2)}) collective-permute-start(bf16[384,2048]{1,0:T(8,128)(2,1)S(1)} %copy-done.9), channel_id=1, source_target_pairs={{0,1},{1,2},{2,3},{3,0},{4,7},{5,4},{6,5},{7,6},{8,9},{9,10},{10,1... | collective-permute-start | bytes 4718600 | tf_op jit(solution)/shard_map/ppermute | solution.py:43
  186.4 47.6 %collective-permute-start.26 = (bf16[384,2048]{1,0:T(8,128)(2,1)S(1)}, bf16[384,2048]{1,0:T(8,128)(2,1)S(1)}, u32[]{:S(2)}, u32[]{:S(2)}) collective-permute-start(bf16[384,2048]{1,0:T(8,128)(2,1)S(1)} %copy-done.11), channel_id=1, source_target_pairs={{0,1},{1,2},{2,3},{3,0},{4,7},{5,4},{6,5},{7,6},{8,9},{9,10},{10,1... | collective-permute-start | bytes 4718600 | tf_op jit(solution)/shard_map/ppermute | solution.py:43
  245.5 5.2 %collective-permute-start.28 = (f32[8,1024]{1,0:T(8,128)S(1)}, f32[8,1024]{1,0:T(8,128)S(1)}, u32[]{:S(2)}, u32[]{:S(2)}) collective-permute-start(f32[8,1024]{1,0:T(8,128)S(1)} %get-tuple-element.30.refs_0_), channel_id=1, source_target_pairs={{0,1},{1,2},{2,3},{3,0},{4,7},{5,4},{6,5},{7,6},{8,9},{9,10},{10,1... | collective-permute-start | bytes 98312 | tf_op jit(solution)/shard_map/ppermute | solution.py:43
  245.6 5.1 %collective-permute-start.29 = (f32[8,1024]{1,0:T(8,128)S(1)}, f32[8,1024]{1,0:T(8,128)S(1)}, u32[]{:S(2)}, u32[]{:S(2)}) collective-permute-start(f32[8,1024]{1,0:T(8,128)S(1)} %get-tuple-element.30.refs_0_), channel_id=1, source_target_pairs={{0,3},{1,0},{2,1},{3,2},{4,5},{5,6},{6,7},{7,4},{8,11},{9,8},{10,9... | collective-permute-start | bytes 98312 | tf_op jit(solution)/shard_map/ppermute | solution.py:43
  248.8 5.4 %collective-permute-start.30 = (f32[8,1024]{1,0:T(8,128)S(1)}, f32[8,1024]{1,0:T(8,128)S(1)}, u32[]{:S(2)}, u32[]{:S(2)}) collective-permute-start(f32[8,1024]{1,0:T(8,128)S(1)} %get-tuple-element.30.refs_0_), channel_id=1, source_target_pairs={{0,2},{1,3},{2,0},{3,1},{4,6},{5,7},{6,4},{7,5},{8,10},{9,11},{10,... | collective-permute-start | bytes 98312 | tf_op jit(solution)/shard_map/ppermute | solution.py:53

commit v3 on v2

--- a/solution.py
+++ b/solution.py
@@ -158,7 +158,7 @@
 
 def left_kernel(low, pos, left, *refs):
     (first, second, side), lines, (acc, a_v, t_v, a_sem, t_sem) = refs[:3], refs[3:9], refs[9:]
-    sources = [left.at[pl.ds(0, low), :]], [first, second], [side]
+    sources = [left.at[pl.ds(0, low), :]], [first, second], [side.at[pl.ds(0, low), :]]
     half, nt, seg = acc.shape[1] // 2, t_v.shape[2], a_v.shape[1] // 12
     blocks, where = plan(pos)
     fetch = left_tiles(pos, lines, blocks, nt, seg, t_v, t_sem)
@@ -184,10 +184,10 @@
 
 
 def right_kernel(low, pos, a_in, before, left, *refs):
-    chunks, lines, (acc, a_v, t_v, a_sem, t_sem) = refs[:5], refs[5:11], refs[11:]
+    chunks, side, lines, (acc, a_v, t_v, a_sem, t_sem) = refs[:3], refs[3], refs[4:10], refs[10:]
     rows = left.shape[0]
-    upper = [left.at[pl.ds(0, low), :]], chunks[:2], chunks[3:4]
-    lower = [left.at[pl.ds(low, rows - low), :]], chunks[2:3], chunks[4:]
+    upper = [left.at[pl.ds(0, low), :]], chunks[:2], [side.at[pl.ds(0, low), :]]
+    lower = [left.at[pl.ds(low, rows - low), :]], chunks[2:], [side.at[pl.ds(low, rows - low), :]]
     pieces = [None, [lines[2 * k:2 * k + 2] for k in range(3)]]
     half, nt, seg = acc.shape[1] // 2, t_v.shape[2], a_v.shape[1] // 12
     blocks, where = plan(pos)
@@ -196,29 +196,27 @@
         copy_right_half(
             pos, pieces, s * nt, [blocks[p]], range(3), lambda _, t: (3 * p + t) * seg, t_v.at[s % 2], t_sem.at[s % 2, p])
 
-    fetch(0, 0)
-    for b in range(3):
-        copy_left(lower[b], low, lambda x: spot(where[b], turned(x, pos[1]), seg), seg, a_v, a_sem.at[0])
-    for p in range(1, 3):
+    for p in range(3):
         fetch(0, p)
     for b in range(3):
         @pl.when(where[b] == 2)
         def _():
             copy_left(upper[b], 0, lambda x: spot(2, turned(x, pos[1]), seg), seg, a_v, a_sem.at[1])
+    for b in range(3):
+        copy_left(lower[b], low, lambda x: spot(where[b], turned(x, pos[1]), seg), seg, a_v, a_sem.at[0])
     for s in range(half // nt):
         for p in range(3):
             if (s + 1) * nt < half:
                 fetch(s + 1, p)
         for p in range(3):
-            if (s, p) == (0, 0):
-                landed(a_v.at[pl.ds(low, rows - low), :], a_sem.at[0])
             if (s, p) == (0, 2):
                 landed(a_v.at[pl.ds(0, low), pl.ds(0, 4 * seg)], a_sem.at[1])
             landed(t_v.at[s % 2, pl.ds(0, 3 * seg), :], t_sem.at[s % 2, p])
             if s == 0:
-                multiply(a_v, t_v.at[0], acc, half, (((2 + 3 * p) * seg, 3 * p * seg, 3 * seg),), p > 0)
-        if s > 0:
-            multiply(a_v, t_v.at[s % 2], acc, half + s * nt, ((2 * seg, 0, 9 * seg),), False)
+                multiply(a_v, t_v.at[0], acc, half, (((2 + 3 * p) * seg, 3 * p * seg, 3 * seg),), p > 0, 0, low)
+        if s == 0:
+            landed(a_v.at[pl.ds(low, rows - low), :], a_sem.at[0])
+        multiply(a_v, t_v.at[s % 2], acc, half + s * nt, ((2 * seg, 0, 9 * seg),), False, low if s == 0 else 0)
 
 
 def tail_kernel(low, pos, a_in, before, *refs):
@@ -338,7 +336,7 @@
 
 def near(pos, left, behind, ahead, pieces):
     rows, depth = left.shape
-    half, seg, low = pieces[0].shape[1], depth // 4, ahead[0].shape[0]
+    half, seg, low = pieces[0].shape[1], depth // 4, rows - behind[-1].shape[0]
     total, gathered = pltpu.VMEM((rows, 2 * half), jnp.float32), pltpu.VMEM((rows, 12 * seg), left.dtype)
     both = total, gathered
     flops = 2 * rows * half * seg
@@ -347,11 +345,11 @@
     acc, blocks = call(
         functools.partial(left_kernel, low), both, [SMEM] + [ANY] * 10, (VMEM, VMEM),
         [tile, dma((2,)), dma((2, 2))], 6 * flops, NEAR_MIB,
-    )(pos, left, *behind[:2], ahead[0], *pieces[:6])
+    )(pos, left, *behind[:2], ahead, *pieces[:6])
     acc, blocks = call(
-        functools.partial(right_kernel, low), both, [SMEM, VMEM, VMEM] + [ANY] * 12, (VMEM, VMEM),
+        functools.partial(right_kernel, low), both, [SMEM, VMEM, VMEM] + [ANY] * 11, (VMEM, VMEM),
         [pltpu.VMEM((2, 9 * seg, NT), left.dtype), dma((2,)), dma((2, 3))], 9 * flops, NEAR_MIB, {1: 1, 2: 0},
-    )(pos, kept(blocks), kept(acc), left, *behind, *ahead, *pieces[8:14])
+    )(pos, kept(blocks), kept(acc), left, *behind, ahead, *pieces[8:14])
     acc, blocks = call(
         functools.partial(tail_kernel, low), both, [SMEM, VMEM, VMEM] + [ANY] * 6, (VMEM, VMEM),
         [tile, dma((2, 2))], 2 * flops, NEAR_MIB, {1: 1, 2: 0},
@@ -390,8 +388,7 @@
     me, z = lax.axis_index("gy"), lax.axis_index("gx")
     pos = jnp.stack([me // (NX * NC), (me // NC) % NX, me % NC, z]).astype(jnp.int32)
 
-    most = sum(ROW_CHUNKS[:-1])
-    ahead = [move(left[:most], "z", False), move(left[most:], "z", False)]
+    ahead = move(left, "z", False)
     behind, opposite, low = [], [], 0
     for i, size in enumerate(ROW_CHUNKS):
         behind.append(move(left[low:low + size], "z", True))
@@ -403,8 +400,8 @@
         for v in ring(line, b):
             pieces += [v, move(v, "core", True)]
 
-    pieces = [apart(v) for v in pieces]
-    acc, tile = near(pos, apart(left), [apart(v) for v in behind], [apart(v) for v in ahead], pieces)
+    pieces = [v if i % 8 == 7 else apart(v) for i, v in enumerate(pieces)]
+    acc, tile = near(pos, apart(left), [apart(v) for v in behind], apart(ahead), pieces)
     acc, tile, power = far(acc, tile, opposite[:-1], [])
     acc, tile, power = far(acc, tile, opposite[-1:], [power])
     return scale(width * NZ, acc, exchange(power))

time: 258 us -> 237 us (0.919)
  waiting for transfers between devices: 158 us -> 141 us
  starting transfers between devices: 35.6 us -> 32.4 us
    ppermute x30 -> x29, waiting for transfers between devices: 155 us -> 138 us  [move(): return lax.ppermute(value, name, along(axis, first))]
    ppermute x30 -> x29, starting transfers between devices: 35.3 us -> 32.4 us  [move(): return lax.ppermute(value, name, along(axis, first))]
  transfers between devices with their start and end apart: 31 -> 30, of which waited for: 13 -> 13; matrix products, arithmetic and copies ran while one was open for 2% -> 2% of each run, Pallas kernels for 20% -> 21%
where the time goes in v3:
time: 237 us
  waiting for transfers between devices  141 us (59%)
  Pallas kernels  57 us (24%)
  starting transfers between devices  32.4 us (14%)
  local copies, waits for them, and re-layouts  3.69 us (2%)
    ppermute x29, waiting for transfers between devices, move(): return lax.ppermute(value, name, along(axis, first))  138 us
    ppermute x29, starting transfers between devices, move(): return lax.ppermute(value, name, along(axis, first))  32.4 us
    pallas_call x1, Pallas kernels, near(): call(functools.partial(right_kernel, low), both, [SMEM, VMEM, VMEM] + [AN...  13.4 us
    pallas_call x2, Pallas kernels, far(): call(functools.partial(far_kernel, low), out, [VMEM, VMEM] + [VMEM] * len...  11.8 us
    pallas_call x1, Pallas kernels, near(): call(rest_kernel, (total, pltpu.VMEM((parts, depth, NT), left.dtype)), [S...  11.7 us
    pallas_call x1, Pallas kernels, near(): call(functools.partial(left_kernel, low), both, [SMEM] + [ANY] * 10, (VME...  11.6 us
    pallas_call x1, Pallas kernels, near(): call(functools.partial(tail_kernel, low), both, [SMEM, VMEM, VMEM] + [ANY...  4.89 us
  transfers between devices with their start and end apart: 30, of which 13 were waited for; matrix products, arithmetic and copies ran while one was open for 2% of the time, Pallas kernels for 21%

profile of v3, /device:TPU:0, one launch (start us, length us, event | category | flops | bytes accessed | tf_op | source)
XLA Modules:
  0.0 236.5 jit_solution(9968581299121765029)
XLA Ops:
  0.0 1.3 fusion.1
  1.3 1.7 collective-permute-start.3
  3.0 1.6 collective-permute-start.4
  4.6 11.3 %collective-permute-done.3 = bf16[256,1024]{1,0:T(8,128)(2,1)S(1)} collective-permute-done((bf16[256,1024]{1,0:T(8,128)(2,1)S(1)}, bf16[256,1024]{1,0:T(8,128)(2,1)S(1)}, u32[]{:S(2)}, u32[]{:S(2)}) %collective-permute-start.3) | collective-permute-done | bytes 524320 | tf_op jit(solution)/shard_map/ppermute | solution.py:43
  15.9 1.7 collective-permute-start.5
  17.6 2.3 fusion
  19.9 2.0 collective-permute-start
  21.9 1.6 collective-permute-start.12
  23.5 1.7 collective-permute-start.13
  25.1 0.1 slice.18
  25.3 2.0 collective-permute-start.11
  27.2 0.2 pad_maximum_fusion.refs_3_.refs_0_
  27.4 0.9 collective-permute-start.7
  28.4 6.2 %collective-permute-done.12 = bf16[256,1024]{1,0:T(8,128)(2,1)S(1)} collective-permute-done((bf16[256,1024]{1,0:T(8,128)(2,1)S(1)}, bf16[256,1024]{1,0:T(8,128)(2,1)S(1)}, u32[]{:S(2)}, u32[]{:S(2)}) %collective-permute-start.12) | collective-permute-done | bytes 524320 | tf_op jit(solution)/shard_map/ppermute | solution.py:43
  34.6 2.0 collective-permute-start.14
  36.6 1.6 collective-permute-done.13
  38.3 1.8 collective-permute-start.1
  40.0 25.9 %collective-permute-done.14 = bf16[256,1024]{1,0:T(8,128)(2,1)S(1)} collective-permute-done((bf16[256,1024]{1,0:T(8,128)(2,1)S(1)}, bf16[256,1024]{1,0:T(8,128)(2,1)S(1)}, u32[]{:S(2)}, u32[]{:S(2)}) %collective-permute-start.14) | collective-permute-done | bytes 524320 | tf_op jit(solution)/shard_map/ppermute | solution.py:43
  66.0 2.2 collective-permute-start.2
  68.2 1.0 collective-permute-start.9
  69.2 1.5 pad_maximum_fusion.1.refs_4_.refs_8_
  70.8 0.8 collective-permute-done.1.refs_1_
  71.5 2.8 %collective-permute-start.16 = (bf16[1024,1024]{1,0:T(8,128)(2,1)}, bf16[1024,1024]{1,0:T(8,128)(2,1)}, u32[]{:S(2)}, u32[]{:S(2)}) collective-permute-start(bf16[1024,1024]{1,0:T(8,128)(2,1)} %pad_maximum_fusion.1.refs_4_.refs_8_), channel_id=1, source_target_pairs={{0,8},{4,28},{8,16},{12,4},{16,24},{20,12},{24,0},{28,20},{32,40},... | collective-permute-start | bytes 6291464 | tf_op jit(solution)/shard_map/ppermute | solution.py:43
  74.4 0.4 collective-permute-start.18
  74.8 19.5 %collective-permute-done.9.refs_7_.refs_4_ = bf16[1024,1024]{1,0:T(8,128)(2,1)S(1)} collective-permute-done((bf16[1024,1024]{1,0:T(8,128)(2,1)S(1)}, bf16[1024,1024]{1,0:T(8,128)(2,1)S(1)}, u32[]{:S(2)}, u32[]{:S(2)}) %collective-permute-start.9) | collective-permute-done | bytes 2097184 | tf_op jit(solution)/shard_map/ppermute | solution.py:43
  94.3 0.5 collective-permute-start.10
  94.8 26.2 %collective-permute-done.16.refs_6_.refs_10_ = bf16[1024,1024]{1,0:T(8,128)(2,1)} collective-permute-done((bf16[1024,1024]{1,0:T(8,128)(2,1)}, bf16[1024,1024]{1,0:T(8,128)(2,1)}, u32[]{:S(2)}, u32[]{:S(2)}) %collective-permute-start.16) | collective-permute-done | bytes 2097184 | tf_op jit(solution)/shard_map/ppermute | solution.py:43
  120.9 1.9 collective-permute-start.20
  122.9 0.1 collective-permute-start.15
  123.0 0.5 collective-permute-start.17
  123.5 0.1 collective-permute-start.19
  123.6 24.7 %collective-permute-done.20.refs_6_ = bf16[1024,1024]{1,0:T(8,128)(2,1)} collective-permute-done((bf16[1024,1024]{1,0:T(8,128)(2,1)S(1)}, bf16[1024,1024]{1,0:T(8,128)(2,1)}, u32[]{:S(2)}, u32[]{:S(2)}) %collective-permute-start.20) | collective-permute-done | bytes 2097184 | tf_op jit(solution)/shard_map/ppermute | solution.py:43
  148.3 2.1 collective-permute-done.22.refs_14_
  150.5 0.1 pad_add_fusion.pos
  150.6 11.6 %shard_map.28 = (f32[1024,2048]{1,0:T(8,128)S(1)}, bf16[1024,6144]{1,0:T(8,128)(2,1)S(1)}) custom-call(s32[4]{0:T(128)S(1)} %pad_add_fusion.pos, bf16[1024,2048]{1,0:T(8,128)(2,1)} %left.3, bf16[384,2048]{1,0:T(8,128)(2,1)} %collective-permute-done.refs_0_, bf16[384,2048]{1,0:T(8,128)(2,1)} %copy-done.8, bf16[1024,2048]{1,0:T(8,128)(2,1)} %copy-done.7, ...), custom_call_target="tpu_custom_call" | custom-call | flops 6442450944 | bytes 16777216 | tf_op jit(solution)/shard_map/pallas_call | solution.py:345
  162.3 0.3 collective-permute-start.24
  162.6 2.2 collective-permute-start.25
  164.8 13.4 %shard_map.29 = (f32[1024,2048]{1,0:T(8,128)S(1)}, bf16[1024,6144]{1,0:T(8,128)(2,1)S(1)}) custom-call(s32[4]{0:T(128)S(1)} %pad_add_fusion.pos, bf16[1024,6144]{1,0:T(8,128)(2,1)S(1)} %get-tuple-element.18.a_in, f32[1024,2048]{1,0:T(8,128)S(1)} %get-tuple-element.19.before, bf16[1024,2048]{1,0:T(8,128)(2,1)} %left.3, ...), custom_call_target="tpu_custom_call", output_to_operand_aliasing={{1}: (1, {}), {0}: (2, {})} | custom-call | flops 9663676416 | bytes 16777216 | tf_op jit(solution)/shard_map/pallas_call | solution.py:349
  178.2 4.9 %shard_map.30 = (f32[1024,2048]{1,0:T(8,128)S(1)}, bf16[1024,6144]{1,0:T(8,128)(2,1)S(1)}) custom-call(s32[4]{0:T(128)S(1)} %pad_add_fusion.pos, bf16[1024,6144]{1,0:T(8,128)(2,1)S(1)} %get-tuple-element.20.a_in, f32[1024,2048]{1,0:T(8,128)S(1)} %get-tuple-element.21.before, ...), custom_call_target="tpu_custom_call", output_to_operand_aliasing={{1}: (1, {}), {0}: (2, {})} | custom-call | flops 2147483648 | bytes 16777216 | tf_op jit(solution)/shard_map/pallas_call | solution.py:353
  183.1 11.7 %shard_map.31 = (f32[1024,2048]{1,0:T(8,128)S(1)}, bf16[4,2048,512]{2,1,0:T(8,128)(2,1)S(1)}) custom-call(s32[4]{0:T(128)S(1)} %pad_add_fusion.pos, bf16[1024,6144]{1,0:T(8,128)(2,1)S(1)} %get-tuple-element.22.a_v, f32[1024,2048]{1,0:T(8,128)S(1)} %get-tuple-element.23.before, bf16[1024,1024]{1,0:T(8,128)(2,1)} %copy-done.1, ...), custom_call_target="tpu_custom_call", output_to_operand_aliasing={{0}: (2, {})} | custom-call | flops 7516192768 | bytes 16777216 | tf_op jit(solution)/shard_map/pallas_call | solution.py:358
  194.9 0.5 collective-permute-done.24.refs_0_
  195.4 16.9 %collective-permute-done.25.refs_1_ = bf16[384,2048]{1,0:T(8,128)(2,1)S(1)} collective-permute-done((bf16[384,2048]{1,0:T(8,128)(2,1)S(1)}, bf16[384,2048]{1,0:T(8,128)(2,1)S(1)}, u32[]{:S(2)}, u32[]{:S(2)}) %collective-permute-start.25) | collective-permute-done | bytes 1572896 | tf_op jit(solution)/shard_map/ppermute | solution.py:43
  212.2 9.2 %shard_map.32 = (f32[1024,2048]{1,0:T(8,128)S(1)}, bf16[4,2048,512]{2,1,0:T(8,128)(2,1)S(1)}, f32[8,768]{1,0:T(8,128)S(1)}) custom-call(f32[1024,2048]{1,0:T(8,128)S(1)} %get-tuple-element.24.before, bf16[4,2048,512]{2,1,0:T(8,128)(2,1)S(1)} %get-tuple-element.25.t_in, ...), custom_call_target="tpu_custom_call", output_to_operand_aliasing={{0}: (0, {}), {1}: (1, {})} | custom-call | flops 6442450944 | bytes 16777216 | tf_op jit(solution)/shard_map/pallas_call | solution.py:369
  221.4 2.6 %shard_map.33 = (f32[1024,2048]{1,0:T(8,128)S(1)}, bf16[4,2048,512]{2,1,0:T(8,128)(2,1)S(1)}, f32[8,1024]{1,0:T(8,128)S(1)}) custom-call(f32[1024,2048]{1,0:T(8,128)S(1)} %get-tuple-element.26.before, bf16[4,2048,512]{2,1,0:T(8,128)(2,1)S(1)} %get-tuple-element.27.t_in, ...), custom_call_target="tpu_custom_call", output_to_operand_aliasing={{0}: (0, {}), {1}: (1, {})} | custom-call | flops 2147483648 | bytes 16777216 | tf_op jit(solution)/shard_map/pallas_call | solution.py:369
  224.1 3.2 %collective-permute-start.28 = (f32[8,1024]{1,0:T(8,128)S(1)}, f32[8,1024]{1,0:T(8,128)S(1)}, u32[]{:S(2)}, u32[]{:S(2)}) collective-permute-start(f32[8,1024]{1,0:T(8,128)S(1)} %get-tuple-element.30.refs_0_), channel_id=1, source_target_pairs={{0,3},{1,0},{2,1},{3,2},{4,5},{5,6},{6,7},{7,4},{8,11},{9,8},{10,9... | collective-permute-start | bytes 98312 | tf_op jit(solution)/shard_map/ppermute | solution.py:43
  227.3 1.9 collective-permute-done.27.refs_1_
  229.2 3.5 %collective-permute-done.29.refs_3_ = f32[8,1024]{1,0:T(8,128)S(1)} collective-permute-done((f32[8,1024]{1,0:T(8,128)S(1)}, f32[8,1024]{1,0:T(8,128)S(1)}, u32[]{:S(2)}, u32[]{:S(2)}) %collective-permute-start.29) | collective-permute-done | bytes 32800 | tf_op jit(solution)/shard_map/ppermute | solution.py:53
  232.7 3.7 %shard_map.34 = f32[1024,2048]{1,0:T(8,128)} custom-call(f32[1024,2048]{1,0:T(8,128)S(1)} %get-tuple-element.29.acc, f32[8,1024]{1,0:T(8,128)S(1)} %get-tuple-element.30.refs_0_, f32[8,1024]{1,0:T(8,128)S(1)} %collective-permute-done.27.refs_1_, f32[8,1024]{1,0:T(8,128)S(1)} %collective-permute-done.28.refs_2_, f32[8,1024]{1,0:T(8,128)S(1)} %collective-permute-done.29.refs_3_), custom_call_target="tpu_custom_call" | custom-call | flops 62914560 | bytes 16777216 | tf_op jit(solution)/shard_map/pallas_call | solution.py:378
  (45 shorter events, 0.3 us)
Async XLA Ops:
  1.3 23.9 %copy-start = (bf16[1024,2048]{1,0:T(8,128)(2,1)S(1)}, bf16[1024,2048]{1,0:T(8,128)(2,1)}, u32[]{:S(2)}) copy-start(bf16[1024,2048]{1,0:T(8,128)(2,1)} %left.3) | copy-start | bytes 12582916
  1.3 14.6 %collective-permute-start.3 = (bf16[256,1024]{1,0:T(8,128)(2,1)S(1)}, bf16[256,1024]{1,0:T(8,128)(2,1)S(1)}, u32[]{:S(2)}, u32[]{:S(2)}) collective-permute-start(bf16[256,1024]{1,0:T(8,128)(2,1)S(1)} %get-tuple-element.34), channel_id=1, source_target_pairs={{0,8},{4,28},{8,16},{12,4},{16,24},{20,12},{24,0},{28,20},{32,40},... | collective-permute-start | bytes 1572872 | tf_op jit(solution)/shard_map/ppermute | solution.py:43
  3.0 22.3 %collective-permute-start.4 = (bf16[256,1024]{1,0:T(8,128)(2,1)S(1)}, bf16[256,1024]{1,0:T(8,128)(2,1)S(1)}, u32[]{:S(2)}, u32[]{:S(2)}) collective-permute-start(bf16[256,1024]{1,0:T(8,128)(2,1)S(1)} %get-tuple-element.34), channel_id=1, source_target_pairs={{0,24},{4,12},{8,0},{12,20},{16,8},{20,28},{24,16},{28,4},{32,56},... | collective-permute-start | bytes 1572872 | tf_op jit(solution)/shard_map/ppermute | solution.py:43
  15.9 11.3 %collective-permute-start.5 = (bf16[256,1024]{1,0:T(8,128)(2,1)S(1)}, bf16[256,1024]{1,0:T(8,128)(2,1)S(1)}, u32[]{:S(2)}, u32[]{:S(2)}) collective-permute-start(bf16[256,1024]{1,0:T(8,128)(2,1)S(1)} %collective-permute-done.3), channel_id=1, source_target_pairs={{0,8},{4,28},{8,16},{12,4},{16,24},{20,12},{24,0},{28,20},{32,40},... | collective-permute-start | bytes 1572872 | tf_op jit(solution)/shard_map/ppermute | solution.py:43
  19.9 49.3 %collective-permute-start = (bf16[384,2048]{1,0:T(8,128)(2,1)S(1)}, bf16[384,2048]{1,0:T(8,128)(2,1)}, u32[]{:S(2)}, u32[]{:S(2)}) collective-permute-start(bf16[384,2048]{1,0:T(8,128)(2,1)S(1)} %get-tuple-element.32), channel_id=1, source_target_pairs={{0,1},{1,2},{2,3},{3,0},{4,7},{5,4},{6,5},{7,6},{8,9},{9,10},{10,1... | collective-permute-start | bytes 4718600 | tf_op jit(solution)/shard_map/ppermute | solution.py:43
  21.9 12.7 %collective-permute-start.12 = (bf16[256,1024]{1,0:T(8,128)(2,1)S(1)}, bf16[256,1024]{1,0:T(8,128)(2,1)S(1)}, u32[]{:S(2)}, u32[]{:S(2)}) collective-permute-start(bf16[256,1024]{1,0:T(8,128)(2,1)S(1)} %get-tuple-element.33), channel_id=1, source_target_pairs={{0,32},{4,100},{8,40},{12,108},{16,48},{20,116},{24,56},{28,124},{... | collective-permute-start | bytes 1572872 | tf_op jit(solution)/shard_map/ppermute | solution.py:43
  23.5 14.8 %collective-permute-start.13 = (bf16[256,1024]{1,0:T(8,128)(2,1)S(1)}, bf16[256,1024]{1,0:T(8,128)(2,1)S(1)}, u32[]{:S(2)}, u32[]{:S(2)}) collective-permute-start(bf16[256,1024]{1,0:T(8,128)(2,1)S(1)} %get-tuple-element.33), channel_id=1, source_target_pairs={{0,96},{4,36},{8,104},{12,44},{16,112},{20,52},{24,120},{28,60},{3... | collective-permute-start | bytes 1572872 | tf_op jit(solution)/shard_map/ppermute | solution.py:43
  25.3 42.9 %collective-permute-start.11 = (bf16[256,2048]{1,0:T(8,128)(2,1)S(1)}, bf16[256,2048]{1,0:T(8,128)(2,1)}, u32[]{:S(2)}, u32[]{:S(2)}) collective-permute-start(bf16[256,2048]{1,0:T(8,128)(2,1)S(1)} %slice.18), channel_id=1, source_target_pairs={{0,1},{1,2},{2,3},{3,0},{4,7},{5,4},{6,5},{7,6},{8,9},{9,10},{10,1... | collective-permute-start | bytes 3145736 | tf_op jit(solution)/shard_map/ppermute | solution.py:43
  27.4 43.3 %copy-start.1 = (bf16[1024,1024]{1,0:T(8,128)(2,1)}, bf16[1024,1024]{1,0:T(8,128)(2,1)S(1)}, u32[]{:S(2)}) copy-start(bf16[1024,1024]{1,0:T(8,128)(2,1)S(1)} %pad_maximum_fusion.refs_3_.refs_0_) | copy-start | bytes 6291460
  27.4 46.9 %collective-permute-start.7 = (bf16[1024,1024]{1,0:T(8,128)(2,1)S(1)}, bf16[1024,1024]{1,0:T(8,128)(2,1)S(1)}, u32[]{:S(2)}, u32[]{:S(2)}) collective-permute-start(bf16[1024,1024]{1,0:T(8,128)(2,1)S(1)} %pad_maximum_fusion.refs_3_.refs_0_), channel_id=1, source_target_pairs={{0,32},{4,100},{8,40},{12,108},{16,48},{20,116},{24,56},{28,124},{... | collective-permute-start | bytes 6291464 | tf_op jit(solution)/shard_map/ppermute | solution.py:43
  34.6 31.4 %collective-permute-start.14 = (bf16[256,1024]{1,0:T(8,128)(2,1)S(1)}, bf16[256,1024]{1,0:T(8,128)(2,1)S(1)}, u32[]{:S(2)}, u32[]{:S(2)}) collective-permute-start(bf16[256,1024]{1,0:T(8,128)(2,1)S(1)} %collective-permute-done.12), channel_id=1, source_target_pairs={{0,32},{4,100},{8,40},{12,108},{16,48},{20,116},{24,56},{28,124},{... | collective-permute-start | bytes 1572872 | tf_op jit(solution)/shard_map/ppermute | solution.py:43
  38.3 33.3 %collective-permute-start.1 = (bf16[384,2048]{1,0:T(8,128)(2,1)S(1)}, bf16[384,2048]{1,0:T(8,128)(2,1)S(1)}, u32[]{:S(2)}, u32[]{:S(2)}) collective-permute-start(bf16[384,2048]{1,0:T(8,128)(2,1)S(1)} %get-tuple-element.31), channel_id=1, source_target_pairs={{0,1},{1,2},{2,3},{3,0},{4,7},{5,4},{6,5},{7,6},{8,9},{9,10},{10,1... | collective-permute-start | bytes 4718600 | tf_op jit(solution)/shard_map/ppermute | solution.py:43
  66.0 56.9 %collective-permute-start.2 = (bf16[1024,2048]{1,0:T(8,128)(2,1)S(1)}, bf16[1024,2048]{1,0:T(8,128)(2,1)S(1)}, u32[]{:S(2)}, u32[]{:S(2)}) collective-permute-start(bf16[1024,2048]{1,0:T(8,128)(2,1)S(1)} %copy-done), channel_id=1, source_target_pairs={{0,3},{1,0},{2,1},{3,2},{4,5},{5,6},{6,7},{7,4},{8,11},{9,8},{10,9... | collective-permute-start | bytes 12582920 | tf_op jit(solution)/shard_map/ppermute | solution.py:43
  68.2 26.0 %collective-permute-start.9 = (bf16[1024,1024]{1,0:T(8,128)(2,1)S(1)}, bf16[1024,1024]{1,0:T(8,128)(2,1)S(1)}, u32[]{:S(2)}, u32[]{:S(2)}) collective-permute-start(bf16[1024,1024]{1,0:T(8,128)(2,1)S(1)} %pad_maximum_fusion.refs_3_.refs_0_), channel_id=1, source_target_pairs={{0,96},{4,36},{8,104},{12,44},{16,112},{20,52},{24,120},{28,60},{3... | collective-permute-start | bytes 6291464 | tf_op jit(solution)/shard_map/ppermute | solution.py:43
  69.2 25.0 %collective-permute-start.6 = (bf16[1024,1024]{1,0:T(8,128)(2,1)S(1)}, bf16[1024,1024]{1,0:T(8,128)(2,1)S(1)}, u32[]{:S(2)}, u32[]{:S(2)}) collective-permute-start(bf16[1024,1024]{1,0:T(8,128)(2,1)S(1)} %pad_maximum_fusion.refs_3_.refs_0_), channel_id=1, source_target_pairs={{0,4},{4,0},{8,12},{12,8},{16,20},{20,16},{24,28},{28,24},{32,36},... | collective-permute-start | bytes 6291464 | tf_op jit(solution)/shard_map/ppermute | solution.py:43
  71.5 78.9 %copy-start.8 = (bf16[384,2048]{1,0:T(8,128)(2,1)}, bf16[384,2048]{1,0:T(8,128)(2,1)S(1)}, u32[]{:S(2)}) copy-start(bf16[384,2048]{1,0:T(8,128)(2,1)S(1)} %collective-permute-done.1.refs_1_) | copy-start | bytes 4718596
  71.5 49.4 %collective-permute-start.16 = (bf16[1024,1024]{1,0:T(8,128)(2,1)}, bf16[1024,1024]{1,0:T(8,128)(2,1)}, u32[]{:S(2)}, u32[]{:S(2)}) collective-permute-start(bf16[1024,1024]{1,0:T(8,128)(2,1)} %pad_maximum_fusion.1.refs_4_.refs_8_), channel_id=1, source_target_pairs={{0,8},{4,28},{8,16},{12,4},{16,24},{20,12},{24,0},{28,20},{32,40},... | collective-permute-start | bytes 6291464 | tf_op jit(solution)/shard_map/ppermute | solution.py:43
  74.4 48.5 %copy-start.2 = (bf16[1024,1024]{1,0:T(8,128)(2,1)}, bf16[1024,1024]{1,0:T(8,128)(2,1)S(1)}, u32[]{:S(2)}) copy-start(bf16[1024,1024]{1,0:T(8,128)(2,1)S(1)} %collective-permute-done.7.refs_5_.refs_2_) | copy-start | bytes 6291460
  74.4 48.5 %collective-permute-start.18 = (bf16[1024,1024]{1,0:T(8,128)(2,1)}, bf16[1024,1024]{1,0:T(8,128)(2,1)}, u32[]{:S(2)}, u32[]{:S(2)}) collective-permute-start(bf16[1024,1024]{1,0:T(8,128)(2,1)} %pad_maximum_fusion.1.refs_4_.refs_8_), channel_id=1, source_target_pairs={{0,24},{4,12},{8,0},{12,20},{16,8},{20,28},{24,16},{28,4},{32,56},... | collective-permute-start | bytes 6291464 | tf_op jit(solution)/shard_map/ppermute | solution.py:43
  94.2 54.0 %copy-start.3 = (bf16[1024,1024]{1,0:T(8,128)(2,1)}, bf16[1024,1024]{1,0:T(8,128)(2,1)S(1)}, u32[]{:S(2)}) copy-start(bf16[1024,1024]{1,0:T(8,128)(2,1)S(1)} %collective-permute-done.9.refs_7_.refs_4_) | copy-start | bytes 6291460
  94.2 28.8 %collective-permute-start.8 = (bf16[1024,1024]{1,0:T(8,128)(2,1)S(1)}, bf16[1024,1024]{1,0:T(8,128)(2,1)S(1)}, u32[]{:S(2)}, u32[]{:S(2)}) collective-permute-start(bf16[1024,1024]{1,0:T(8,128)(2,1)S(1)} %collective-permute-done.7.refs_5_.refs_2_), channel_id=1, source_target_pairs={{0,4},{4,0},{8,12},{12,8},{16,20},{20,16},{24,28},{28,24},{32,36},... | collective-permute-start | bytes 6291464 | tf_op jit(solution)/shard_map/ppermute | solution.py:43
  94.2 54.0 %copy-start.4 = (bf16[1024,1024]{1,0:T(8,128)(2,1)}, bf16[1024,1024]{1,0:T(8,128)(2,1)S(1)}, u32[]{:S(2)}) copy-start(bf16[1024,1024]{1,0:T(8,128)(2,1)S(1)} %collective-permute-done.6.refs_4_.refs_1_) | copy-start | bytes 6291460
  94.3 29.2 %collective-permute-start.10 = (bf16[1024,1024]{1,0:T(8,128)(2,1)S(1)}, bf16[1024,1024]{1,0:T(8,128)(2,1)S(1)}, u32[]{:S(2)}, u32[]{:S(2)}) collective-permute-start(bf16[1024,1024]{1,0:T(8,128)(2,1)S(1)} %collective-permute-done.9.refs_7_.refs_4_), channel_id=1, source_target_pairs={{0,4},{4,0},{8,12},{12,8},{16,20},{20,16},{24,28},{28,24},{32,36},... | collective-permute-start | bytes 6291464 | tf_op jit(solution)/shard_map/ppermute | solution.py:43
  120.9 27.4 %collective-permute-start.20 = (bf16[1024,1024]{1,0:T(8,128)(2,1)S(1)}, bf16[1024,1024]{1,0:T(8,128)(2,1)}, u32[]{:S(2)}, u32[]{:S(2)}) collective-permute-start(bf16[1024,1024]{1,0:T(8,128)(2,1)S(1)} %collective-permute-done.7.refs_5_.refs_2_), channel_id=1, source_target_pairs={{0,32},{4,100},{8,40},{12,108},{16,48},{20,116},{24,56},{28,124},{... | collective-permute-start | bytes 6291464 | tf_op jit(solution)/shard_map/ppermute | solution.py:43
  122.9 27.6 %collective-permute-start.22 = (bf16[1024,1024]{1,0:T(8,128)(2,1)}, bf16[1024,1024]{1,0:T(8,128)(2,1)}, u32[]{:S(2)}, u32[]{:S(2)}) collective-permute-start(bf16[1024,1024]{1,0:T(8,128)(2,1)} %collective-permute-done.16.refs_6_.refs_10_), channel_id=1, source_target_pairs={{0,8},{4,28},{8,16},{12,4},{16,24},{20,12},{24,0},{28,20},{32,40},... | collective-permute-start | bytes 6291464 | tf_op jit(solution)/shard_map/ppermute | solution.py:43
  122.9 27.6 %copy-start.7 = (bf16[1024,2048]{1,0:T(8,128)(2,1)}, bf16[1024,2048]{1,0:T(8,128)(2,1)S(1)}, u32[]{:S(2)}) copy-start(bf16[1024,2048]{1,0:T(8,128)(2,1)S(1)} %collective-permute-done.2.refs_2_.refs_3_) | copy-start | bytes 12582916
  122.9 39.3 %collective-permute-start.15 = (bf16[1024,1024]{1,0:T(8,128)(2,1)}, bf16[1024,1024]{1,0:T(8,128)(2,1)}, u32[]{:S(2)}, u32[]{:S(2)}) collective-permute-start(bf16[1024,1024]{1,0:T(8,128)(2,1)} %pad_maximum_fusion.1.refs_4_.refs_8_), channel_id=1, source_target_pairs={{0,4},{4,0},{8,12},{12,8},{16,20},{20,16},{24,28},{28,24},{32,36},... | collective-permute-start | bytes 6291464 | tf_op jit(solution)/shard_map/ppermute | solution.py:43
  123.0 27.4 %copy-start.5 = (bf16[1024,1024]{1,0:T(8,128)(2,1)}, bf16[1024,1024]{1,0:T(8,128)(2,1)S(1)}, u32[]{:S(2)}) copy-start(bf16[1024,1024]{1,0:T(8,128)(2,1)S(1)} %collective-permute-done.8.refs_6_.refs_3_) | copy-start | bytes 6291460
  123.0 39.3 %collective-permute-start.17 = (bf16[1024,1024]{1,0:T(8,128)(2,1)}, bf16[1024,1024]{1,0:T(8,128)(2,1)}, u32[]{:S(2)}, u32[]{:S(2)}) collective-permute-start(bf16[1024,1024]{1,0:T(8,128)(2,1)} %collective-permute-done.16.refs_6_.refs_10_), channel_id=1, source_target_pairs={{0,4},{4,0},{8,12},{12,8},{16,20},{20,16},{24,28},{28,24},{32,36},... | collective-permute-start | bytes 6291464 | tf_op jit(solution)/shard_map/ppermute | solution.py:43
  123.5 27.0 %copy-start.6 = (bf16[1024,1024]{1,0:T(8,128)(2,1)}, bf16[1024,1024]{1,0:T(8,128)(2,1)S(1)}, u32[]{:S(2)}) copy-start(bf16[1024,1024]{1,0:T(8,128)(2,1)S(1)} %collective-permute-done.10.refs_8_.refs_5_) | copy-start | bytes 6291460
  123.5 39.1 %collective-permute-start.19 = (bf16[1024,1024]{1,0:T(8,128)(2,1)}, bf16[1024,1024]{1,0:T(8,128)(2,1)}, u32[]{:S(2)}, u32[]{:S(2)}) collective-permute-start(bf16[1024,1024]{1,0:T(8,128)(2,1)} %collective-permute-done.18.refs_8_.refs_12_), channel_id=1, source_target_pairs={{0,4},{4,0},{8,12},{12,8},{16,20},{20,16},{24,28},{28,24},{32,36},... | collective-permute-start | bytes 6291464 | tf_op jit(solution)/shard_map/ppermute | solution.py:43
  148.3 34.9 %collective-permute-start.21 = (bf16[1024,1024]{1,0:T(8,128)(2,1)}, bf16[1024,1024]{1,0:T(8,128)(2,1)}, u32[]{:S(2)}, u32[]{:S(2)}) collective-permute-start(bf16[1024,1024]{1,0:T(8,128)(2,1)} %collective-permute-done.20.refs_6_), channel_id=1, source_target_pairs={{0,4},{4,0},{8,12},{12,8},{16,20},{20,16},{24,28},{28,24},{32,36},... | collective-permute-start | bytes 6291464 | tf_op jit(solution)/shard_map/ppermute | solution.py:43
  150.4 32.7 %collective-permute-start.23 = (bf16[1024,1024]{1,0:T(8,128)(2,1)}, bf16[1024,1024]{1,0:T(8,128)(2,1)}, u32[]{:S(2)}, u32[]{:S(2)}) collective-permute-start(bf16[1024,1024]{1,0:T(8,128)(2,1)} %collective-permute-done.22.refs_14_), channel_id=1, source_target_pairs={{0,4},{4,0},{8,12},{12,8},{16,20},{20,16},{24,28},{28,24},{32,36},... | collective-permute-start | bytes 6291464 | tf_op jit(solution)/shard_map/ppermute | solution.py:43
  150.6 12.0 %copy-start.9 = (bf16[384,2048]{1,0:T(8,128)(2,1)S(1)}, bf16[384,2048]{1,0:T(8,128)(2,1)}, u32[]{:S(2)}) copy-start(bf16[384,2048]{1,0:T(8,128)(2,1)} %copy-done.8) | copy-start | bytes 4718596
  162.2 59.2 %collective-permute-start.26 = (bf16[256,2048]{1,0:T(8,128)(2,1)}, bf16[256,2048]{1,0:T(8,128)(2,1)S(1)}, u32[]{:S(2)}, u32[]{:S(2)}) collective-permute-start(bf16[256,2048]{1,0:T(8,128)(2,1)} %collective-permute-done.11.refs_2_), channel_id=1, source_target_pairs={{0,1},{1,2},{2,3},{3,0},{4,7},{5,4},{6,5},{7,6},{8,9},{9,10},{10,1... | collective-permute-start | bytes 3145736 | tf_op jit(solution)/shard_map/ppermute | solution.py:43
  162.3 33.0 %collective-permute-start.24 = (bf16[384,2048]{1,0:T(8,128)(2,1)}, bf16[384,2048]{1,0:T(8,128)(2,1)S(1)}, u32[]{:S(2)}, u32[]{:S(2)}) collective-permute-start(bf16[384,2048]{1,0:T(8,128)(2,1)} %collective-permute-done.refs_0_), channel_id=1, source_target_pairs={{0,1},{1,2},{2,3},{3,0},{4,7},{5,4},{6,5},{7,6},{8,9},{9,10},{10,1... | collective-permute-start | bytes 4718600 | tf_op jit(solution)/shard_map/ppermute | solution.py:43
  162.6 49.6 %collective-permute-start.25 = (bf16[384,2048]{1,0:T(8,128)(2,1)S(1)}, bf16[384,2048]{1,0:T(8,128)(2,1)S(1)}, u32[]{:S(2)}, u32[]{:S(2)}) collective-permute-start(bf16[384,2048]{1,0:T(8,128)(2,1)S(1)} %copy-done.9), channel_id=1, source_target_pairs={{0,1},{1,2},{2,3},{3,0},{4,7},{5,4},{6,5},{7,6},{8,9},{9,10},{10,1... | collective-permute-start | bytes 4718600 | tf_op jit(solution)/shard_map/ppermute | solution.py:43
  224.0 5.2 %collective-permute-start.27 = (f32[8,1024]{1,0:T(8,128)S(1)}, f32[8,1024]{1,0:T(8,128)S(1)}, u32[]{:S(2)}, u32[]{:S(2)}) collective-permute-start(f32[8,1024]{1,0:T(8,128)S(1)} %get-tuple-element.30.refs_0_), channel_id=1, source_target_pairs={{0,1},{1,2},{2,3},{3,0},{4,7},{5,4},{6,5},{7,6},{8,9},{9,10},{10,1... | collective-permute-start | bytes 98312 | tf_op jit(solution)/shard_map/ppermute | solution.py:43
  224.1 5.1 %collective-permute-start.28 = (f32[8,1024]{1,0:T(8,128)S(1)}, f32[8,1024]{1,0:T(8,128)S(1)}, u32[]{:S(2)}, u32[]{:S(2)}) collective-permute-start(f32[8,1024]{1,0:T(8,128)S(1)} %get-tuple-element.30.refs_0_), channel_id=1, source_target_pairs={{0,3},{1,0},{2,1},{3,2},{4,5},{5,6},{6,7},{7,4},{8,11},{9,8},{10,9... | collective-permute-start | bytes 98312 | tf_op jit(solution)/shard_map/ppermute | solution.py:43
  227.3 5.4 %collective-permute-start.29 = (f32[8,1024]{1,0:T(8,128)S(1)}, f32[8,1024]{1,0:T(8,128)S(1)}, u32[]{:S(2)}, u32[]{:S(2)}) collective-permute-start(f32[8,1024]{1,0:T(8,128)S(1)} %get-tuple-element.30.refs_0_), channel_id=1, source_target_pairs={{0,2},{1,3},{2,0},{3,1},{4,6},{5,7},{6,4},{7,5},{8,10},{9,11},{10,... | collective-permute-start | bytes 98312 | tf_op jit(solution)/shard_map/ppermute | solution.py:53

commit v4 on v3

--- a/solution.py
+++ b/solution.py
@@ -170,15 +170,15 @@
         fetch(0, p)
     for s in range(half // nt):
         for p in range(2):
-            if (s + 1) * nt < half:
-                fetch(s + 1, p)
-        for p in range(2):
             if s == 0:
                 landed(a_v.at[pl.ds(0, low), pl.ds(0, 4 * seg)], a_sem.at[p])
             landed(t_v.at[s % 2, pl.ds(0, 4 * seg), :], t_sem.at[s % 2, p])
             if s == 0:
                 one, three = p * seg, (2 + 3 * p) * seg
                 multiply(a_v, t_v.at[0], acc, 0, ((one, one, seg), (three, three, 3 * seg)), p > 0, 0, low)
+            if p == 0 and (s + 1) * nt < half:
+                fetch(s + 1, 0)
+                fetch(s + 1, 1)
         if s > 0:
             multiply(a_v, t_v.at[s % 2], acc, s * nt, ((0, 0, 8 * seg),), False, 0, low)
 
@@ -261,13 +261,14 @@
     landed(far_v, f_sem)
 
 
-def far_multiply(low, mt, a_v, tile, acc, p_v, s):
-    rows, nt = a_v.shape[0], tile.shape[1]
-
-    @pl.loop(0, rows // mt)
+def far_multiply(low, first, count, a_v, tile, acc, p_v, s):
+    nt = tile.shape[1]
+    mt = max(m for m in (384, 256) if count % m == 0)
+
+    @pl.loop(0, count // mt)
     def _(t):
-        at = pl.ds(pl.multiple_of(t * mt, mt), mt)
-        to, cols = pl.ds(pl.multiple_of(low + t * mt, 128), mt), pl.ds(s * nt, nt)
+        at = pl.ds(pl.multiple_of(first + t * mt, 128), mt)
+        to, cols = pl.ds(pl.multiple_of(low + first + t * mt, 128), mt), pl.ds(s * nt, nt)
         r = acc[to, cols] + jnp.dot(a_v[at, :], tile[...], preferred_element_type=jnp.float32)
         acc[to, cols] = r
         lanes = r[:, 0:128] * r[:, 0:128]
@@ -279,15 +280,16 @@
 def far_kernel(low, before, t_in, *refs):
     acc, t_v, power, a_v, p_v, a_sem = refs[-6:]
     chunks = refs[:-6] if low == 0 else refs[1:-6]
-    at = 0
-    for chunk in chunks:
-        pltpu.make_async_copy(chunk, a_v.at[pl.ds(at, chunk.shape[0]), :], a_sem).start()
-        at += chunk.shape[0]
+    sizes = [chunk.shape[0] for chunk in chunks]
+    for i, chunk in enumerate(chunks):
+        pltpu.make_async_copy(chunk, a_v.at[pl.ds(sum(sizes[:i]), sizes[i]), :], a_sem.at[i]).start()
     if low > 0:
         power[:, 0:low] = refs[0][...]
-    landed(a_v, a_sem)
-    for s in range(t_v.shape[0]):
-        far_multiply(low, min(256, a_v.shape[0]), a_v, t_in.at[s], acc, p_v, s)
+    for i, size in enumerate(sizes):
+        landed(a_v.at[pl.ds(sum(sizes[:i]), size), :], a_sem.at[i])
+        far_multiply(low, sum(sizes[:i]), size, a_v, t_in.at[0], acc, p_v, 0)
+    for s in range(1, t_v.shape[0]):
+        far_multiply(low, 0, sum(sizes), a_v, t_in.at[s], acc, p_v, s)
     for m in range(0, p_v.shape[0], 128):
         power[:, low + m:low + m + 128] = (
             jnp.sum(p_v[m:m + 128, :].T, axis=0, keepdims=True) + jnp.zeros((8, 128), jnp.float32))
@@ -368,7 +370,8 @@
     out = pltpu.VMEM(acc.shape, acc.dtype), pltpu.VMEM(tile.shape, tile.dtype), jax.ShapeDtypeStruct((8, low + rows), jnp.float32)
     return call(
         functools.partial(far_kernel, low), out, [VMEM, VMEM] + [VMEM] * len(powers) + [ANY] * len(chunks), (VMEM, VMEM, VMEM),
-        [pltpu.VMEM((rows, depth), chunks[0].dtype), pltpu.VMEM((rows, 128), jnp.float32), pltpu.SemaphoreType.DMA],
+        [pltpu.VMEM((rows, depth), chunks[0].dtype), pltpu.VMEM((rows, 128), jnp.float32),
+         pltpu.SemaphoreType.DMA((len(chunks),))],
         2 * rows * depth * acc.shape[1], FAR_MIB, {0: 0, 1: 1},
     )(kept(acc), kept(tile), *powers, *chunks)
 

time: 237 us -> 235 us (level)
  no operation moved by 1% of the time
where the time goes in v4:
time: 235 us
  waiting for transfers between devices  141 us (60%)
  Pallas kernels  55.8 us (24%)
  starting transfers between devices  32.4 us (14%)
  local copies, waits for them, and re-layouts  3.69 us (2%)
    ppermute x29, waiting for transfers between devices, move(): return lax.ppermute(value, name, along(axis, first))  138 us
    ppermute x29, starting transfers between devices, move(): return lax.ppermute(value, name, along(axis, first))  32.4 us
    pallas_call x1, Pallas kernels, near(): call(functools.partial(right_kernel, low), both, [SMEM, VMEM, VMEM] + [AN...  13.4 us
    pallas_call x1, Pallas kernels, near(): call(rest_kernel, (total, pltpu.VMEM((parts, depth, NT), left.dtype)), [S...  11.7 us
    pallas_call x2, Pallas kernels, far(): call(functools.partial(far_kernel, low), out, [VMEM, VMEM] + [VMEM] * len...  11.1 us
    pallas_call x1, Pallas kernels, near(): call(functools.partial(left_kernel, low), both, [SMEM] + [ANY] * 10, (VME...  11 us
    pallas_call x1, Pallas kernels, near(): call(functools.partial(tail_kernel, low), both, [SMEM, VMEM, VMEM] + [ANY...  4.89 us
  transfers between devices with their start and end apart: 30, of which 13 were waited for; matrix products, arithmetic and copies ran while one was open for 2% of the time, Pallas kernels for 21%

profile of v4, /device:TPU:0, one launch (start us, length us, event | category | flops | bytes accessed | tf_op | source)
XLA Modules:
  0.0 235.3 jit_solution(863753794084514468)
XLA Ops:
  0.0 1.3 fusion.1
  1.3 1.7 collective-permute-start.3
  3.0 1.6 collective-permute-start.4
  4.6 11.3 %collective-permute-done.3 = bf16[256,1024]{1,0:T(8,128)(2,1)S(1)} collective-permute-done((bf16[256,1024]{1,0:T(8,128)(2,1)S(1)}, bf16[256,1024]{1,0:T(8,128)(2,1)S(1)}, u32[]{:S(2)}, u32[]{:S(2)}) %collective-permute-start.3) | collective-permute-done | bytes 524320 | tf_op jit(solution)/shard_map/ppermute | solution.py:43
  15.9 1.7 collective-permute-start.5
  17.6 2.3 fusion
  19.9 2.0 collective-permute-start
  21.9 1.6 collective-permute-start.12
  23.5 1.7 collective-permute-start.13
  25.1 0.1 slice.18
  25.3 2.0 collective-permute-start.11
  27.2 0.2 pad_maximum_fusion.refs_3_.refs_0_
  27.4 0.9 collective-permute-start.7
  28.4 6.2 %collective-permute-done.12 = bf16[256,1024]{1,0:T(8,128)(2,1)S(1)} collective-permute-done((bf16[256,1024]{1,0:T(8,128)(2,1)S(1)}, bf16[256,1024]{1,0:T(8,128)(2,1)S(1)}, u32[]{:S(2)}, u32[]{:S(2)}) %collective-permute-start.12) | collective-permute-done | bytes 524320 | tf_op jit(solution)/shard_map/ppermute | solution.py:43
  34.6 2.0 collective-permute-start.14
  36.6 1.6 collective-permute-done.13
  38.3 1.8 collective-permute-start.1
  40.0 25.9 %collective-permute-done.14 = bf16[256,1024]{1,0:T(8,128)(2,1)S(1)} collective-permute-done((bf16[256,1024]{1,0:T(8,128)(2,1)S(1)}, bf16[256,1024]{1,0:T(8,128)(2,1)S(1)}, u32[]{:S(2)}, u32[]{:S(2)}) %collective-permute-start.14) | collective-permute-done | bytes 524320 | tf_op jit(solution)/shard_map/ppermute | solution.py:43
  66.0 2.2 collective-permute-start.2
  68.2 1.0 collective-permute-start.9
  69.2 1.5 pad_maximum_fusion.1.refs_4_.refs_8_
  70.8 0.8 collective-permute-done.1.refs_1_
  71.5 2.8 %collective-permute-start.16 = (bf16[1024,1024]{1,0:T(8,128)(2,1)}, bf16[1024,1024]{1,0:T(8,128)(2,1)}, u32[]{:S(2)}, u32[]{:S(2)}) collective-permute-start(bf16[1024,1024]{1,0:T(8,128)(2,1)} %pad_maximum_fusion.1.refs_4_.refs_8_), channel_id=1, source_target_pairs={{0,8},{4,28},{8,16},{12,4},{16,24},{20,12},{24,0},{28,20},{32,40},... | collective-permute-start | bytes 6291464 | tf_op jit(solution)/shard_map/ppermute | solution.py:43
  74.4 0.4 collective-permute-start.18
  74.8 19.5 %collective-permute-done.9.refs_7_.refs_4_ = bf16[1024,1024]{1,0:T(8,128)(2,1)S(1)} collective-permute-done((bf16[1024,1024]{1,0:T(8,128)(2,1)S(1)}, bf16[1024,1024]{1,0:T(8,128)(2,1)S(1)}, u32[]{:S(2)}, u32[]{:S(2)}) %collective-permute-start.9) | collective-permute-done | bytes 2097184 | tf_op jit(solution)/shard_map/ppermute | solution.py:43
  94.3 0.5 collective-permute-start.10
  94.8 26.2 %collective-permute-done.16.refs_6_.refs_10_ = bf16[1024,1024]{1,0:T(8,128)(2,1)} collective-permute-done((bf16[1024,1024]{1,0:T(8,128)(2,1)}, bf16[1024,1024]{1,0:T(8,128)(2,1)}, u32[]{:S(2)}, u32[]{:S(2)}) %collective-permute-start.16) | collective-permute-done | bytes 2097184 | tf_op jit(solution)/shard_map/ppermute | solution.py:43
  120.9 1.9 collective-permute-start.20
  122.9 0.1 collective-permute-start.15
  123.0 0.5 collective-permute-start.17
  123.5 0.1 collective-permute-start.19
  123.6 24.7 %collective-permute-done.20.refs_6_ = bf16[1024,1024]{1,0:T(8,128)(2,1)} collective-permute-done((bf16[1024,1024]{1,0:T(8,128)(2,1)S(1)}, bf16[1024,1024]{1,0:T(8,128)(2,1)}, u32[]{:S(2)}, u32[]{:S(2)}) %collective-permute-start.20) | collective-permute-done | bytes 2097184 | tf_op jit(solution)/shard_map/ppermute | solution.py:43
  148.3 2.1 collective-permute-done.22.refs_14_
  150.5 0.1 pad_add_fusion.pos
  150.6 11.0 %shard_map.28 = (f32[1024,2048]{1,0:T(8,128)S(1)}, bf16[1024,6144]{1,0:T(8,128)(2,1)S(1)}) custom-call(s32[4]{0:T(128)S(1)} %pad_add_fusion.pos, bf16[1024,2048]{1,0:T(8,128)(2,1)} %left.3, bf16[384,2048]{1,0:T(8,128)(2,1)} %collective-permute-done.refs_0_, bf16[384,2048]{1,0:T(8,128)(2,1)} %copy-done.8, bf16[1024,2048]{1,0:T(8,128)(2,1)} %copy-done.7, ...), custom_call_target="tpu_custom_call" | custom-call | flops 6442450944 | bytes 16777216 | tf_op jit(solution)/shard_map/pallas_call | solution.py:347
  161.7 0.3 collective-permute-start.24
  162.0 2.2 collective-permute-start.25
  164.3 13.4 %shard_map.29 = (f32[1024,2048]{1,0:T(8,128)S(1)}, bf16[1024,6144]{1,0:T(8,128)(2,1)S(1)}) custom-call(s32[4]{0:T(128)S(1)} %pad_add_fusion.pos, bf16[1024,6144]{1,0:T(8,128)(2,1)S(1)} %get-tuple-element.18.a_in, f32[1024,2048]{1,0:T(8,128)S(1)} %get-tuple-element.19.before, bf16[1024,2048]{1,0:T(8,128)(2,1)} %left.3, ...), custom_call_target="tpu_custom_call", output_to_operand_aliasing={{1}: (1, {}), {0}: (2, {})} | custom-call | flops 9663676416 | bytes 16777216 | tf_op jit(solution)/shard_map/pallas_call | solution.py:351
  177.7 4.9 %shard_map.30 = (f32[1024,2048]{1,0:T(8,128)S(1)}, bf16[1024,6144]{1,0:T(8,128)(2,1)S(1)}) custom-call(s32[4]{0:T(128)S(1)} %pad_add_fusion.pos, bf16[1024,6144]{1,0:T(8,128)(2,1)S(1)} %get-tuple-element.20.a_in, f32[1024,2048]{1,0:T(8,128)S(1)} %get-tuple-element.21.before, ...), custom_call_target="tpu_custom_call", output_to_operand_aliasing={{1}: (1, {}), {0}: (2, {})} | custom-call | flops 2147483648 | bytes 16777216 | tf_op jit(solution)/shard_map/pallas_call | solution.py:355
  182.6 11.7 %shard_map.31 = (f32[1024,2048]{1,0:T(8,128)S(1)}, bf16[4,2048,512]{2,1,0:T(8,128)(2,1)S(1)}) custom-call(s32[4]{0:T(128)S(1)} %pad_add_fusion.pos, bf16[1024,6144]{1,0:T(8,128)(2,1)S(1)} %get-tuple-element.22.a_v, f32[1024,2048]{1,0:T(8,128)S(1)} %get-tuple-element.23.before, bf16[1024,1024]{1,0:T(8,128)(2,1)} %copy-done.1, ...), custom_call_target="tpu_custom_call", output_to_operand_aliasing={{0}: (2, {})} | custom-call | flops 7516192768 | bytes 16777216 | tf_op jit(solution)/shard_map/pallas_call | solution.py:360
  194.3 0.5 collective-permute-done.24.refs_0_
  194.8 16.9 %collective-permute-done.25.refs_1_ = bf16[384,2048]{1,0:T(8,128)(2,1)S(1)} collective-permute-done((bf16[384,2048]{1,0:T(8,128)(2,1)S(1)}, bf16[384,2048]{1,0:T(8,128)(2,1)S(1)}, u32[]{:S(2)}, u32[]{:S(2)}) %collective-permute-start.25) | collective-permute-done | bytes 1572896 | tf_op jit(solution)/shard_map/ppermute | solution.py:43
  211.6 8.5 %shard_map.32 = (f32[1024,2048]{1,0:T(8,128)S(1)}, bf16[4,2048,512]{2,1,0:T(8,128)(2,1)S(1)}, f32[8,768]{1,0:T(8,128)S(1)}) custom-call(f32[1024,2048]{1,0:T(8,128)S(1)} %get-tuple-element.24.before, bf16[4,2048,512]{2,1,0:T(8,128)(2,1)S(1)} %get-tuple-element.25.t_in, ...), custom_call_target="tpu_custom_call", output_to_operand_aliasing={{0}: (0, {}), {1}: (1, {})} | custom-call | flops 6442450944 | bytes 16777216 | tf_op jit(solution)/shard_map/pallas_call | solution.py:371
  220.2 2.6 %shard_map.33 = (f32[1024,2048]{1,0:T(8,128)S(1)}, bf16[4,2048,512]{2,1,0:T(8,128)(2,1)S(1)}, f32[8,1024]{1,0:T(8,128)S(1)}) custom-call(f32[1024,2048]{1,0:T(8,128)S(1)} %get-tuple-element.26.before, bf16[4,2048,512]{2,1,0:T(8,128)(2,1)S(1)} %get-tuple-element.27.t_in, ...), custom_call_target="tpu_custom_call", output_to_operand_aliasing={{0}: (0, {}), {1}: (1, {})} | custom-call | flops 2147483648 | bytes 16777216 | tf_op jit(solution)/shard_map/pallas_call | solution.py:371
  222.8 3.2 %collective-permute-start.28 = (f32[8,1024]{1,0:T(8,128)S(1)}, f32[8,1024]{1,0:T(8,128)S(1)}, u32[]{:S(2)}, u32[]{:S(2)}) collective-permute-start(f32[8,1024]{1,0:T(8,128)S(1)} %get-tuple-element.30.refs_0_), channel_id=1, source_target_pairs={{0,3},{1,0},{2,1},{3,2},{4,5},{5,6},{6,7},{7,4},{8,11},{9,8},{10,9... | collective-permute-start | bytes 98312 | tf_op jit(solution)/shard_map/ppermute | solution.py:43
  226.1 1.9 collective-permute-done.27.refs_1_
  227.9 3.5 %collective-permute-done.29.refs_3_ = f32[8,1024]{1,0:T(8,128)S(1)} collective-permute-done((f32[8,1024]{1,0:T(8,128)S(1)}, f32[8,1024]{1,0:T(8,128)S(1)}, u32[]{:S(2)}, u32[]{:S(2)}) %collective-permute-start.29) | collective-permute-done | bytes 32800 | tf_op jit(solution)/shard_map/ppermute | solution.py:53
  231.5 3.7 %shard_map.34 = f32[1024,2048]{1,0:T(8,128)} custom-call(f32[1024,2048]{1,0:T(8,128)S(1)} %get-tuple-element.29.acc, f32[8,1024]{1,0:T(8,128)S(1)} %get-tuple-element.30.refs_0_, f32[8,1024]{1,0:T(8,128)S(1)} %collective-permute-done.27.refs_1_, f32[8,1024]{1,0:T(8,128)S(1)} %collective-permute-done.28.refs_2_, f32[8,1024]{1,0:T(8,128)S(1)} %collective-permute-done.29.refs_3_), custom_call_target="tpu_custom_call" | custom-call | flops 62914560 | bytes 16777216 | tf_op jit(solution)/shard_map/pallas_call | solution.py:381
  (45 shorter events, 0.3 us)
Async XLA Ops:
  1.3 23.9 %copy-start = (bf16[1024,2048]{1,0:T(8,128)(2,1)S(1)}, bf16[1024,2048]{1,0:T(8,128)(2,1)}, u32[]{:S(2)}) copy-start(bf16[1024,2048]{1,0:T(8,128)(2,1)} %left.3) | copy-start | bytes 12582916
  1.3 14.6 %collective-permute-start.3 = (bf16[256,1024]{1,0:T(8,128)(2,1)S(1)}, bf16[256,1024]{1,0:T(8,128)(2,1)S(1)}, u32[]{:S(2)}, u32[]{:S(2)}) collective-permute-start(bf16[256,1024]{1,0:T(8,128)(2,1)S(1)} %get-tuple-element.34), channel_id=1, source_target_pairs={{0,8},{4,28},{8,16},{12,4},{16,24},{20,12},{24,0},{28,20},{32,40},... | collective-permute-start | bytes 1572872 | tf_op jit(solution)/shard_map/ppermute | solution.py:43
  3.0 22.3 %collective-permute-start.4 = (bf16[256,1024]{1,0:T(8,128)(2,1)S(1)}, bf16[256,1024]{1,0:T(8,128)(2,1)S(1)}, u32[]{:S(2)}, u32[]{:S(2)}) collective-permute-start(bf16[256,1024]{1,0:T(8,128)(2,1)S(1)} %get-tuple-element.34), channel_id=1, source_target_pairs={{0,24},{4,12},{8,0},{12,20},{16,8},{20,28},{24,16},{28,4},{32,56},... | collective-permute-start | bytes 1572872 | tf_op jit(solution)/shard_map/ppermute | solution.py:43
  15.9 11.3 %collective-permute-start.5 = (bf16[256,1024]{1,0:T(8,128)(2,1)S(1)}, bf16[256,1024]{1,0:T(8,128)(2,1)S(1)}, u32[]{:S(2)}, u32[]{:S(2)}) collective-permute-start(bf16[256,1024]{1,0:T(8,128)(2,1)S(1)} %collective-permute-done.3), channel_id=1, source_target_pairs={{0,8},{4,28},{8,16},{12,4},{16,24},{20,12},{24,0},{28,20},{32,40},... | collective-permute-start | bytes 1572872 | tf_op jit(solution)/shard_map/ppermute | solution.py:43
  19.9 49.3 %collective-permute-start = (bf16[384,2048]{1,0:T(8,128)(2,1)S(1)}, bf16[384,2048]{1,0:T(8,128)(2,1)}, u32[]{:S(2)}, u32[]{:S(2)}) collective-permute-start(bf16[384,2048]{1,0:T(8,128)(2,1)S(1)} %get-tuple-element.32), channel_id=1, source_target_pairs={{0,1},{1,2},{2,3},{3,0},{4,7},{5,4},{6,5},{7,6},{8,9},{9,10},{10,1... | collective-permute-start | bytes 4718600 | tf_op jit(solution)/shard_map/ppermute | solution.py:43
  21.9 12.7 %collective-permute-start.12 = (bf16[256,1024]{1,0:T(8,128)(2,1)S(1)}, bf16[256,1024]{1,0:T(8,128)(2,1)S(1)}, u32[]{:S(2)}, u32[]{:S(2)}) collective-permute-start(bf16[256,1024]{1,0:T(8,128)(2,1)S(1)} %get-tuple-element.33), channel_id=1, source_target_pairs={{0,32},{4,100},{8,40},{12,108},{16,48},{20,116},{24,56},{28,124},{... | collective-permute-start | bytes 1572872 | tf_op jit(solution)/shard_map/ppermute | solution.py:43
  23.5 14.8 %collective-permute-start.13 = (bf16[256,1024]{1,0:T(8,128)(2,1)S(1)}, bf16[256,1024]{1,0:T(8,128)(2,1)S(1)}, u32[]{:S(2)}, u32[]{:S(2)}) collective-permute-start(bf16[256,1024]{1,0:T(8,128)(2,1)S(1)} %get-tuple-element.33), channel_id=1, source_target_pairs={{0,96},{4,36},{8,104},{12,44},{16,112},{20,52},{24,120},{28,60},{3... | collective-permute-start | bytes 1572872 | tf_op jit(solution)/shard_map/ppermute | solution.py:43
  25.3 42.9 %collective-permute-start.11 = (bf16[256,2048]{1,0:T(8,128)(2,1)S(1)}, bf16[256,2048]{1,0:T(8,128)(2,1)}, u32[]{:S(2)}, u32[]{:S(2)}) collective-permute-start(bf16[256,2048]{1,0:T(8,128)(2,1)S(1)} %slice.18), channel_id=1, source_target_pairs={{0,1},{1,2},{2,3},{3,0},{4,7},{5,4},{6,5},{7,6},{8,9},{9,10},{10,1... | collective-permute-start | bytes 3145736 | tf_op jit(solution)/shard_map/ppermute | solution.py:43
  27.4 43.3 %copy-start.1 = (bf16[1024,1024]{1,0:T(8,128)(2,1)}, bf16[1024,1024]{1,0:T(8,128)(2,1)S(1)}, u32[]{:S(2)}) copy-start(bf16[1024,1024]{1,0:T(8,128)(2,1)S(1)} %pad_maximum_fusion.refs_3_.refs_0_) | copy-start | bytes 6291460
  27.4 46.9 %collective-permute-start.7 = (bf16[1024,1024]{1,0:T(8,128)(2,1)S(1)}, bf16[1024,1024]{1,0:T(8,128)(2,1)S(1)}, u32[]{:S(2)}, u32[]{:S(2)}) collective-permute-start(bf16[1024,1024]{1,0:T(8,128)(2,1)S(1)} %pad_maximum_fusion.refs_3_.refs_0_), channel_id=1, source_target_pairs={{0,32},{4,100},{8,40},{12,108},{16,48},{20,116},{24,56},{28,124},{... | collective-permute-start | bytes 6291464 | tf_op jit(solution)/shard_map/ppermute | solution.py:43
  34.6 31.4 %collective-permute-start.14 = (bf16[256,1024]{1,0:T(8,128)(2,1)S(1)}, bf16[256,1024]{1,0:T(8,128)(2,1)S(1)}, u32[]{:S(2)}, u32[]{:S(2)}) collective-permute-start(bf16[256,1024]{1,0:T(8,128)(2,1)S(1)} %collective-permute-done.12), channel_id=1, source_target_pairs={{0,32},{4,100},{8,40},{12,108},{16,48},{20,116},{24,56},{28,124},{... | collective-permute-start | bytes 1572872 | tf_op jit(solution)/shard_map/ppermute | solution.py:43
  38.3 33.3 %collective-permute-start.1 = (bf16[384,2048]{1,0:T(8,128)(2,1)S(1)}, bf16[384,2048]{1,0:T(8,128)(2,1)S(1)}, u32[]{:S(2)}, u32[]{:S(2)}) collective-permute-start(bf16[384,2048]{1,0:T(8,128)(2,1)S(1)} %get-tuple-element.31), channel_id=1, source_target_pairs={{0,1},{1,2},{2,3},{3,0},{4,7},{5,4},{6,5},{7,6},{8,9},{9,10},{10,1... | collective-permute-start | bytes 4718600 | tf_op jit(solution)/shard_map/ppermute | solution.py:43
  66.0 56.9 %collective-permute-start.2 = (bf16[1024,2048]{1,0:T(8,128)(2,1)S(1)}, bf16[1024,2048]{1,0:T(8,128)(2,1)S(1)}, u32[]{:S(2)}, u32[]{:S(2)}) collective-permute-start(bf16[1024,2048]{1,0:T(8,128)(2,1)S(1)} %copy-done), channel_id=1, source_target_pairs={{0,3},{1,0},{2,1},{3,2},{4,5},{5,6},{6,7},{7,4},{8,11},{9,8},{10,9... | collective-permute-start | bytes 12582920 | tf_op jit(solution)/shard_map/ppermute | solution.py:43
  68.2 26.0 %collective-permute-start.9 = (bf16[1024,1024]{1,0:T(8,128)(2,1)S(1)}, bf16[1024,1024]{1,0:T(8,128)(2,1)S(1)}, u32[]{:S(2)}, u32[]{:S(2)}) collective-permute-start(bf16[1024,1024]{1,0:T(8,128)(2,1)S(1)} %pad_maximum_fusion.refs_3_.refs_0_), channel_id=1, source_target_pairs={{0,96},{4,36},{8,104},{12,44},{16,112},{20,52},{24,120},{28,60},{3... | collective-permute-start | bytes 6291464 | tf_op jit(solution)/shard_map/ppermute | solution.py:43
  69.2 25.0 %collective-permute-start.6 = (bf16[1024,1024]{1,0:T(8,128)(2,1)S(1)}, bf16[1024,1024]{1,0:T(8,128)(2,1)S(1)}, u32[]{:S(2)}, u32[]{:S(2)}) collective-permute-start(bf16[1024,1024]{1,0:T(8,128)(2,1)S(1)} %pad_maximum_fusion.refs_3_.refs_0_), channel_id=1, source_target_pairs={{0,4},{4,0},{8,12},{12,8},{16,20},{20,16},{24,28},{28,24},{32,36},... | collective-permute-start | bytes 6291464 | tf_op jit(solution)/shard_map/ppermute | solution.py:43
  71.5 78.9 %copy-start.8 = (bf16[384,2048]{1,0:T(8,128)(2,1)}, bf16[384,2048]{1,0:T(8,128)(2,1)S(1)}, u32[]{:S(2)}) copy-start(bf16[384,2048]{1,0:T(8,128)(2,1)S(1)} %collective-permute-done.1.refs_1_) | copy-start | bytes 4718596
  71.5 49.4 %collective-permute-start.16 = (bf16[1024,1024]{1,0:T(8,128)(2,1)}, bf16[1024,1024]{1,0:T(8,128)(2,1)}, u32[]{:S(2)}, u32[]{:S(2)}) collective-permute-start(bf16[1024,1024]{1,0:T(8,128)(2,1)} %pad_maximum_fusion.1.refs_4_.refs_8_), channel_id=1, source_target_pairs={{0,8},{4,28},{8,16},{12,4},{16,24},{20,12},{24,0},{28,20},{32,40},... | collective-permute-start | bytes 6291464 | tf_op jit(solution)/shard_map/ppermute | solution.py:43
  74.4 48.5 %copy-start.2 = (bf16[1024,1024]{1,0:T(8,128)(2,1)}, bf16[1024,1024]{1,0:T(8,128)(2,1)S(1)}, u32[]{:S(2)}) copy-start(bf16[1024,1024]{1,0:T(8,128)(2,1)S(1)} %collective-permute-done.7.refs_5_.refs_2_) | copy-start | bytes 6291460
  74.4 48.5 %collective-permute-start.18 = (bf16[1024,1024]{1,0:T(8,128)(2,1)}, bf16[1024,1024]{1,0:T(8,128)(2,1)}, u32[]{:S(2)}, u32[]{:S(2)}) collective-permute-start(bf16[1024,1024]{1,0:T(8,128)(2,1)} %pad_maximum_fusion.1.refs_4_.refs_8_), channel_id=1, source_target_pairs={{0,24},{4,12},{8,0},{12,20},{16,8},{20,28},{24,16},{28,4},{32,56},... | collective-permute-start | bytes 6291464 | tf_op jit(solution)/shard_map/ppermute | solution.py:43
  94.2 54.0 %copy-start.3 = (bf16[1024,1024]{1,0:T(8,128)(2,1)}, bf16[1024,1024]{1,0:T(8,128)(2,1)S(1)}, u32[]{:S(2)}) copy-start(bf16[1024,1024]{1,0:T(8,128)(2,1)S(1)} %collective-permute-done.9.refs_7_.refs_4_) | copy-start | bytes 6291460
  94.2 28.8 %collective-permute-start.8 = (bf16[1024,1024]{1,0:T(8,128)(2,1)S(1)}, bf16[1024,1024]{1,0:T(8,128)(2,1)S(1)}, u32[]{:S(2)}, u32[]{:S(2)}) collective-permute-start(bf16[1024,1024]{1,0:T(8,128)(2,1)S(1)} %collective-permute-done.7.refs_5_.refs_2_), channel_id=1, source_target_pairs={{0,4},{4,0},{8,12},{12,8},{16,20},{20,16},{24,28},{28,24},{32,36},... | collective-permute-start | bytes 6291464 | tf_op jit(solution)/shard_map/ppermute | solution.py:43
  94.2 54.0 %copy-start.4 = (bf16[1024,1024]{1,0:T(8,128)(2,1)}, bf16[1024,1024]{1,0:T(8,128)(2,1)S(1)}, u32[]{:S(2)}) copy-start(bf16[1024,1024]{1,0:T(8,128)(2,1)S(1)} %collective-permute-done.6.refs_4_.refs_1_) | copy-start | bytes 6291460
  94.3 29.2 %collective-permute-start.10 = (bf16[1024,1024]{1,0:T(8,128)(2,1)S(1)}, bf16[1024,1024]{1,0:T(8,128)(2,1)S(1)}, u32[]{:S(2)}, u32[]{:S(2)}) collective-permute-start(bf16[1024,1024]{1,0:T(8,128)(2,1)S(1)} %collective-permute-done.9.refs_7_.refs_4_), channel_id=1, source_target_pairs={{0,4},{4,0},{8,12},{12,8},{16,20},{20,16},{24,28},{28,24},{32,36},... | collective-permute-start | bytes 6291464 | tf_op jit(solution)/shard_map/ppermute | solution.py:43
  120.9 27.4 %collective-permute-start.20 = (bf16[1024,1024]{1,0:T(8,128)(2,1)S(1)}, bf16[1024,1024]{1,0:T(8,128)(2,1)}, u32[]{:S(2)}, u32[]{:S(2)}) collective-permute-start(bf16[1024,1024]{1,0:T(8,128)(2,1)S(1)} %collective-permute-done.7.refs_5_.refs_2_), channel_id=1, source_target_pairs={{0,32},{4,100},{8,40},{12,108},{16,48},{20,116},{24,56},{28,124},{... | collective-permute-start | bytes 6291464 | tf_op jit(solution)/shard_map/ppermute | solution.py:43
  122.9 27.6 %collective-permute-start.22 = (bf16[1024,1024]{1,0:T(8,128)(2,1)}, bf16[1024,1024]{1,0:T(8,128)(2,1)}, u32[]{:S(2)}, u32[]{:S(2)}) collective-permute-start(bf16[1024,1024]{1,0:T(8,128)(2,1)} %collective-permute-done.16.refs_6_.refs_10_), channel_id=1, source_target_pairs={{0,8},{4,28},{8,16},{12,4},{16,24},{20,12},{24,0},{28,20},{32,40},... | collective-permute-start | bytes 6291464 | tf_op jit(solution)/shard_map/ppermute | solution.py:43
  122.9 27.6 %copy-start.7 = (bf16[1024,2048]{1,0:T(8,128)(2,1)}, bf16[1024,2048]{1,0:T(8,128)(2,1)S(1)}, u32[]{:S(2)}) copy-start(bf16[1024,2048]{1,0:T(8,128)(2,1)S(1)} %collective-permute-done.2.refs_2_.refs_3_) | copy-start | bytes 12582916
  122.9 38.7 %collective-permute-start.15 = (bf16[1024,1024]{1,0:T(8,128)(2,1)}, bf16[1024,1024]{1,0:T(8,128)(2,1)}, u32[]{:S(2)}, u32[]{:S(2)}) collective-permute-start(bf16[1024,1024]{1,0:T(8,128)(2,1)} %pad_maximum_fusion.1.refs_4_.refs_8_), channel_id=1, source_target_pairs={{0,4},{4,0},{8,12},{12,8},{16,20},{20,16},{24,28},{28,24},{32,36},... | collective-permute-start | bytes 6291464 | tf_op jit(solution)/shard_map/ppermute | solution.py:43
  123.0 27.4 %copy-start.5 = (bf16[1024,1024]{1,0:T(8,128)(2,1)}, bf16[1024,1024]{1,0:T(8,128)(2,1)S(1)}, u32[]{:S(2)}) copy-start(bf16[1024,1024]{1,0:T(8,128)(2,1)S(1)} %collective-permute-done.8.refs_6_.refs_3_) | copy-start | bytes 6291460
  123.0 38.7 %collective-permute-start.17 = (bf16[1024,1024]{1,0:T(8,128)(2,1)}, bf16[1024,1024]{1,0:T(8,128)(2,1)}, u32[]{:S(2)}, u32[]{:S(2)}) collective-permute-start(bf16[1024,1024]{1,0:T(8,128)(2,1)} %collective-permute-done.16.refs_6_.refs_10_), channel_id=1, source_target_pairs={{0,4},{4,0},{8,12},{12,8},{16,20},{20,16},{24,28},{28,24},{32,36},... | collective-permute-start | bytes 6291464 | tf_op jit(solution)/shard_map/ppermute | solution.py:43
  123.5 27.0 %copy-start.6 = (bf16[1024,1024]{1,0:T(8,128)(2,1)}, bf16[1024,1024]{1,0:T(8,128)(2,1)S(1)}, u32[]{:S(2)}) copy-start(bf16[1024,1024]{1,0:T(8,128)(2,1)S(1)} %collective-permute-done.10.refs_8_.refs_5_) | copy-start | bytes 6291460
  123.5 38.5 %collective-permute-start.19 = (bf16[1024,1024]{1,0:T(8,128)(2,1)}, bf16[1024,1024]{1,0:T(8,128)(2,1)}, u32[]{:S(2)}, u32[]{:S(2)}) collective-permute-start(bf16[1024,1024]{1,0:T(8,128)(2,1)} %collective-permute-done.18.refs_8_.refs_12_), channel_id=1, source_target_pairs={{0,4},{4,0},{8,12},{12,8},{16,20},{20,16},{24,28},{28,24},{32,36},... | collective-permute-start | bytes 6291464 | tf_op jit(solution)/shard_map/ppermute | solution.py:43
  148.3 34.3 %collective-permute-start.21 = (bf16[1024,1024]{1,0:T(8,128)(2,1)}, bf16[1024,1024]{1,0:T(8,128)(2,1)}, u32[]{:S(2)}, u32[]{:S(2)}) collective-permute-start(bf16[1024,1024]{1,0:T(8,128)(2,1)} %collective-permute-done.20.refs_6_), channel_id=1, source_target_pairs={{0,4},{4,0},{8,12},{12,8},{16,20},{20,16},{24,28},{28,24},{32,36},... | collective-permute-start | bytes 6291464 | tf_op jit(solution)/shard_map/ppermute | solution.py:43
  150.4 32.1 %collective-permute-start.23 = (bf16[1024,1024]{1,0:T(8,128)(2,1)}, bf16[1024,1024]{1,0:T(8,128)(2,1)}, u32[]{:S(2)}, u32[]{:S(2)}) collective-permute-start(bf16[1024,1024]{1,0:T(8,128)(2,1)} %collective-permute-done.22.refs_14_), channel_id=1, source_target_pairs={{0,4},{4,0},{8,12},{12,8},{16,20},{20,16},{24,28},{28,24},{32,36},... | collective-permute-start | bytes 6291464 | tf_op jit(solution)/shard_map/ppermute | solution.py:43
  150.6 11.4 %copy-start.9 = (bf16[384,2048]{1,0:T(8,128)(2,1)S(1)}, bf16[384,2048]{1,0:T(8,128)(2,1)}, u32[]{:S(2)}) copy-start(bf16[384,2048]{1,0:T(8,128)(2,1)} %copy-done.8) | copy-start | bytes 4718596
  161.7 58.5 %collective-permute-start.26 = (bf16[256,2048]{1,0:T(8,128)(2,1)}, bf16[256,2048]{1,0:T(8,128)(2,1)S(1)}, u32[]{:S(2)}, u32[]{:S(2)}) collective-permute-start(bf16[256,2048]{1,0:T(8,128)(2,1)} %collective-permute-done.11.refs_2_), channel_id=1, source_target_pairs={{0,1},{1,2},{2,3},{3,0},{4,7},{5,4},{6,5},{7,6},{8,9},{9,10},{10,1... | collective-permute-start | bytes 3145736 | tf_op jit(solution)/shard_map/ppermute | solution.py:43
  161.7 33.0 %collective-permute-start.24 = (bf16[384,2048]{1,0:T(8,128)(2,1)}, bf16[384,2048]{1,0:T(8,128)(2,1)S(1)}, u32[]{:S(2)}, u32[]{:S(2)}) collective-permute-start(bf16[384,2048]{1,0:T(8,128)(2,1)} %collective-permute-done.refs_0_), channel_id=1, source_target_pairs={{0,1},{1,2},{2,3},{3,0},{4,7},{5,4},{6,5},{7,6},{8,9},{9,10},{10,1... | collective-permute-start | bytes 4718600 | tf_op jit(solution)/shard_map/ppermute | solution.py:43
  162.0 49.6 %collective-permute-start.25 = (bf16[384,2048]{1,0:T(8,128)(2,1)S(1)}, bf16[384,2048]{1,0:T(8,128)(2,1)S(1)}, u32[]{:S(2)}, u32[]{:S(2)}) collective-permute-start(bf16[384,2048]{1,0:T(8,128)(2,1)S(1)} %copy-done.9), channel_id=1, source_target_pairs={{0,1},{1,2},{2,3},{3,0},{4,7},{5,4},{6,5},{7,6},{8,9},{9,10},{10,1... | collective-permute-start | bytes 4718600 | tf_op jit(solution)/shard_map/ppermute | solution.py:43
  222.7 5.2 %collective-permute-start.27 = (f32[8,1024]{1,0:T(8,128)S(1)}, f32[8,1024]{1,0:T(8,128)S(1)}, u32[]{:S(2)}, u32[]{:S(2)}) collective-permute-start(f32[8,1024]{1,0:T(8,128)S(1)} %get-tuple-element.30.refs_0_), channel_id=1, source_target_pairs={{0,1},{1,2},{2,3},{3,0},{4,7},{5,4},{6,5},{7,6},{8,9},{9,10},{10,1... | collective-permute-start | bytes 98312 | tf_op jit(solution)/shard_map/ppermute | solution.py:43
  222.8 5.1 %collective-permute-start.28 = (f32[8,1024]{1,0:T(8,128)S(1)}, f32[8,1024]{1,0:T(8,128)S(1)}, u32[]{:S(2)}, u32[]{:S(2)}) collective-permute-start(f32[8,1024]{1,0:T(8,128)S(1)} %get-tuple-element.30.refs_0_), channel_id=1, source_target_pairs={{0,3},{1,0},{2,1},{3,2},{4,5},{5,6},{6,7},{7,4},{8,11},{9,8},{10,9... | collective-permute-start | bytes 98312 | tf_op jit(solution)/shard_map/ppermute | solution.py:43
  226.0 5.4 %collective-permute-start.29 = (f32[8,1024]{1,0:T(8,128)S(1)}, f32[8,1024]{1,0:T(8,128)S(1)}, u32[]{:S(2)}, u32[]{:S(2)}) collective-permute-start(f32[8,1024]{1,0:T(8,128)S(1)} %get-tuple-element.30.refs_0_), channel_id=1, source_target_pairs={{0,2},{1,3},{2,0},{3,1},{4,6},{5,7},{6,4},{7,5},{8,10},{9,11},{10,... | collective-permute-start | bytes 98312 | tf_op jit(solution)/shard_map/ppermute | solution.py:53
